TPU v7x, 32 devices: a whole 2x2x4 slice. The times are simulated.
32 devices in a mesh: seq: 8 (over z, y), fsdp: 4 (over x, core).
Axes of the slice: x: 2, y: 2, z: 4, core: 2. Of those that a mesh axis runs over, the one named last changes fastest.
Arguments:
- inputs: bfloat16 [4, 1024, 2560], P('fsdp', 'seq'), may hold values from -6 to 6
- gain_first: float32 [2560], replicated, may hold values from 0.5 to 1.5
- branch_weight: bfloat16 [5120, 2560], P(('seq', 'fsdp')), may hold values from -0.125 to 0.125
- branch_bias: float32 [5120], replicated, may hold values from -3 to 3
- conv_weight: float32 [4, 2560], replicated, may hold values from -3 to 3
- conv_bias: float32 [2560], replicated, may hold values from -2 to 2
- gate_weight: bfloat16 [2, 10, 256, 256], replicated, may hold values from -0.375 to 0.375
- gate_bias: float32 [2, 2560], replicated, may hold values from -4 to 4
- decay: float32 [2560], replicated, may hold values from -12 to -3.8
- out_weight: bfloat16 [2560, 2560], P(('seq', 'fsdp')), may hold values from -0.25 to 0.25
- out_bias: float32 [2560], replicated, may hold values from -2 to 2
- gain_second: float32 [2560], replicated, may hold values from 0.5 to 1.5
- mlp_weight: bfloat16 [15360, 2560], P(('seq', 'fsdp')), may hold values from -0.125 to 0.125
- down_weight: bfloat16 [2560, 7680], P(('seq', 'fsdp')), may hold values from -0.125 to 0.125
- cotangent: bfloat16 [4, 1024, 2560], P('fsdp', 'seq'), may hold values from -6 to 6
Outputs:
- output: bfloat16 [4, 1024, 2560], P('fsdp', 'seq')
- input_grad: float32 [4, 1024, 2560], P('fsdp', 'seq')
- gain_first_grad: float32 [2560], replicated
- branch_weight_grad: float32 [5120, 2560], P(('seq', 'fsdp'))
- branch_bias_grad: float32 [5120], replicated
- conv_weight_grad: float32 [4, 2560], replicated
- conv_bias_grad: float32 [2560], replicated
- gate_weight_grad: float32 [2, 10, 256, 256], replicated
- gate_bias_grad: float32 [2, 2560], replicated
- decay_grad: float32 [2560], replicated
- out_weight_grad: float32 [2560, 2560], P(('seq', 'fsdp'))
- out_bias_grad: float32 [2560], replicated
- gain_second_grad: float32 [2560], replicated
- mlp_weight_grad: float32 [15360, 2560], P(('seq', 'fsdp'))
- down_weight_grad: float32 [2560, 7680], P(('seq', 'fsdp'))
All inputs are finite; a program needn't handle non-finite values.
Results may differ from a plain program's by a relative error of at most 0.014.
Values may be sent and summed in bfloat16 or wider, within the bound.
A program may use at most 384 MiB of HBM per device.

v0:
```python
import jax
import jax.numpy as jnp
from jax import lax
from jax.sharding import PartitionSpec as P

epsilon = 1e-06


def from_behind(block, axis, distance):
    devices = range(lax.axis_size(axis))
    route = [(i - distance, i) for i in devices if i - distance in devices]
    return lax.ppermute(block, axis, route)


def normed(values, scales):
    return values * lax.rsqrt(jnp.mean(values * values, -1, keepdims=True) + epsilon) * scales


def affine(earlier, latter):
    return (latter[0] * earlier[0], latter[0] * earlier[1] + latter[1])


def lru_inputs(gates, decay, conv_out, opening):
    rgate = jax.nn.sigmoid(gates[0])
    igate = jax.nn.sigmoid(gates[1])
    log_rate = -8.0 * jax.nn.softplus(decay) * rgate
    decays = jnp.exp(log_rate)
    scaling = jnp.where(opening, 1.0, jnp.sqrt(-jnp.expm1(2.0 * log_rate)))
    return (decays, scaling * igate * conv_out)


def gated_unit(preact):
    half_width = preact.shape[1] // 2
    return jax.nn.gelu(preact[:, :half_width], approximate=True) * preact[:, half_width:]


def project(operand, weight):
    return lax.dot_general(
        operand,
        lax.all_gather(weight, ("seq", "fsdp"), axis=0, tiled=True),
        (((1,), (1,)), ((), ())),
        preferred_element_type=jnp.float32,
    )


def project_back(gradient, weight):
    return jnp.dot(
        gradient,
        lax.all_gather(weight, ("seq", "fsdp"), axis=0, tiled=True),
        preferred_element_type=jnp.float32,
    )


def weight_sums(gradient, operand):
    return lax.psum_scatter(
        lax.dot_general(
            gradient, operand, (((0,), (0,)), ((), ())), preferred_element_type=jnp.float32
        ),
        ("seq", "fsdp"),
        scatter_dimension=0,
        tiled=True,
    )


def group_project(operand, weight):
    return lax.dot_general(
        operand,
        lax.all_gather(weight, "seq", axis=0, tiled=True),
        (((1,), (1,)), ((), ())),
        preferred_element_type=jnp.float32,
    )


def group_back(gradient, weight):
    return jnp.dot(
        gradient,
        lax.all_gather(weight, "seq", axis=0, tiled=True),
        preferred_element_type=jnp.float32,
    )


def group_sums(gradient, operand):
    return lax.psum_scatter(
        lax.dot_general(
            gradient, operand, (((0,), (0,)), ((), ())), preferred_element_type=jnp.float32
        ).astype(jnp.bfloat16),
        "seq",
        scatter_dimension=0,
        tiled=True,
    ).astype(jnp.float32)


def peers_gather(values):
    return lax.all_gather(values, "fsdp", axis=0, tiled=True)


def peers_sum(values):
    return lax.psum_scatter(values, "fsdp", scatter_dimension=0, tiled=True)


def peers_swap(values):
    return lax.all_to_all(
        values.astype(jnp.bfloat16), "fsdp", split_axis=0, concat_axis=0, tiled=True
    ).astype(values.dtype)


def rim_rows(values, offset):
    return from_behind(values, "seq", offset)


def to_channels(values):
    return lax.all_to_all(values, "seq", split_axis=2, concat_axis=1, tiled=True)


def to_tokens(values):
    return lax.all_to_all(values, "seq", split_axis=1, concat_axis=2, tiled=True)


def body(
    inputs,
    gain_first,
    branch_weight,
    branch_bias,
    conv_weight,
    conv_bias,
    gate_weight,
    gate_bias,
    decay,
    out_weight,
    out_bias,
    gain_second,
    mlp_weight,
    down_weight,
    cotangent,
):
    source = inputs[0].astype(jnp.float32)
    row_count, model_width = source.shape
    tap_count = conv_weight.shape[0]
    head_count = gate_weight.shape[1]
    block_width = gate_weight.shape[2]
    first_in = normed(source, gain_first).astype(jnp.bfloat16)
    branch_pre = project(first_in, branch_weight) + branch_bias
    gate_pre = branch_pre[:, :model_width]
    conv_in = branch_pre[:, model_width:]
    gelu_gate, gelu_back = jax.vjp(lambda values: jax.nn.gelu(values, approximate=True), gate_pre)
    conv_before = rim_rows(conv_in[row_count - (tap_count - 1) :], 1)
    extended = jnp.concatenate([conv_before, conv_in], 0)
    conv_out = conv_bias + jnp.zeros_like(conv_in)
    for lagged in range(tap_count):
        conv_out = (
            conv_out
            + conv_weight[lagged]
            * extended[tap_count - 1 - lagged : tap_count - 1 - lagged + row_count]
        )
    conv_low = conv_out.astype(jnp.bfloat16).reshape(row_count, head_count, block_width)
    gates = jnp.einsum("rhb,ghbc->grhc", conv_low, gate_weight, preferred_element_type=jnp.float32)
    gates = gates.reshape(2, row_count, model_width) + gate_bias[:, None, :]
    opening = (lax.broadcasted_iota(jnp.int32, (row_count, 1), 0) == 0) & (
        lax.axis_index("seq") == 0
    )
    decays, drive = lru_inputs(gates, decay, conv_out, opening)
    channel_pair = to_channels(jnp.stack([decays, drive], 0))
    decay_ch = channel_pair[0]
    states_ch = lax.associative_scan(affine, (decay_ch, channel_pair[1]), axis=0)[1]
    states = to_tokens(states_ch[None])[0]
    mixed = (states * gelu_gate).astype(jnp.bfloat16)
    middle = source + project(mixed, out_weight) + out_bias
    second_in = normed(middle, gain_second).astype(jnp.bfloat16)
    peer_count = lax.axis_size("fsdp")
    seq_count = lax.axis_size("seq")
    all_rows = peer_count * row_count
    second_all = peers_gather(second_in[None]).reshape(all_rows, model_width)
    mlp_pre = group_project(second_all, mlp_weight)
    mlp_hidden, gated_back = jax.vjp(gated_unit, mlp_pre)
    mlp_hidden = mlp_hidden.astype(jnp.bfloat16)
    local_width = mlp_hidden.shape[1]
    half_count = seq_count // 2
    unit_rows = mlp_weight.shape[0]
    hidden_all = peers_gather(mlp_hidden[None]).reshape(peer_count, all_rows, half_count, unit_rows)
    hidden_all = hidden_all.transpose(1, 2, 0, 3).reshape(all_rows, peer_count * local_width)
    down_part = group_project(hidden_all, down_weight)
    down_rows = down_weight.shape[0]
    down_full = peers_swap(down_part.reshape(peer_count, row_count, seq_count, down_rows))
    down_full = down_full.transpose(1, 2, 0, 3).reshape(row_count, model_width)
    result = middle + down_full
    output = result.astype(jnp.bfloat16)[None]
    grad_out = cotangent[0]
    cot_parts = (
        grad_out.astype(jnp.float32)
        .reshape(row_count, seq_count, peer_count, down_rows)
        .transpose(2, 0, 1, 3)
    )
    cot_all = peers_swap(cot_parts).reshape(all_rows, seq_count * down_rows).astype(jnp.bfloat16)
    hidden_part = group_back(cot_all, down_weight)
    hidden_part = hidden_part.reshape(all_rows, half_count, peer_count, unit_rows).transpose(
        2, 0, 1, 3
    )
    grad_hidden = peers_sum(hidden_part).reshape(all_rows, local_width)
    down_grad = group_sums(cot_all, hidden_all)
    grad_pre = gated_back(grad_hidden)[0].astype(jnp.bfloat16)
    second_part = group_back(grad_pre, mlp_weight)
    grad_second = peers_sum(second_part.reshape(peer_count, row_count, model_width))[0]
    mlp_grad = group_sums(grad_pre, second_all)
    norm_second, second_back = jax.vjp(normed, middle, gain_second)
    grad_mid_norm, gain_second_term = second_back(grad_second)
    grad_middle = grad_out.astype(jnp.float32) + grad_mid_norm
    grad_branch = grad_middle.astype(jnp.bfloat16)
    out_bias_term = jnp.sum(grad_branch.astype(jnp.float32), 0)
    grad_mixed = project_back(grad_branch, out_weight)
    out_grad = weight_sums(grad_branch, mixed)
    grad_states = grad_mixed * gelu_gate
    grad_gelu = grad_mixed * states
    grad_ch = to_channels(grad_states[None])[0]
    channel_zero = jnp.zeros((1, decay_ch.shape[1]), jnp.float32)
    before_ch = jnp.concatenate([channel_zero, states_ch[:-1]], 0)
    flowing = lax.associative_scan(affine, (decay_ch, decay_ch * grad_ch), reverse=True, axis=0)[1]
    adjoint_ch = grad_ch + jnp.concatenate([flowing[1:], channel_zero], 0)
    grad_pair = to_tokens(jnp.stack([adjoint_ch * before_ch, adjoint_ch], 0))
    grad_decays = grad_pair[0]
    grad_drive = grad_pair[1]
    lru_out, lru_back = jax.vjp(
        lambda gates_in, decay_in, conv_value: lru_inputs(gates_in, decay_in, conv_value, opening),
        gates,
        decay,
        conv_out,
    )
    grad_gates, decay_term, grad_conv = lru_back((grad_decays, grad_drive))
    gates_low = grad_gates.astype(jnp.bfloat16)
    gate_bias_term = jnp.sum(gates_low.astype(jnp.float32), 1)
    split_grads = gates_low.reshape(2, row_count, head_count, block_width)
    gate_weight_term = jnp.einsum(
        "rhb,grhc->ghbc", conv_low, split_grads, preferred_element_type=jnp.float32
    )
    grad_conv = grad_conv + jnp.einsum(
        "grhc,ghbc->rhb", split_grads, gate_weight, preferred_element_type=jnp.float32
    ).reshape(row_count, model_width)
    conv_after = rim_rows(grad_conv[: tap_count - 1], -1)
    ahead = jnp.concatenate([grad_conv, conv_after], 0)
    grad_conv_in = jnp.zeros_like(grad_conv)
    conv_weight_rows = []
    for lagged in range(tap_count):
        grad_conv_in = grad_conv_in + conv_weight[lagged] * ahead[lagged : lagged + row_count]
        conv_weight_rows.append(
            jnp.sum(
                grad_conv * extended[tap_count - 1 - lagged : tap_count - 1 - lagged + row_count], 0
            )
        )
    conv_weight_term = jnp.stack(conv_weight_rows, 0)
    conv_bias_term = jnp.sum(grad_conv, 0)
    grad_gate_pre = gelu_back(grad_gelu)[0]
    grad_branch_pre = jnp.concatenate([grad_gate_pre, grad_conv_in], 1).astype(jnp.bfloat16)
    branch_bias_term = jnp.sum(grad_branch_pre.astype(jnp.float32), 0)
    grad_first = project_back(grad_branch_pre, branch_weight)
    branch_grad = weight_sums(grad_branch_pre, first_in)
    norm_first, first_back = jax.vjp(normed, source, gain_first)
    grad_src_norm, gain_first_term = first_back(grad_first)
    input_grad = (grad_middle + grad_src_norm)[None]
    summed = lax.psum(
        (
            gain_first_term,
            branch_bias_term,
            conv_weight_term,
            conv_bias_term,
            gate_weight_term,
            gate_bias_term,
            decay_term,
            out_bias_term,
            gain_second_term,
        ),
        ("seq", "fsdp"),
    )
    return (
        output,
        input_grad,
        summed[0],
        branch_grad,
        summed[1],
        summed[2],
        summed[3],
        summed[4],
        summed[5],
        summed[6],
        out_grad,
        summed[7],
        summed[8],
        mlp_grad,
        down_grad,
    )


def solution(mesh):
    return jax.shard_map(
        body,
        mesh=mesh,
        in_specs=(
            P("fsdp", "seq", None),
            P(),
            P(("seq", "fsdp"), None),
            P(),
            P(),
            P(),
            P(),
            P(),
            P(),
            P(("seq", "fsdp"), None),
            P(),
            P(),
            P(("seq", "fsdp"), None),
            P(("seq", "fsdp"), None),
            P("fsdp", "seq", None),
        ),
        out_specs=(
            P("fsdp", "seq", None),
            P("fsdp", "seq", None),
            P(),
            P(("seq", "fsdp"), None),
            P(),
            P(),
            P(),
            P(),
            P(),
            P(),
            P(("seq", "fsdp"), None),
            P(),
            P(),
            P(("seq", "fsdp"), None),
            P(("seq", "fsdp"), None),
        ),
        check_vma=False,
    )
```

profile of v0, /device:TPU:1, one launch (start us, length us, event | category | flops | bytes accessed | tf_op | source)
XLA Modules:
  0.0 3607.7 jit_solution(16752651913719436142)
XLA Ops:
  10.9 13.6 all_to_all.70
  25.1 128.7 %all-gather.15.cloned.1.call-done = bf16[640,7680]{1,0:T(8,128)(2,1)} async-done(((bf16[80,7680]{1,0:T(8,128)(2,1)}), bf16[640,7680]{1,0:T(8,128)(2,1)}) %all-gather.15.cloned.1.call-update) | async-done | bytes 9830416 | tf_op jit(solution)/shard_map/all_gather | solution.py:68
  153.8 13.9 copy.211
  167.7 13.6 convolution_bitcast_fusion
  183.3 131.8 %all-gather.9.cloned.1.call-done = bf16[5120,2560]{1,0:T(8,128)(2,1)} async-done(((bf16[160,2560]{1,0:T(8,128)(2,1)}), bf16[5120,2560]{1,0:T(8,128)(2,1)}) %all-gather.9.cloned.1.call-update) | async-done | bytes 26214416 | tf_op jit(solution)/shard_map/all_gather | solution.py:40
  315.0 15.2 convolution_add_fusion
  362.8 99.0 %all_to_all.71 = f32[2,128,2560]{1,0,2:T(2,128)S(1)} all-to-all(f32[2,128,2560]{1,0,2:T(2,128)} %copy.183), channel_id=1, replica_groups=mesh['seq'=8,'fsdp'=4] {'seq'}, dimensions={2} | all-to-all | bytes 5242880 | tf_op jit(solution)/shard_map/all_to_all | solution.py:112
  465.5 24.5 slice.580
  490.0 24.5 slice.581
  514.5 24.5 slice.585
  542.5 24.9 slice.653
  567.3 24.5 slice.583
  591.8 24.5 slice.582
  632.4 13.2 slice.591
  823.0 13.2 slice.586
  926.5 13.4 pad.153
  942.1 13.4 pad.152
  960.5 26.4 pad.154
  986.9 26.7 pad.155
  1021.4 53.0 %all_to_all.72 = f32[1,1024,320]{2,0,1:T(1,128)} all-to-all(f32[1,1024,320]{2,0,1:T(1,128)} %copy.199), channel_id=1, replica_groups=mesh['seq'=8,'fsdp'=4] {'seq'}, dimensions={1} | all-to-all | bytes 2621440 | tf_op jit(solution)/shard_map/all_to_all | solution.py:116
  1124.1 28.1 all-gather.17.cloned.1.call-done
  1152.1 17.8 fusion.122
  1177.5 18.4 fusion.73
  1195.9 37.0 %all-gather.19.cloned.1.call-done = bf16[2048,1920]{1,0:T(8,128)(2,1)} async-done(((bf16[512,1920]{1,0:T(8,128)(2,1)}), bf16[2048,1920]{1,0:T(8,128)(2,1)}) %all-gather.19.cloned.1.call-update) | async-done | bytes 7864336 | tf_op jit(solution)/shard_map/all_gather | solution.py:94
  1232.9 21.7 reshape.214
  1254.6 18.1 copy.261
  1272.7 16.7 reshape.209
  1351.0 24.0 slice.658
  1387.5 24.5 slice.663
  1412.0 24.0 slice.661
  1450.4 13.2 slice.668
  1671.2 24.9 slice.734
  1754.9 13.4 pad.174
  1778.7 24.6 pad.234
  1803.2 26.7 pad.378
  1832.9 13.2 reverse.10
  1856.1 75.3 %all_to_all.73 = f32[2,1024,320]{2,0,1:T(2,128)} all-to-all(f32[2,1024,320]{2,0,1:T(2,128)} %copy.230), channel_id=1, replica_groups=mesh['seq'=8,'fsdp'=4] {'seq'}, dimensions={1} | all-to-all | bytes 5242880 | tf_op jit(solution)/shard_map/all_to_all | solution.py:116
  1960.7 14.9 copy.204
  1986.7 13.9 copy.269
  2000.7 18.5 convolution_convert_fusion
  2060.7 14.0 fusion.32
  2075.1 14.5 fusion.99
  2089.7 21.8 fusion.75
  2121.3 158.1 %reduce-scatter.19.cloned.1.call-done = bf16[80,7680]{1,0:T(8,128)(2,1)} async-done(((bf16[640,7680]{1,0:T(8,128)(2,1)}), bf16[80,7680]{1,0:T(8,128)(2,1)}) %reduce-scatter.19.cloned.1.call-update) | async-done | bytes 1228816
  2286.9 319.1 %reduce-scatter.17.cloned.1.call-done = bf16[480,2560]{1,0:T(8,128)(2,1)} async-done(((bf16[3840,2560]{1,0:T(8,128)(2,1)}), bf16[480,2560]{1,0:T(8,128)(2,1)}) %reduce-scatter.17.cloned.1.call-update) | async-done | bytes 2457616 | tf_op jit(solution)/shard_map/reduce_scatter | solution.py:83
  2610.6 128.2 %all-reduce.56.cloned.1.call-done = (f32[2560]{0:T(1024)}, f32[5120]{0:T(1024)}, f32[4,2560]{1,0:T(4,128)}, f32[2560]{0:T(1024)}, f32[2,2560]{1,0:T(2,128)}, /*i...) async-done(((f32[2560]{0:T(1024)}, f32[5120]{0:T(1024)}, f32[4,2560]{1,0:T(4,128)}, f32[2560]{0:T(1024)}, f32[2,2560]{1,0:T(2,128)}, /*index=5*/f32[2560]{0:T(1024)}, ...) | async-done | bytes 133136 | tf_op jit(solution)/shard_map/psum | solution.py:258
  2738.8 287.3 %reduce-scatter.15.cloned.1.call-done = f32[80,2560]{1,0:T(8,128)} async-done(((f32[2560,2560]{1,0:T(8,128)}), f32[80,2560]{1,0:T(8,128)}) %reduce-scatter.15.cloned.1.call-update) | async-done | bytes 819216 | tf_op jit(solution)/shard_map/reduce_scatter | solution.py:55
  3026.1 564.2 %reduce-scatter.13.cloned.1.call-done = f32[160,2560]{1,0:T(8,128)} async-done(((f32[5120,2560]{1,0:T(8,128)}), f32[160,2560]{1,0:T(8,128)}) %reduce-scatter.13.cloned.1.call-update) | async-done | bytes 1638416 | tf_op jit(solution)/shard_map/reduce_scatter | solution.py:55
  (566 shorter events, 893.5 us)
Async XLA Ops:
  7.2 332.9 %copy-start = (bf16[2,10,256,256]{3,2,1,0:T(8,128)(2,1)S(1)}, bf16[2,10,256,256]{3,2,1,0:T(8,128)(2,1)}, u32[]{:S(2)}) copy-start(bf16[2,10,256,256]{3,2,1,0:T(8,128)(2,1)} %param.21) | copy-start | bytes 7864324
  7.2 146.6 %all-gather.15.cloned.1.call-start = ((), (), s32[]{:S(2)}) async-start(), calls=%async_computation.14 | async-start | bytes 11059200 | tf_op jit(solution)/shard_map/all_gather | solution.py:68
  7.9 307.1 %all-gather.9.cloned.1.call-start = ((), (), s32[]{:S(2)}) async-start(), calls=%async_computation.11 | async-start | bytes 27033600 | tf_op jit(solution)/shard_map/all_gather | solution.py:40
  8.7 1079.9 %all-gather.11.cloned.1.call-start = ((), (), s32[]{:S(2)}) async-start(), calls=%async_computation.12 | async-start | bytes 13516800 | tf_op jit(solution)/shard_map/all_gather | solution.py:40
  9.4 1091.3 %all-reduce.54.cloned.1.call-start = ((), (), s32[]{:S(2)}) async-start(), calls=%async_computation.23 | async-start | bytes 31457280
  25.1 142.6 %copy-start.53 = (bf16[4,128,8,80]{1,0,3,2:T(4,128)(2,1)}, bf16[4,128,8,80]{1,0,3,2:T(4,128)(2,1)S(1)}, u32[]{:S(2)}) copy-start(bf16[4,128,8,80]{1,0,3,2:T(4,128)(2,1)S(1)} %copy.210) | copy-start | bytes 1966084
  181.3 133.7 %copy-start.67 = (f32[2560]{0:T(1024)S(1)}, f32[2560]{0:T(1024)}, u32[]{:S(2)}) copy-start(f32[2560]{0:T(1024)} %param.16) | copy-start | bytes 30724
  181.4 133.7 %copy-start.83 = (f32[5120]{0:T(1024)S(1)}, f32[5120]{0:T(1024)}, u32[]{:S(2)}) copy-start(f32[5120]{0:T(1024)} %param.18) | copy-start | bytes 61444
  181.4 942.7 %all-gather.13.cloned.1.call-start = ((), (), s32[]{:S(2)}) async-start(), calls=%async_computation.13 | async-start | bytes 22118400 | tf_op jit(solution)/shard_map/all_gather | solution.py:68
  182.0 970.2 %all-gather.17.cloned.1.call-start = ((), (), s32[]{:S(2)}) async-start(), calls=%async_computation.20 | async-start | bytes 3276800 | tf_op jit(solution)/shard_map/all_gather | solution.py:94
  182.4 153.5 %copy-start.71 = (f32[2560]{0:T(1024)}, f32[2560]{0:T(1024)S(1)}, u32[]{:S(2)}) copy-start(f32[2560]{0:T(1024)S(1)} %get-tuple-element.83) | copy-start | bytes 30724
  182.4 153.5 %copy-start.73 = (f32[2560]{0:T(1024)}, f32[2560]{0:T(1024)S(1)}, u32[]{:S(2)}) copy-start(f32[2560]{0:T(1024)S(1)} %get-tuple-element.84) | copy-start | bytes 30724
  182.4 153.5 %copy-start.75 = (f32[2560]{0:T(1024)}, f32[2560]{0:T(1024)S(1)}, u32[]{:S(2)}) copy-start(f32[2560]{0:T(1024)S(1)} %get-tuple-element.85) | copy-start | bytes 30724
  182.4 153.6 %copy-start.77 = (f32[2560]{0:T(1024)}, f32[2560]{0:T(1024)S(1)}, u32[]{:S(2)}) copy-start(f32[2560]{0:T(1024)S(1)} %get-tuple-element.86) | copy-start | bytes 30724
  183.2 147.0 %copy-start.85 = (f32[128]{0:T(128)}, f32[128]{0:T(128)S(1)}, u32[]{:S(2)}) copy-start(f32[128]{0:T(128)S(1)} %fusion.95) | copy-start | bytes 1540
  183.3 170.3 %copy-start.65 = (f32[2560]{0:T(1024)}, f32[2560]{0:T(1024)S(1)}, u32[]{:S(2)}) copy-start(f32[2560]{0:T(1024)S(1)} %fusion.94) | copy-start | bytes 30724
  331.2 4.8 collective-permute-start
  334.5 17.7 copy-start.89
  718.1 20.9 copy-start.30
  856.6 11.9 copy-start.26
  868.6 12.0 copy-start.36
  885.8 16.9 copy-start.31
  926.5 14.8 copy-start.57
  1088.5 10.4 copy-start.79
  1100.0 132.9 %all-gather.19.cloned.1.call-start = ((), (), s32[]{:S(2)}) async-start(), calls=%async_computation.21 | async-start | bytes 9830400 | tf_op jit(solution)/shard_map/all_gather | solution.py:94
  1152.1 17.8 copy-start.7
  1177.4 126.4 %reduce-scatter.11.cloned.1.call-start = ((), (), s32[]{:S(2)}) async-start(), calls=%async_computation.15 | async-start | bytes 6553600 | tf_op jit(solution)/shard_map/reduce_scatter | solution.py:98
  1299.6 13.5 all-to-all-start.2
  1334.4 12.1 copy-start.21
  1334.4 48.2 %all-to-all-start.4 = ((f32[1,128,2560]{1,0,2:T(1,128)}), f32[1,128,2560]{1,0,2:T(1,128)}, u32[]{:S(2)}, u32[]{:S(2)}) async-start(f32[1,128,2560]{1,0,2:T(1,128)} %copy.216), calls=%async_computation.5 | async-start | bytes 2621440 | tf_op jit(solution)/shard_map/all_to_all | solution.py:112
  1339.4 775.9 %all-reduce.52.cloned.1.call-start = ((), (), s32[]{:S(2)}) async-start(), calls=%async_computation.17 | async-start | bytes 10485760 | tf_op jit(solution)/shard_map/psum | solution.py:258
  1547.9 20.6 copy-start.28
  1671.1 26.6 copy-start.52
  1671.1 26.7 copy-start.51
  1671.1 26.8 copy-start.50
  1740.4 13.6 copy-start.59
  1960.6 15.0 copy-start.54
  1960.7 318.7 %reduce-scatter.19.cloned.1.call-start = ((), (), s32[]{:S(2)}) async-start(), calls=%async_computation.22 | async-start | bytes 11059200
  2000.6 605.4 %reduce-scatter.17.cloned.1.call-start = ((), (), s32[]{:S(2)}) async-start(), calls=%async_computation.19 | async-start | bytes 22118400 | tf_op jit(solution)/shard_map/reduce_scatter | solution.py:83
  2019.2 719.6 %all-reduce.56.cloned.1.call-start = ((), (), s32[]{:S(2)}) async-start(), calls=%async_computation.24 | async-start | bytes 286720 | tf_op jit(solution)/shard_map/psum | solution.py:258
  2044.0 10.9 copy-start.72
  2044.0 10.9 copy-start.74
  2044.0 10.9 copy-start.76
  2044.0 10.9 copy-start.78
  2050.2 4.7 collective-permute-start.1
  2058.5 16.2 copy-start.15
  2074.8 951.3 %reduce-scatter.15.cloned.1.call-start = ((), (), s32[]{:S(2)}) async-start(), calls=%async_computation.18 | async-start | bytes 27033600 | tf_op jit(solution)/shard_map/reduce_scatter | solution.py:55
  2089.6 1500.7 %reduce-scatter.13.cloned.1.call-start = ((), (), s32[]{:S(2)}) async-start(), calls=%async_computation.16 | async-start | bytes 54067200 | tf_op jit(solution)/shard_map/reduce_scatter | solution.py:55
  (64 other events, 224.1 us)
Sparse Core Ops, SparseCore 0:
  10.2 143.5 all-gather.14
  156.6 158.3 all-gather.8
  317.9 138.9 all-gather.10
  459.2 268.7 all-reduce.53
  729.4 394.5 all-gather.12
  1126.0 26.0 all-gather.16
  1177.6 55.2 all-gather.18
  1236.0 50.7 reduce-scatter.10
  1960.8 145.6 all-reduce.51
  2110.0 169.3 reduce-scatter.18
  2283.2 322.7 reduce-scatter.16
  2613.4 125.3 all-reduce.55
  2741.7 284.3 reduce-scatter.14
  3028.8 561.3 reduce-scatter.12
where the time goes:
time: 3630 us; the launch traced here: 3610 us
  waiting for transfers between devices  1810 us (50%)
  local copies, waits for them, and re-layouts  1190 us (33%)
  blocking collectives  241 us (7%)
  matrix products  186 us (5%)
  other arithmetic  153 us (4%)
    reduce_scatter x2, waiting for transfers between devices, weight_sums(): lax.psum_scatter(lax.dot_general(gradient, operand, (((0,), (0,)), ((), (...  851 us
    slice x55, local copies, waits for them, and re-layouts, body(): lax.associative_scan(affine, (decay_ch, channel_pair[1]), axis=0)[1]  354 us
    slice x58, local copies, waits for them, and re-layouts, body(): lax.associative_scan(affine, (decay_ch, decay_ch * grad_ch), reverse=True...  327 us
    reduce_scatter x1, waiting for transfers between devices, group_sums(): lax.psum_scatter(lax.dot_general(gradient, operand, (((0,), (0,)), ((), (...  319 us
    unnamed x16, waiting for transfers between devices  161 us
    all_gather x2, waiting for transfers between devices, group_project(): lax.all_gather(weight, 'seq', axis=0, tiled=True)  142 us
    all_gather x2, waiting for transfers between devices, project(): lax.all_gather(weight, ('seq', 'fsdp'), axis=0, tiled=True)  132 us
    pad x18, local copies, waits for them, and re-layouts, body(): lax.associative_scan(affine, (decay_ch, channel_pair[1]), axis=0)[1]  129 us
  transfers between devices with their start and end apart: 18, of which 12 were waited for; matrix products, arithmetic and copies ran while one was open for 27% of the time, Pallas kernels for 0%

commit v1 on v0

v1 whole, which is shorter than its diff:
```python
import functools

import jax
import jax.numpy as jnp
from jax import lax
from jax.experimental import pallas as pl
from jax.experimental.pallas import tpu as pltpu
from jax.sharding import Mesh
from jax.sharding import PartitionSpec as P

epsilon = 1e-06
low = jnp.bfloat16
wide = jnp.float32

cube = ("b3", "b2", "b1", "b0")
block_size = 16
places = ("g",) + cube
seq_axes = ("g", "b3", "b2")
fsdp_axes = ("b1", "b0")
orders = (("b3", "b1", "b2"), ("b3", "b2", "b1"))
back_orders = (("b1", "b2", "b3"), ("b2", "b1", "b3"))

anywhere = pl.BlockSpec(memory_space=pl.ANY)
in_vmem = pl.BlockSpec(memory_space=pltpu.VMEM)
in_smem = pl.BlockSpec(memory_space=pltpu.SMEM)
whole_vmem = 67000000


def bit_of(axis):
    return 1 << (len(cube) - 1 - cube.index(axis))


def slot_at(mask):
    slot = 0
    for axis in cube:
        here = lax.axis_index(axis)
        slot = slot * 2 + (1 - here if mask & bit_of(axis) else here)
    return slot


def device_at(mask):
    return {axis: 1 - lax.axis_index(axis) for axis in cube if mask & bit_of(axis)}


def greet(masks):
    barrier = pltpu.get_barrier_semaphore()
    for mask in masks:
        pl.semaphore_signal(
            barrier, inc=1, device_id=device_at(mask), device_id_type=pl.DeviceIdType.MESH
        )
    pl.semaphore_wait(barrier, len(masks))


def split_rows(rows, unit):
    tiles = rows // unit
    sizes = [(tiles + 1 - part) // 2 * unit for part in range(2)]
    return [(part, part * sizes[0], size) for part, size in enumerate(sizes) if size > 0]


def remote_params(collective):
    return pltpu.CompilerParams(
        collective_id=collective, has_side_effects=True, vmem_limit_bytes=whole_vmem
    )


def gather_kernel(pieces, x_ref, out_ref, send_sem, recv_sem, local_sem):
    greet([bit_of(axis) for axis in cube])
    sent = []

    def push(part, start, size, mask, axis):
        slot = slot_at(mask)
        source = (x_ref if mask == 0 else out_ref.at[slot]).at[pl.ds(start, size)]
        copy = pltpu.make_async_remote_copy(
            src_ref=source,
            dst_ref=out_ref.at[slot].at[pl.ds(start, size)],
            send_sem=send_sem.at[len(sent)],
            recv_sem=recv_sem.at[part, mask ^ bit_of(axis)],
            device_id=device_at(bit_of(axis)),
            device_id_type=pl.DeviceIdType.MESH,
        )
        copy.start()
        sent.append(copy)

    def arrive(part, start, size, mask):
        target = out_ref.at[slot_at(mask)].at[pl.ds(start, size)]
        pltpu.make_async_copy(target, target, recv_sem.at[part, mask]).wait()

    own = pltpu.make_async_copy(x_ref, out_ref.at[slot_at(0)], local_sem)
    own.start()
    for stage in range(4):
        for part, start, size in pieces:
            order = orders[part] + ("b0",)
            masks = [0]
            if stage > 0:
                for axis in order[: stage - 1]:
                    masks = masks + [mask | bit_of(axis) for mask in masks]
                masks = [mask | bit_of(order[stage - 1]) for mask in masks]
            for mask in masks:
                if mask:
                    arrive(part, start, size, mask)
                for axis in order[stage:]:
                    push(part, start, size, mask, axis)
    for part, start, size in pieces:
        for mask in range(block_size):
            if mask & bit_of("b0"):
                arrive(part, start, size, mask)
    for copy in sent:
        copy.wait_send()
    own.wait()


def block_gather(values, collective):
    rows, width = values.shape
    pieces = split_rows(rows, 16)
    return pl.pallas_call(
        functools.partial(gather_kernel, pieces),
        out_shape=jax.ShapeDtypeStruct((block_size, rows, width), values.dtype),
        in_specs=[in_vmem],
        out_specs=anywhere,
        scratch_shapes=[
            pltpu.SemaphoreType.DMA((15 * len(pieces),)),
            pltpu.SemaphoreType.DMA((2, block_size)),
            pltpu.SemaphoreType.DMA,
        ],
        compiler_params=remote_params(collective),
        name="block_gather",
    )(values)


def scatter_kernel(pieces, source_count, *refs):
    sources = refs[:source_count]
    out_ref, own, away, send_sem, recv_sem, load_sem = refs[source_count:]
    core = bit_of("b0")
    greet([bit_of(axis) for axis in cube])
    sent = []

    def push(source, number, hop, index, axis):
        _, _, _, start, size = pieces[number]
        copy = pltpu.make_async_remote_copy(
            src_ref=source,
            dst_ref=away.at[hop, index].at[pl.ds(start, size)],
            send_sem=send_sem.at[len(sent)],
            recv_sem=recv_sem.at[number, hop, index],
            device_id=device_at(bit_of(axis)),
            device_id_type=pl.DeviceIdType.MESH,
        )
        copy.start()
        sent.append(copy)

    def sequence(order):
        first, second, third = (bit_of(axis) for axis in back_orders[order])
        return [
            first | second | third,
            first | second,
            first | third,
            first,
            second | third,
            second,
            third,
            0,
        ]

    def arrive(number, hop, index):
        _, _, _, start, size = pieces[number]
        target = away.at[hop, index].at[pl.ds(start, size)]
        pltpu.make_async_copy(target, target, recv_sem.at[number, hop, index]).wait()

    loads = {}
    for turn in range(8):
        for number, (order, source, begin, start, size) in enumerate(pieces):
            mask = sequence(order)[turn]
            rows = pl.ds(begin, size)
            push(
                sources[source].at[slot_at(mask | core)].at[rows], number, 0, mask >> 1, "b0"
            )
    for turn in range(8):
        for number, (order, source, begin, start, size) in enumerate(pieces):
            mask = sequence(order)[turn]
            load = pltpu.make_async_copy(
                sources[source].at[slot_at(mask)].at[pl.ds(begin, size)],
                own.at[mask >> 1].at[pl.ds(start, size)],
                load_sem.at[number, mask >> 1],
            )
            load.start()
            loads[number, mask] = load
    for turn in range(8):
        for number, (order, source, begin, start, size) in enumerate(pieces):
            mask = sequence(order)[turn]
            index = mask >> 1
            bits = [bit_of(axis) for axis in back_orders[order]]
            loads[number, mask].wait()
            hops = [0]
            arrive(number, 0, index)
            target = None
            for hop, bit in enumerate(bits):
                if mask & bit:
                    target = hop
                    break
                arrive(number, hop + 1, index)
                hops.append(hop + 1)

            def add_tile(i, carry, index=index, start=start, hops=hops, target=target):
                at = pl.ds(pl.multiple_of(start + i * 16, 16), 16)
                total = own[index, at, :].astype(wide)
                for hop in hops:
                    total = total + away[hop, index, at, :].astype(wide)
                if target is None:
                    out_ref[at, :] = total.astype(out_ref.dtype)
                else:
                    own[index, at, :] = total.astype(own.dtype)
                return carry

            lax.fori_loop(0, size // 16, add_tile, 0)
            if target is not None:
                push(
                    own.at[index].at[pl.ds(start, size)],
                    number,
                    target + 1,
                    (mask ^ bits[target]) >> 1,
                    back_orders[order][target],
                )
    for copy in sent:
        copy.wait_send()


def block_scatter(collective, *partials):
    width = partials[0].shape[2]
    pieces = []
    rows = 0
    for source, partial in enumerate(partials):
        for order, begin, size in split_rows(partial.shape[1], 16):
            pieces.append((order, source, begin, rows + begin, size))
        rows += partial.shape[1]
    return pl.pallas_call(
        functools.partial(scatter_kernel, pieces, len(partials)),
        out_shape=jax.ShapeDtypeStruct((rows, width), wide),
        in_specs=[anywhere] * len(partials),
        out_specs=in_vmem,
        scratch_shapes=[
            pltpu.VMEM((8, rows, width), low),
            pltpu.VMEM((4, 8, rows, width), low),
            pltpu.SemaphoreType.DMA((15 * len(pieces),)),
            pltpu.SemaphoreType.DMA((len(pieces), 4, 8)),
            pltpu.SemaphoreType.DMA((len(pieces), 8)),
        ],
        compiler_params=remote_params(collective),
        name="block_scatter",
    )(*partials)


def swap_kernel(x_ref, out_ref, send_sem, recv_sem, local_sem):
    greet(list(range(1, block_size)))
    sent = []
    here = slot_at(0)
    for mask in (15, 14, 13, 11, 7, 12, 10, 6, 9, 5, 3, 8, 4, 2, 1):
        copy = pltpu.make_async_remote_copy(
            src_ref=x_ref.at[slot_at(mask)],
            dst_ref=out_ref.at[here],
            send_sem=send_sem.at[mask],
            recv_sem=recv_sem.at[mask],
            device_id=device_at(mask),
            device_id_type=pl.DeviceIdType.MESH,
        )
        copy.start()
        sent.append(copy)
    own = pltpu.make_async_copy(x_ref.at[here], out_ref.at[here], local_sem)
    own.start()
    for mask in range(1, block_size):
        target = out_ref.at[slot_at(mask)]
        pltpu.make_async_copy(target, target, recv_sem.at[mask]).wait()
    for copy in sent:
        copy.wait_send()
    own.wait()


def block_swap(values, collective):
    return pl.pallas_call(
        swap_kernel,
        out_shape=jax.ShapeDtypeStruct(values.shape, values.dtype),
        in_specs=[in_vmem],
        out_specs=in_vmem,
        scratch_shapes=[
            pltpu.SemaphoreType.DMA((block_size,)),
            pltpu.SemaphoreType.DMA((block_size,)),
            pltpu.SemaphoreType.DMA,
        ],
        compiler_params=remote_params(collective),
        name="block_swap",
    )(values)


def group_gather(values):
    return lax.all_gather(values, "g", axis=0)


def group_sum(partials):
    return lax.psum_scatter(partials.astype(low), "g", scatter_dimension=0).astype(wide)


def group_total(values):
    count = lax.axis_size("g")
    total = values
    for distance in range(1, count):
        route = [(i, (i + distance) % count) for i in range(count)]
        total = total + lax.ppermute(values.astype(low), "g", route).astype(wide)
    return total


def spread_kernel(group_count, x_ref, out_ref, send_sem, recv_sem, local_sem):
    here_g, here_3, here_2 = (lax.axis_index(axis) for axis in seq_axes)
    peers = []
    for step in range(group_count):
        for mask in range(4):
            if step or mask:
                peers.append((step, mask))

    def place(step, mask):
        return (
            lax.rem(here_g + step, group_count),
            1 - here_3 if mask & 2 else here_3,
            1 - here_2 if mask & 1 else here_2,
        )

    barrier = pltpu.get_barrier_semaphore()
    for step, mask in peers:
        pl.semaphore_signal(
            barrier,
            inc=1,
            device_id=dict(zip(seq_axes, place(step, mask))),
            device_id_type=pl.DeviceIdType.MESH,
        )
    pl.semaphore_wait(barrier, len(peers))
    mine = here_g * 4 + here_3 * 2 + here_2
    sent = []
    for number, (step, mask) in enumerate(peers):
        copy = pltpu.make_async_remote_copy(
            src_ref=x_ref,
            dst_ref=out_ref.at[mine],
            send_sem=send_sem.at[number],
            recv_sem=recv_sem.at[number],
            device_id=dict(zip(seq_axes, place(step, mask))),
            device_id_type=pl.DeviceIdType.MESH,
        )
        copy.start()
        sent.append(copy)
    own = pltpu.make_async_copy(x_ref, out_ref.at[mine], local_sem)
    own.start()
    for number, (step, mask) in enumerate(peers):
        from_g, from_3, from_2 = place(group_count - step, mask)
        target = out_ref.at[from_g * 4 + from_3 * 2 + from_2]
        pltpu.make_async_copy(target, target, recv_sem.at[number]).wait()
    for copy in sent:
        copy.wait_send()
    own.wait()


def seq_spread(values, collective):
    group_count = lax.axis_size("g")
    count = 4 * group_count
    return pl.pallas_call(
        functools.partial(spread_kernel, group_count),
        out_shape=jax.ShapeDtypeStruct((count,) + values.shape, values.dtype),
        in_specs=[in_vmem],
        out_specs=in_vmem,
        scratch_shapes=[
            pltpu.SemaphoreType.DMA((count,)),
            pltpu.SemaphoreType.DMA((count,)),
            pltpu.SemaphoreType.DMA,
        ],
        compiler_params=remote_params(collective),
        name="seq_spread",
    )(values)


def rim_rows(values, offset):
    count = 4 * lax.axis_size("g")
    route = [(i - offset, i) for i in range(count) if 0 <= i - offset < count]
    return lax.ppermute(values, seq_axes, route)


def gelu_parts(v):
    inner = 0.7978845608028654 * (v + 0.044715 * v * v * v)
    t = jnp.tanh(inner)
    value = 0.5 * v * (1.0 + t)
    slope = 0.5 * (1.0 + t) + 0.5 * v * (1.0 - t * t) * 0.7978845608028654 * (
        1.0 + 0.134145 * v * v
    )
    return value, slope


def shifted(values, distance, fill):
    rows = values.shape[0]
    if distance % 8 == 0:
        head = jnp.full((distance,) + values.shape[1:], fill, values.dtype)
        return jnp.concatenate([head, values[: rows - distance]], 0)
    row = lax.broadcasted_iota(jnp.int32, values.shape, 0)
    return jnp.where(row >= distance, pltpu.roll(values, distance, 0), fill)


def shifted_back(values, distance, fill):
    rows = values.shape[0]
    if distance % 8 == 0:
        tail = jnp.full((distance,) + values.shape[1:], fill, values.dtype)
        return jnp.concatenate([values[distance:], tail], 0)
    row = lax.broadcasted_iota(jnp.int32, values.shape, 0)
    return jnp.where(row < rows - distance, pltpu.roll(values, rows - distance, 0), fill)


def scan_rows(rates, terms, shift):
    distance = 1
    while distance < rates.shape[0]:
        terms = terms + rates * shift(terms, distance, 0.0)
        rates = rates * shift(rates, distance, 1.0)
        distance *= 2
    return rates, terms


def one_minus_square(log_rate):
    x = 2.0 * log_rate
    series = 1.0
    for n in (9, 8, 7, 6, 5, 4, 3, 2):
        series = 1.0 + x * (1.0 / n) * series
    return jnp.where(x > -0.5, -x * series, 1.0 - jnp.exp(x))


def lagged_sum(ext, weights, start):
    total = start
    for lag in range(weights.shape[0]):
        moved = pltpu.roll(ext, lag, 0) if lag else ext
        total = total + weights[lag : lag + 1, :] * moved[8:, :]
    return total


def opening_rows(shape, position):
    return (lax.broadcasted_iota(jnp.int32, shape, 0) == 0) & (position == 0)


def local_states_kernel(
    position_ref,
    conv_in_ref,
    before_ref,
    taps_ref,
    bias_ref,
    weight_ref,
    gate_bias_ref,
    rate_ref,
    conv_out_ref,
    rgate_ref,
    igate_ref,
    decay_ref,
    local_ref,
    product_ref,
    ends_ref,
):
    ext = jnp.concatenate([before_ref[...], conv_in_ref[...]], 0)
    conv_out = lagged_sum(ext, taps_ref[...], bias_ref[...])
    conv_low = conv_out.astype(low)
    gates = [
        jax.nn.sigmoid(
            jnp.dot(conv_low, weight_ref[j, 0], preferred_element_type=wide)
            + gate_bias_ref[j : j + 1, :]
        )
        for j in range(2)
    ]
    log_rate = rate_ref[...] * gates[0]
    rates = jnp.exp(log_rate)
    scaling = jnp.where(
        opening_rows(rates.shape, position_ref[0]), 1.0, jnp.sqrt(one_minus_square(log_rate))
    )
    product, states = scan_rows(rates, scaling * gates[1] * conv_out, shifted)
    conv_out_ref[...] = conv_out
    rgate_ref[...] = gates[0]
    igate_ref[...] = gates[1]
    decay_ref[...] = rates
    local_ref[...] = states
    product_ref[...] = product
    rows = rates.shape[0]
    ends_ref[...] = jnp.concatenate(
        [
            product[rows - 1 :],
            states[rows - 1 :],
        ],
        0,
    )


def full_states_kernel(
    position_ref, local_ref, product_ref, ends_ref, gate_pre_ref, states_ref, mixed_ref, entry_ref
):
    entry = jnp.zeros((1, local_ref.shape[1]), wide)
    for s in range(ends_ref.shape[0]):
        later = ends_ref[s, 0:1, :] * entry + ends_ref[s, 1:2, :]
        entry = jnp.where(s < position_ref[0], later, entry)
    states = local_ref[...] + product_ref[...] * entry
    states_ref[...] = states
    mixed_ref[...] = (states * gelu_parts(gate_pre_ref[...])[0]).astype(low)
    entry_ref[...] = jnp.broadcast_to(entry, entry_ref.shape)


def local_adjoint_kernel(
    grad_mixed_ref, gate_pre_ref, decay_ref, local_ref, product_ref, ends_ref
):
    grad_states = grad_mixed_ref[...] * gelu_parts(gate_pre_ref[...])[0]
    rates = decay_ref[...]
    product, adjoint = scan_rows(shifted_back(rates, 1, 1.0), grad_states, shifted_back)
    local_ref[...] = adjoint
    product_ref[...] = product
    ends_ref[...] = jnp.concatenate(
        [
            rates[0:1] * product[0:1],
            rates[0:1] * adjoint[0:1],
        ],
        0,
    )


def gate_grads_kernel(
    position_ref,
    local_ref,
    product_ref,
    ends_ref,
    decay_ref,
    rgate_ref,
    igate_ref,
    conv_out_ref,
    states_ref,
    entry_ref,
    conv_in_ref,
    before_ref,
    weight_ref,
    rate_ref,
    grad_conv_ref,
    weight_grad_ref,
    sums_ref,
):
    position = position_ref[0]
    entry = jnp.zeros((1, local_ref.shape[1]), wide)
    for s in range(ends_ref.shape[0] - 1, 0, -1):
        earlier = ends_ref[s, 0:1, :] * entry + ends_ref[s, 1:2, :]
        entry = jnp.where(s > position, earlier, entry)
    adjoint = local_ref[...] + product_ref[...] * entry
    rates = decay_ref[...]
    rgate = rgate_ref[...]
    igate = igate_ref[...]
    conv_out = conv_out_ref[...]
    row = lax.broadcasted_iota(jnp.int32, rates.shape, 0)
    before = jnp.where(row == 0, entry_ref[0:1, :], pltpu.roll(states_ref[...], 1, 0))
    opening = opening_rows(rates.shape, position)
    log_rate = rate_ref[...] * rgate
    root = jnp.sqrt(one_minus_square(log_rate))
    scaling = jnp.where(opening, 1.0, root)
    grad_scaling = adjoint * igate * conv_out
    grad_log = adjoint * before * rates - jnp.where(
        opening, 0.0, grad_scaling * rates * rates / root
    )
    grad_rgate = grad_log * rate_ref[...] * rgate * (1.0 - rgate)
    grad_igate = adjoint * scaling * conv_out * igate * (1.0 - igate)
    grad_conv = adjoint * scaling * igate
    conv_low = conv_out.astype(low)
    sums = []
    for j, grad in enumerate((grad_rgate, grad_igate)):
        grad_low = grad.astype(low)
        sums.append(jnp.sum(grad_low.astype(wide), 0, keepdims=True))
        weight_grad_ref[j, 0] = lax.dot_general(
            conv_low, grad_low, (((0,), (0,)), ((), ())), preferred_element_type=wide
        )
        grad_conv = grad_conv + lax.dot_general(
            grad_low, weight_ref[j, 0], (((1,), (1,)), ((), ())), preferred_element_type=wide
        )
    grad_conv_ref[...] = grad_conv
    sums.append(jnp.sum(grad_log * rgate, 0, keepdims=True))
    sums.append(jnp.sum(grad_conv, 0, keepdims=True))
    ext = jnp.concatenate([before_ref[...], conv_in_ref[...]], 0)
    for lag in range(4):
        moved = pltpu.roll(ext, lag, 0) if lag else ext
        sums.append(jnp.sum(grad_conv * moved[8:, :], 0, keepdims=True))
    sums_ref[...] = jnp.concatenate(sums, 0)


def branch_grads_kernel(
    grad_conv_ref, after_ref, taps_ref, gate_pre_ref, grad_mixed_ref, states_ref, out_ref, sums_ref
):
    grad_conv = grad_conv_ref[...]
    rows = grad_conv.shape[0]
    ext = jnp.concatenate([grad_conv, after_ref[...]], 0)
    total = taps_ref[0:1, :] * grad_conv
    for lag in range(1, taps_ref.shape[0]):
        moved = pltpu.roll(ext, rows + 8 - lag, 0)
        total = total + taps_ref[lag : lag + 1, :] * moved[:rows, :]
    slope = gelu_parts(gate_pre_ref[...])[1]
    grad_gate = slope * grad_mixed_ref[...] * states_ref[...]
    sums = []
    for j, grad in enumerate((grad_gate, total)):
        grad_low = grad.astype(low)
        out_ref[j] = grad_low
        sums.append(jnp.sum(grad_low.astype(wide), 0, keepdims=True))
    sums_ref[...] = jnp.concatenate(sums + [jnp.zeros((6, grad_conv.shape[1]), wide)], 0)


def by_heads(kernel, heads, width, operands, outs, name):
    def spec(shape):
        if len(shape) == 1:
            return in_smem
        if len(shape) == 4:
            return pl.BlockSpec((shape[0], 1, width, width), lambda h: (0, h, 0, 0))
        lead = shape[:-1]
        return pl.BlockSpec(lead + (width,), lambda h, rank=len(lead): (0,) * rank + (h,))

    return pl.pallas_call(
        kernel,
        grid=(heads,),
        out_shape=[jax.ShapeDtypeStruct(shape, dtype) for shape, dtype in outs],
        in_specs=[spec(value.shape) for value in operands],
        out_specs=[spec(shape) for shape, _ in outs],
        compiler_params=pltpu.CompilerParams(vmem_limit_bytes=48000000),
        name=name,
    )(*operands)


def normed(values, scales):
    return values * lax.rsqrt(jnp.mean(values * values, -1, keepdims=True) + epsilon) * scales


def gated_unit(gate, up):
    return jax.nn.gelu(gate, approximate=True) * up


def times_rows(operand, weight):
    return lax.dot_general(
        operand, weight, (((1,), (1,)), ((), ())), preferred_element_type=wide
    )


def times(operand, weight):
    return jnp.dot(operand, weight, preferred_element_type=wide)


def row_sums(gradient, operand):
    return lax.dot_general(
        gradient, operand, (((0,), (0,)), ((), ())), preferred_element_type=wide
    )


def gain_sums(gradient, weight):
    return jnp.sum(gradient * weight.astype(wide), 0)


def member_columns(values):
    rows, width = values.shape
    count = lax.axis_size("g")
    split = values.reshape(rows, count, block_size, width // (count * block_size))
    return split.transpose(2, 0, 1, 3).reshape(block_size, rows, width // block_size)


def body(
    inputs,
    gain_first,
    branch_weight,
    branch_bias,
    conv_weight,
    conv_bias,
    gate_weight,
    gate_bias,
    decay,
    out_weight,
    out_bias,
    gain_second,
    mlp_weight,
    down_weight,
    cotangent,
):
    source = inputs[0].astype(wide)
    rows, width = source.shape
    heads, head_width = gate_weight.shape[1:3]
    count = lax.axis_size("g")
    half = count // 2
    all_rows = block_size * rows
    position = (
        lax.axis_index("g") * 4 + lax.axis_index("b3") * 2 + lax.axis_index("b2")
    ).reshape(1)
    flat = (rows, width)
    small = (8, width)

    branch_rows = group_gather(branch_weight).reshape(-1, width)
    mlp_rows = group_gather(mlp_weight)
    gate_rows = mlp_rows[:half].reshape(-1, width)
    up_rows = mlp_rows[half:].reshape(-1, width)
    down_rows, hidden_width = down_weight.shape
    unit = hidden_width // (half * block_size)
    down_split = (
        down_weight.reshape(down_rows, half, block_size, unit)
        .transpose(2, 0, 1, 3)
        .reshape(block_size, down_rows, half * unit)
    )
    down_columns = group_gather(block_swap(down_split, 0)).reshape(width, half * unit)
    out_rows = lax.all_gather(out_weight, places, axis=0, tiled=True)

    first_in = normed(source, gain_first).astype(low)
    first_all = block_gather(first_in, 1).reshape(all_rows, width)
    grad_out = cotangent[0]
    cot_all = block_gather(grad_out, 12).reshape(all_rows, width)
    pre_part = times_rows(first_all, branch_rows).astype(low)
    pre_part = pre_part.reshape(block_size, rows, 2 * width // block_size)
    pre = block_swap(pre_part, 2).reshape(block_size, rows, count, -1)
    pre = pre.transpose(1, 2, 0, 3).reshape(rows, 2 * width).astype(wide) + branch_bias
    gate_pre = pre[:, :width]
    conv_in = pre[:, width:]
    conv_before = rim_rows(conv_in[rows - 8 :], 1)

    rate = (-8.0 * jax.nn.softplus(decay))[None]
    conv_out, rgate, igate, decays, local, product, ends = by_heads(
        local_states_kernel,
        heads,
        head_width,
        (
            position,
            conv_in,
            conv_before,
            conv_weight,
            conv_bias[None],
            gate_weight,
            gate_bias,
            rate,
        ),
        [(flat, wide)] * 6 + [((2, width), wide)],
        "local_states",
    )
    states, mixed, entry = by_heads(
        full_states_kernel,
        heads,
        head_width,
        (position, local, product, seq_spread(ends, 3), gate_pre),
        [(flat, wide), (flat, low), (small, wide)],
        "full_states",
    )
    mixed_all = lax.all_gather(mixed, cube, axis=0, tiled=True)
    middle = source + times_rows(mixed, out_rows) + out_bias

    grad_hidden = times(cot_all, down_columns)
    second_in = normed(middle, gain_second).astype(low)
    second_all = block_gather(second_in, 4).reshape(all_rows, width)
    mlp_gate = times_rows(second_all, gate_rows)
    mlp_up = times_rows(second_all, up_rows)
    mlp_hidden, gated_back = jax.vjp(gated_unit, mlp_gate, mlp_up)
    mlp_hidden = mlp_hidden.astype(low)
    grad_gate, grad_up = (grad.astype(low) for grad in gated_back(grad_hidden))
    second_part = times(grad_gate, gate_rows) + times(grad_up, up_rows)
    grad_second = block_scatter(5, second_part.astype(low).reshape(block_size, rows, width))
    down_part = times_rows(mlp_hidden, down_columns).astype(low)
    down_part = down_part.reshape(block_size, rows, width)

    gate_sum = row_sums(grad_gate, second_all)
    up_sum = row_sums(grad_up, second_all)
    mlp_sum = jnp.concatenate([gate_sum.astype(low), up_sum.astype(low)], 0)
    mlp_grad = group_sum(mlp_sum.reshape(count, -1, width))
    gain_second_term = gain_sums(gate_sum, gate_rows) + gain_sums(up_sum, up_rows)
    gain_second_term = gain_second_term / gain_second
    down_sum = row_sums(cot_all, mlp_hidden)
    down_sum = group_sum(down_sum.reshape(count, block_size, down_rows, half * unit))
    down_grad = (
        block_swap(down_sum.astype(low), 7)
        .reshape(block_size, down_rows, half, unit)
        .transpose(1, 2, 0, 3)
        .reshape(down_rows, hidden_width)
        .astype(wide)
    )

    norm_second, second_back = jax.vjp(lambda values: normed(values, gain_second), middle)
    grad_middle = grad_out.astype(wide) + second_back(grad_second)[0]
    grad_branch = grad_middle.astype(low)
    out_bias_term = jnp.sum(grad_branch.astype(wide), 0)
    grad_mixed = times(grad_branch, out_rows)
    branch_all = block_swap(member_columns(grad_branch), 8).reshape(all_rows, -1)
    out_grad = group_sum(row_sums(branch_all, mixed_all).reshape(count, -1, width))

    adjoint, tail, adjoint_ends = by_heads(
        local_adjoint_kernel,
        heads,
        head_width,
        (grad_mixed, gate_pre, decays),
        [(flat, wide), (flat, wide), ((2, width), wide)],
        "local_adjoint",
    )
    grad_conv, gate_weight_term, gate_sums = by_heads(
        gate_grads_kernel,
        heads,
        head_width,
        (
            position,
            adjoint,
            tail,
            seq_spread(adjoint_ends, 9),
            decays,
            rgate,
            igate,
            conv_out,
            states,
            entry,
            conv_in,
            conv_before,
            gate_weight,
            rate,
        ),
        [(flat, wide), (gate_weight.shape, wide), (small, wide)],
        "gate_grads",
    )
    conv_after = rim_rows(grad_conv[:8], -1)
    pre_grads, pre_sums = by_heads(
        branch_grads_kernel,
        heads,
        head_width,
        (grad_conv, conv_after, conv_weight, gate_pre, grad_mixed, states),
        [((2, rows, width), low), (small, wide)],
        "branch_grads",
    )

    columns = pre_grads.reshape(2, rows, half, block_size, -1).transpose(3, 1, 0, 2, 4)
    pre_all = block_swap(columns.reshape(block_size, rows, -1), 10).reshape(all_rows, -1)
    branch_sum = row_sums(pre_all, first_all)
    branch_grad = group_sum(branch_sum.reshape(count, -1, width))
    gain_first_term = gain_sums(branch_sum, branch_rows) / gain_first
    first_part = times(pre_all, branch_rows).astype(low)

    vectors = jnp.concatenate(
        [
            gain_first_term[None],
            pre_sums[:2],
            gate_sums[4:8],
            gate_sums[3:4],
            gate_sums[:2],
            gate_sums[2:3] * (-8.0 * jax.nn.sigmoid(decay)),
            out_bias_term[None],
            gain_second_term[None],
            jnp.zeros((block_size - 13, width), wide),
        ],
        0,
    ).astype(low)
    gate_terms = gate_weight_term.reshape(block_size, -1, width).astype(low)
    gate_unit = gate_terms.shape[1]
    shared_part = jnp.concatenate(
        [
            gate_terms,
            vectors[:, None, :],
            jnp.zeros((block_size, 15, width), low),
        ],
        1,
    )
    scattered = block_scatter(11, first_part.reshape(block_size, rows, width), shared_part)
    grad_first = scattered[:rows]
    shared = group_total(scattered[rows:]).astype(low)
    norm_first, first_back = jax.vjp(lambda values: normed(values, gain_first), source)
    input_grad = (grad_middle + first_back(grad_first)[0])[None]

    down_part, shared = lax.optimization_barrier((down_part, shared))
    down_full = block_scatter(6, down_part)
    output = (middle + down_full).astype(low)[None]
    shared_all = block_gather(shared, 13).astype(wide)
    gate_weight_grad = shared_all[:, :gate_unit].reshape(gate_weight.shape)
    sums = shared_all[:, gate_unit]
    return (
        output,
        input_grad,
        sums[0],
        branch_grad,
        sums[1:3].reshape(-1),
        sums[3:7],
        sums[7],
        gate_weight_grad,
        sums[8:10],
        sums[10],
        out_grad,
        sums[11],
        sums[12],
        mlp_grad,
        down_grad,
    )


def solution(mesh):
    count = mesh.devices.size // block_size
    blocks = Mesh(mesh.devices.reshape((count,) + (2,) * len(cube)), places)
    tokens = P(fsdp_axes, seq_axes, None)
    owned = P(places, None)
    return jax.shard_map(
        body,
        mesh=blocks,
        in_specs=(
            tokens,
            P(),
            owned,
            P(),
            P(),
            P(),
            P(),
            P(),
            P(),
            owned,
            P(),
            P(),
            owned,
            owned,
            tokens,
        ),
        out_specs=(
            tokens,
            tokens,
            P(),
            owned,
            P(),
            P(),
            P(),
            P(),
            P(),
            P(),
            owned,
            P(),
            P(),
            owned,
            owned,
        ),
        check_vma=False,
    )
```

time: 3630 us -> 1060 us (0.29)
  waiting for transfers between devices: 1810 us -> 44.6 us
  local copies, waits for them, and re-layouts: 1190 us -> 82.9 us
  Pallas kernels: 0 us -> 711 us
  blocking collectives: 241 us -> 0 us
  other arithmetic: 153 us -> 44.6 us
  matrix products: 186 us -> 147 us
    reduce_scatter x4, waiting for transfers between devices: 1170 us -> 0.01 us  [group_sum(): lax.psum_scatter(partials.astype(low), 'g', scatter_dimension=0)]
    pallas_call x0 -> x19, Pallas kernels: none -> 711 us  [the longest x4 253 us: block_gather(): pl.pallas_call(functools.partial(gather_kernel, pieces), out_shape=jax.Sh...]
    slice x124 -> x8, local copies, waits for them, and re-layouts: 716 us -> 11 us  [the longest x1 4.93 us: body(): gate_weight_grad = shared_all[:, :gate_unit].reshape(gate_weight.shape)]
    all_gather x6 -> x5, waiting for transfers between devices: 338 us -> 0.07 us  [the longest x3 0.02 us: group_gather(): return lax.all_gather(values, 'g', axis=0)]
    all_to_all x4 -> x0, blocking collectives: 241 us -> none  [the longest x2 128 us: to_tokens(): lax.all_to_all(values, 'seq', split_axis=1, concat_axis=2, tiled=True)]
    pad x34 -> x0, local copies, waits for them, and re-layouts: 182 us -> none  [the longest x18 129 us: body(): lax.associative_scan(affine, (decay_ch, channel_pair[1]), axis=0)[1]]
    unnamed x16 -> x9, waiting for transfers between devices: 161 us -> 2.16 us
    psum x2 -> x0, waiting for transfers between devices: 128 us -> none  [body(): lax.psum((gain_first_term, branch_bias_term, conv_weight_term, conv_bias_...]
  transfers between devices with their start and end apart: 18 -> 12, of which waited for: 12 -> 2; matrix products, arithmetic and copies ran while one was open for 27% -> 22% of each run, Pallas kernels for 0% -> 68%
where the time goes in v1:
time: 1060 us; the launch traced here: 1050 us
  Pallas kernels  711 us (67%)
  matrix products  147 us (14%)
  local copies, waits for them, and re-layouts  82.9 us (8%)
  waiting for transfers between devices  44.6 us (4%)
  other arithmetic  44.6 us (4%)
  between operations  15.2 us (1%)
    pallas_call x4, Pallas kernels, block_gather(): pl.pallas_call(functools.partial(gather_kernel, pieces), out_shape=jax.Sh...  253 us
    pallas_call x3, Pallas kernels, block_scatter(): pl.pallas_call(functools.partial(scatter_kernel, pieces, len(partials)),...  205 us
    pallas_call x5, Pallas kernels, block_swap(): pl.pallas_call(swap_kernel, out_shape=jax.ShapeDtypeStruct(values.shape,...  150 us
    pallas_call x2, Pallas kernels, seq_spread(): pl.pallas_call(functools.partial(spread_kernel, group_count), out_shape=j...  73.1 us
    dot_general x5, matrix products, times(): return jnp.dot(operand, weight, preferred_element_type=wide)  53.5 us
    dot_general x5, matrix products, row_sums(): lax.dot_general(gradient, operand, (((0,), (0,)), ((), ())), preferred_el...  48.5 us
    dot_general x5, matrix products, times_rows(): lax.dot_general(operand, weight, (((1,), (1,)), ((), ())), preferred_elem...  44.7 us
    ppermute x1, waiting for transfers between devices, group_total(): total = total + lax.ppermute(values.astype(low), 'g', route).astype(wide)  38.5 us
  transfers between devices with their start and end apart: 12, of which 2 were waited for; matrix products, arithmetic and copies ran while one was open for 22% of the time, Pallas kernels for 68%

profile of v1, /device:TPU:1, one launch (start us, length us, event | category | flops | bytes accessed | tf_op | source)
XLA Modules:
  0.0 1050.2 jit_solution(12299267960721624498)
XLA Ops:
  13.5 35.6 %block_swap.6 = bf16[16,80,480]{2,1,0:T(8,128)(2,1)} custom-call(bf16[16,80,480]{2,1,0:T(8,128)(2,1)} %bitcast.144), custom_call_target="tpu_custom_call" | custom-call | tf_op jit(solution)/shard_map/block_swap/pallas_call | solution.py:277
  53.7 63.0 %block_gather.4 = bf16[16,128,2560]{2,1,0:T(8,128)(2,1)} custom-call(bf16[128,2560]{1,0:T(8,128)(2,1)} %fusion.26.x_ref), custom_call_target="tpu_custom_call" | custom-call | tf_op jit(solution)/shard_map/block_gather/pallas_call | solution.py:115
  118.6 8.0 convolution_convert_fusion.3
  128.1 41.9 %block_swap.5 = bf16[16,128,320]{2,1,0:T(8,128)(2,1)} custom-call(bf16[16,128,320]{2,1,0:T(8,128)(2,1)} %bitcast.142), custom_call_target="tpu_custom_call" | custom-call | tf_op jit(solution)/shard_map/block_swap/pallas_call | solution.py:277
  175.9 3.2 collective-permute-start
  180.8 9.3 local_states.1
  197.1 64.6 %seq_spread.2.ends_ref = f32[8,2,2560]{2,1,0:T(2,128)} custom-call(f32[2,2560]{1,0:T(2,128)} %copy-done.35), custom_call_target="tpu_custom_call" | custom-call | tf_op jit(solution)/shard_map/seq_spread/pallas_call | solution.py:360
  266.6 3.9 full_states.1
  272.3 82.5 %block_gather.6 = bf16[16,128,2560]{2,1,0:T(8,128)(2,1)} custom-call(bf16[128,2560]{1,0:T(8,128)(2,1)} %bitcast.143), custom_call_target="tpu_custom_call" | custom-call | tf_op jit(solution)/shard_map/block_gather/pallas_call | solution.py:115
  354.8 10.4 multiply_reduce_fusion.4
  368.7 80.3 %block_gather.5 = bf16[16,128,2560]{2,1,0:T(8,128)(2,1)} custom-call(bf16[128,2560]{1,0:T(8,128)(2,1)} %multiply_convert_fusion.2.x_ref), custom_call_target="tpu_custom_call" | custom-call | tf_op jit(solution)/shard_map/block_gather/pallas_call | solution.py:115
  449.0 10.6 %fusion.15 = f32[2048,480]{0,1:T(8,128)} fusion(bf16[2048,2560]{1,0:T(8,128)(2,1)} %bitcast.128, bf16[960,2560]{1,0:T(8,128)(2,1)} %all-gather.15.cloned.1.call-done), kind=kOutput, calls=%fused_computation.38 | convolution fusion | flops 5033164800 | bytes 16875520 | tf_op jit(solution)/shard_map/dot_general | solution.py:629
  459.6 7.2 fusion.19
  466.8 14.7 %multiply_convert_fusion = (bf16[2048,480]{0,1:T(8,128)(2,1)}, bf16[2048,480]{0,1:T(8,128)(2,1)S(1)}, bf16[2048,480]{0,1:T(8,128)(2,1)}) fusion(f32[2048,480]{0,1:T(8,128)} %fusion.19, f32[2048,480]{0,1:T(8,128)} %fusion.15, bf16[2048,2560]{1,0:T(8,128)(2,1)} %bitcast.132, bf16[2560,480]{1,0:T(8,128)(2,1)} %bitcast.157), kind=kOutput, calls=%fused_computation.21 | convolution fusion | flops 5058723840 | bytes 26705920 | tf_op jit(solution)/shard_map/dot_general | solution.py:635
  481.5 10.2 fusion.17
  491.6 13.2 %add_convert_fusion = bf16[2048,2560]{1,0:T(8,128)(2,1)} fusion(f32[2048,2560]{1,0:T(8,128)} %fusion.17, bf16[2048,480]{0,1:T(8,128)(2,1)} %get-tuple-element.64, bf16[960,2560]{1,0:T(8,128)(2,1)S(1)} %bitcast.156), kind=kOutput, calls=%fused_computation | convolution fusion | flops 5043650560 | bytes 35880960 | tf_op jit(solution)/shard_map/dot_general | solution.py:635
  504.9 57.5 %block_scatter.3 = f32[128,2560]{1,0:T(8,128)} custom-call(bf16[16,128,2560]{2,1,0:T(8,128)(2,1)} %bitcast.135), custom_call_target="tpu_custom_call" | custom-call | tf_op jit(solution)/shard_map/block_scatter/pallas_call | solution.py:234
  564.8 2.5 fusion.34
  569.8 21.2 %block_swap.8 = bf16[16,128,160]{2,1,0:T(8,128)(2,1)} custom-call(bf16[16,128,160]{2,1,0:T(8,128)(2,1)} %copy.105.x_ref), custom_call_target="tpu_custom_call" | custom-call | tf_op jit(solution)/shard_map/block_swap/pallas_call | solution.py:277
  592.5 6.8 fusion.10
  599.4 7.0 fusion.39.grad_mixed_ref
  606.4 2.7 local_adjoint.1
  611.9 8.5 seq_spread.3.ends_ref
  630.4 11.4 %gate_grads.1 = (f32[128,2560]{1,0:T(8,128)S(1)}, f32[2,10,256,256]{3,2,1,0:T(8,128)}, f32[8,2560]{1,0:T(8,128)S(1)}) custom-call(s32[1]{0:T(128)} %bitcast.1.position_ref, f32[128,2560]{1,0:T(8,128)S(1)} %copy-done.16, f32[128,2560]{1,0:T(8,128)S(1)} %copy-done.18, f32[8,2,2560]{2,1,0:T(2,128)S(1)} %copy-done.24, f32[128,2560]{1,0:T(8,128)S(1)} %copy-done.9, ...), custom_call_target="tpu_custom_call" | custom-call | tf_op jit(solution)/shard_map/gate_grads/pallas_call | solution.py:609
  643.1 3.9 collective-permute-done.1.after_ref
  652.0 29.2 %block_swap.7 = bf16[16,128,320]{2,1,0:T(8,128)(2,1)} custom-call(bf16[16,128,320]{2,1,0:T(8,128)(2,1)} %copy.98.x_ref), custom_call_target="tpu_custom_call" | custom-call | tf_op jit(solution)/shard_map/block_swap/pallas_call | solution.py:277
  681.2 9.7 fusion.37
  691.1 8.6 fusion.2
  699.7 2.7 copy.107
  703.9 11.0 %fusion.40 = f32[480,2560]{1,0:T(8,128)} fusion(bf16[2048,480]{0,1:T(8,128)(2,1)S(1)} %copy-done.72, bf16[2048,2560]{1,0:T(8,128)(2,1)} %bitcast.129), kind=kOutput, calls=%fused_computation.101 | convolution fusion | flops 5033164800 | bytes 17367040 | tf_op jit(solution)/shard_map/dot_general | solution.py:639
  714.9 4.3 convert_element_type.165
  719.2 5.0 convert_element_type.166
  724.2 12.4 %multiply_reduce_fusion = (f32[2560]{0:T(1024)S(1)}, f32[2560]{0:T(1024)S(1)}, bf16[480,2560]{1,0:T(8,128)(2,1)S(1)}, bf16[480,2560]{1,0:T(8,128)(2,1)S(1)}) fusion(bf16[960,2560]{1,0:T(8,128)(2,1)} %all-gather.15.cloned.1.call-done, f32[480,2560]{1,0:T(8,128)} %fusion.40, bf16[2048,480]{0,1:T(8,128)(2,1)} %get-tuple-element.64, bf16[2048,2560]{1,0:T(8,128)(2,1)} %bitcast.130), kind=kOutput, calls=%fused_computation.8 | convolution fusion | flops 5042990080 | bytes 27217920 | tf_op jit(solution)/shard_map/dot_general | solution.py:639
  736.6 2.8 pad_maximum_fusion
  740.7 8.5 convolution_convert_fusion
  751.1 2.7 maximum_maximum_fusion.refs_1_
  753.8 8.4 convolution_convert_fusion.1
  762.3 90.3 %block_scatter.4 = f32[176,2560]{1,0:T(8,128)} custom-call(bf16[16,128,2560]{2,1,0:T(8,128)(2,1)} %bitcast.139, bf16[16,48,2560]{2,1,0:T(8,128)(2,1)} %maximum_maximum_fusion.refs_1_), custom_call_target="tpu_custom_call" | custom-call | tf_op jit(solution)/shard_map/block_scatter/pallas_call | solution.py:234
  855.5 38.5 %collective-permute-done.2 = bf16[48,2560]{1,0:T(8,128)(2,1)S(1)} collective-permute-done((bf16[48,2560]{1,0:T(8,128)(2,1)S(1)}, bf16[48,2560]{1,0:T(8,128)(2,1)S(1)}, u32[]{:S(2)}, u32[]{:S(2)}) %collective-permute-start.2) | collective-permute-done | bytes 245792 | tf_op jit(solution)/shard_map/ppermute | solution.py:305
  895.8 27.4 %block_gather.7 = bf16[16,48,2560]{2,1,0:T(8,128)(2,1)} custom-call(bf16[48,2560]{1,0:T(8,128)(2,1)} %add_convert_fusion.2.x_ref), custom_call_target="tpu_custom_call" | custom-call | tf_op jit(solution)/shard_map/block_gather/pallas_call | solution.py:115
  923.1 4.9 slice.131
  928.1 4.2 convert_element_type.175
  932.3 6.8 reshape.320
  941.9 57.3 %block_scatter.5 = f32[128,2560]{1,0:T(8,128)} custom-call(bf16[16,128,2560]{2,1,0:T(8,128)(2,1)} %bitcast.134), custom_call_target="tpu_custom_call" | custom-call | tf_op jit(solution)/shard_map/block_scatter/pallas_call | solution.py:234
  1001.0 5.1 fusion.23
  1010.5 22.3 %block_swap.9 = bf16[16,80,480]{2,1,0:T(8,128)(2,1)} custom-call(bf16[16,80,480]{2,1,0:T(8,128)(2,1)} %bitcast.151), custom_call_target="tpu_custom_call" | custom-call | tf_op jit(solution)/shard_map/block_swap/pallas_call | solution.py:277
  1036.1 2.6 reshape.330
  1038.7 4.6 bitcast_convert_fusion
  (241 shorter events, 85.8 us)
Async XLA Ops:
  7.2 2.3 copy-start.47
  7.2 111.4 %all-gather.13.cloned.1.call-start = ((), (), s32[]{:S(2)}) async-start(), calls=%async_computation.10 | async-start | bytes 2457600 | tf_op jit(solution)/shard_map/all_gather | solution.py:293
  7.9 346.9 %all-gather.9.cloned.1.call-start = ((), (), s32[]{:S(2)}) async-start(), calls=%async_computation.4 | async-start | bytes 13516800 | tf_op jit(solution)/shard_map/all_gather | solution.py:696
  8.7 440.3 %all-gather.15.cloned.1.call-start = ((), (), s32[]{:S(2)}) async-start(), calls=%async_computation.11 | async-start | bytes 7372800 | tf_op jit(solution)/shard_map/all_gather | solution.py:293
  9.4 457.4 %all-gather.17.cloned.1.call-start = ((), (), s32[]{:S(2)}) async-start(), calls=%async_computation.12 | async-start | bytes 3932160 | tf_op jit(solution)/shard_map/all_gather | solution.py:293
  13.4 38.1 %copy-start.51 = (f32[2560]{0:T(1024)S(1)}, f32[2560]{0:T(1024)}, u32[]{:S(2)}) copy-start(f32[2560]{0:T(1024)} %param.16) | copy-start | bytes 30724
  49.1 543.3 %all-gather.11.cloned.1.call-start = ((), (), s32[]{:S(2)}) async-start(), calls=%async_computation.6 | async-start | bytes 11141120 | tf_op jit(solution)/shard_map/all_gather | solution.py:736
  53.7 63.0 %copy-start.56 = (f32[2560]{0:T(1024)S(1)}, f32[2560]{0:T(1024)}, u32[]{:S(2)}) copy-start(f32[2560]{0:T(1024)} %param.23) | copy-start | bytes 30724
  53.7 64.2 %copy-start.57 = (f32[2560]{0:T(1024)S(1)}, f32[2560]{0:T(1024)}, u32[]{:S(2)}) copy-start(f32[2560]{0:T(1024)} %param.20) | copy-start | bytes 30724
  175.9 4.9 copy-start.27
  175.9 4.9 copy-start.30
  175.9 4.9 copy-start.34
  175.9 4.9 copy-start.37
  175.9 4.9 collective-permute-start
  180.8 9.3 copy-start.25
  272.2 733.9 %reduce-scatter.7.cloned.1.call-start = ((), (), s32[]{:S(2)}) async-start(), calls=%async_computation.7 | async-start | bytes 1228800 | tf_op jit(solution)/shard_map/reduce_scatter | solution.py:297
  354.8 11.5 %copy-start.48 = (f32[2560]{0:T(1024)S(1)}, f32[2560]{0:T(1024)}, u32[]{:S(2)}) copy-start(f32[2560]{0:T(1024)} %param.26) | copy-start | bytes 30724
  449.0 10.7 %copy-start.41 = (bf16[16,128,2560]{2,1,0:T(8,128)(2,1)S(1)}, bf16[16,128,2560]{2,1,0:T(8,128)(2,1)}, u32[]{:S(2)}) copy-start(bf16[16,128,2560]{2,1,0:T(8,128)(2,1)} %block_gather.5) | copy-start | bytes 31457284
  449.0 10.7 %copy-start.69 = (bf16[960,2560]{1,0:T(8,128)(2,1)S(1)}, bf16[960,2560]{1,0:T(8,128)(2,1)}, u32[]{:S(2)}) copy-start(bf16[960,2560]{1,0:T(8,128)(2,1)} %all-gather.15.cloned.1.call-done) | copy-start | bytes 14745604
  459.6 21.9 %slice-start = ((s8[4915200]{0:T(1024)(128)(4,1)}), s8[720896]{0:T(1024)(128)(4,1)S(1)}, s32[]{:S(2)}) async-start(s8[4915200]{0:T(1024)(128)(4,1)} %bitcast.155), calls=%async_computation.13 | async-start | bytes 1441792
  466.8 14.7 %slice-start.1 = ((s8[4915200]{0:T(1024)(128)(4,1)}), s8[4194304]{0:T(1024)(128)(4,1)S(1)}, s32[]{:S(2)}) async-start(s8[4915200]{0:T(1024)(128)(4,1)} %bitcast.155), calls=%async_computation.14 | async-start | bytes 8388608
  481.5 10.2 copy-start.71
  562.5 2.3 copy-start.45
  562.5 2.3 copy-start.49
  564.8 3.7 copy-start.63
  592.5 6.9 copy-start.43
  599.3 7.1 copy-start.1
  599.3 7.1 copy-start.8
  599.3 408.7 %reduce-scatter.5.cloned.1.call-start = ((), (), s32[]{:S(2)}) async-start(), calls=%async_computation.5 | async-start | bytes 2457600 | tf_op jit(solution)/shard_map/reduce_scatter | solution.py:297
  606.4 2.8 copy-start.3
  630.4 16.6 %copy-start.2 = (f32[128,2560]{1,0:T(8,128)S(1)}, f32[128,2560]{1,0:T(8,128)}, u32[]{:S(2)}) copy-start(f32[128,2560]{1,0:T(8,128)} %get-tuple-element.73.gate_pre_ref) | copy-start | bytes 3932164
  630.4 16.6 %copy-start.4 = (f32[128,2560]{1,0:T(8,128)S(1)}, f32[128,2560]{1,0:T(8,128)}, u32[]{:S(2)}) copy-start(f32[128,2560]{1,0:T(8,128)} %copy-done.3) | copy-start | bytes 3932164
  630.4 16.6 %copy-start.6 = (f32[128,2560]{1,0:T(8,128)S(1)}, f32[128,2560]{1,0:T(8,128)}, u32[]{:S(2)}) copy-start(f32[128,2560]{1,0:T(8,128)} %copy-done.5) | copy-start | bytes 3932164
  641.8 7.7 copy-start.28
  641.8 5.2 collective-permute-start.1
  691.0 319.6 %reduce-scatter.11.cloned.1.call-start = ((), (), s32[]{:S(2)}) async-start(), calls=%async_computation.9 | async-start | bytes 3932160 | tf_op jit(solution)/shard_map/reduce_scatter | solution.py:297
  702.3 12.6 %copy-start.29 = (f32[8,2560]{1,0:T(8,128)S(1)}, f32[8,2560]{1,0:T(8,128)}, u32[]{:S(2)}) copy-start(f32[8,2560]{1,0:T(8,128)} %copy-done.28) | copy-start | bytes 245764
  702.3 336.3 %reduce-scatter.9.cloned.1.call-start = ((), (), s32[]{:S(2)}) async-start(), calls=%async_computation.8 | async-start | bytes 7372800 | tf_op jit(solution)/shard_map/reduce_scatter | solution.py:297
  736.6 2.9 copy-start.70
  736.6 4.1 copy-start.73
  751.1 2.7 copy-start.44
  751.1 2.7 copy-start.46
  852.5 2.9 copy-start.68
  853.6 40.4 %collective-permute-start.2 = (bf16[48,2560]{1,0:T(8,128)(2,1)S(1)}, bf16[48,2560]{1,0:T(8,128)(2,1)S(1)}, u32[]{:S(2)}, u32[]{:S(2)}) collective-permute-start(bf16[48,2560]{1,0:T(8,128)(2,1)S(1)} %slice.167), channel_id=1, source_target_pairs={{0,16},{16,0},{1,17},{17,1},{2,18},{18,2},{3,19},{19,3},{4,20},{20... | collective-permute-start | bytes 737288 | tf_op jit(solution)/shard_map/ppermute | solution.py:305
  923.1 4.9 copy-start.39
  941.9 59.1 %copy-start.60 = (f32[128]{0:T(128)S(1)}, f32[128]{0:T(128)}, u32[]{:S(2)}) copy-start(f32[128]{0:T(128)} %copy-done.58) | copy-start | bytes 1540
  941.9 59.1 %copy-start.62 = (f32[128]{0:T(128)S(1)}, f32[128]{0:T(128)}, u32[]{:S(2)}) copy-start(f32[128]{0:T(128)} %copy-done.61) | copy-start | bytes 1540
  941.9 59.1 %copy-start.64 = (f32[128]{0:T(128)S(1)}, f32[128]{0:T(128)}, u32[]{:S(2)}) copy-start(f32[128]{0:T(128)} %copy-done.63) | copy-start | bytes 1540
  (40 other events, 45.6 us)
Sparse Core Ops, SparseCore 0:
  9.5 48.3 all-gather.12
  60.8 127.2 all-gather.8
  189.6 121.7 all-gather.14
  312.8 67.1 all-gather.16
  382.0 86.7 all-gather.10
  599.4 28.2 reduce-scatter.6
  691.1 43.3 reduce-scatter.4
  736.7 65.6 reduce-scatter.10
  805.3 125.3 reduce-scatter.8

commit v2 on v1

--- a/solution.py
+++ b/solution.py
@@ -17,8 +17,8 @@
 places = ("g",) + cube
 seq_axes = ("g", "b3", "b2")
 fsdp_axes = ("b1", "b0")
-orders = (("b3", "b1", "b2"), ("b3", "b2", "b1"))
-back_orders = (("b1", "b2", "b3"), ("b2", "b1", "b3"))
+first_orders = (("b3", "b1", "b2"), ("b3", "b2", "b1"))
+even_orders = (("b1", "b3", "b2"), ("b2", "b3", "b1"))
 
 anywhere = pl.BlockSpec(memory_space=pl.ANY)
 in_vmem = pl.BlockSpec(memory_space=pltpu.VMEM)
@@ -42,37 +42,120 @@
     return {axis: 1 - lax.axis_index(axis) for axis in cube if mask & bit_of(axis)}
 
 
-def greet(masks):
+def greet(masks, paired):
     barrier = pltpu.get_barrier_semaphore()
-    for mask in masks:
+    targets = [device_at(mask) for mask in masks] + [other_block()] * paired
+    for target in targets:
         pl.semaphore_signal(
-            barrier, inc=1, device_id=device_at(mask), device_id_type=pl.DeviceIdType.MESH
+            barrier, inc=1, device_id=target, device_id_type=pl.DeviceIdType.MESH
         )
-    pl.semaphore_wait(barrier, len(masks))
-
-
-def split_rows(rows, unit):
-    tiles = rows // unit
-    sizes = [(tiles + 1 - part) // 2 * unit for part in range(2)]
-    return [(part, part * sizes[0], size) for part, size in enumerate(sizes) if size > 0]
-
-
-def remote_params(collective):
+    pl.semaphore_wait(barrier, len(targets))
+
+
+def other_block():
+    return {"g": 1 - lax.axis_index("g")}
+
+
+class Ride:
+    def __init__(self, riders):
+        self.arrays = [array for array, _, _ in riders]
+        self.ranges = [(start, size) for _, start, size in riders]
+        self.chunks = []
+        for number, (array, start, size) in enumerate(riders):
+            step = 16 if array.shape[1] > 4096 else (48 if array.shape[1] > 1024 else 160)
+            for begin in range(0, size, step):
+                self.chunks.append((number, start + begin, begin, min(step, size - begin)))
+
+    def shapes(self):
+        return [
+            jax.ShapeDtypeStruct((size,) + array.shape[1:], array.dtype)
+            for array, (_, size) in zip(self.arrays, self.ranges)
+        ]
+
+    def semaphores(self):
+        count = max(1, len(self.chunks))
+        return [pltpu.SemaphoreType.DMA((count,)), pltpu.SemaphoreType.DMA((count,))]
+
+    def enter(self, inputs, outputs, send_sem, recv_sem):
+        self.copies = [
+            pltpu.make_async_remote_copy(
+                src_ref=inputs[number].at[pl.ds(begin, size)],
+                dst_ref=outputs[number].at[pl.ds(start, size)],
+                send_sem=send_sem.at[chunk],
+                recv_sem=recv_sem.at[chunk],
+                device_id=other_block(),
+                device_id_type=pl.DeviceIdType.MESH,
+            )
+            for chunk, (number, begin, start, size) in enumerate(self.chunks)
+        ]
+        self.started = 0
+
+    def start(self, share):
+        until = -(-len(self.copies) * share[0] // share[1])
+        for copy in self.copies[self.started : until]:
+            copy.start()
+        self.started = max(self.started, until)
+
+    def finish(self):
+        self.start((1, 1))
+        for copy in self.copies:
+            copy.wait()
+
+
+def split_rows(rows, orders):
+    tiles = rows // 16
+    pieces = []
+    start = 0
+    for number, order in enumerate(orders):
+        size = (tiles + len(orders) - 1 - number) // len(orders) * 16
+        if size:
+            pieces.append((order, start, size))
+        start += size
+    return pieces
+
+
+def hop_orders(riders):
+    return first_orders + even_orders if riders else even_orders
+
+
+def remote_params(collective, held):
     return pltpu.CompilerParams(
-        collective_id=collective, has_side_effects=True, vmem_limit_bytes=whole_vmem
-    )
-
-
-def gather_kernel(pieces, x_ref, out_ref, send_sem, recv_sem, local_sem):
-    greet([bit_of(axis) for axis in cube])
+        collective_id=collective,
+        has_side_effects=True,
+        vmem_limit_bytes=min(whole_vmem, held + (2 << 20)),
+    )
+
+
+def bytes_of(*values):
+    return sum(value.size * value.dtype.itemsize for value in values)
+
+
+def move_kernel(pieces, swap_count, ride, *refs):
+    refs = list(refs)
+
+    def take(count):
+        taken = refs[:count]
+        del refs[:count]
+        return taken
+
+    gathers = 1 if pieces else 0
+    count = len(ride.arrays)
+    sources, swaps, riders = take(gathers), take(swap_count), take(count)
+    targets, swapped, arrivals = take(gathers), take(swap_count), take(count)
+    send_sem, recv_sem, local_sem, swap_send, swap_recv, ride_send, ride_recv = refs
+    neighbours = [bit_of(axis) for axis in cube]
+    greet(list(range(1, block_size)) if swap_count else neighbours, count > 0)
+    ride.enter(riders, arrivals, ride_send, ride_recv)
     sent = []
+    here = slot_at(0)
+    locals_ = []
 
     def push(part, start, size, mask, axis):
         slot = slot_at(mask)
-        source = (x_ref if mask == 0 else out_ref.at[slot]).at[pl.ds(start, size)]
+        source = (sources[0] if mask == 0 else targets[0].at[slot]).at[pl.ds(start, size)]
         copy = pltpu.make_async_remote_copy(
             src_ref=source,
-            dst_ref=out_ref.at[slot].at[pl.ds(start, size)],
+            dst_ref=targets[0].at[slot].at[pl.ds(start, size)],
             send_sem=send_sem.at[len(sent)],
             recv_sem=recv_sem.at[part, mask ^ bit_of(axis)],
             device_id=device_at(bit_of(axis)),
@@ -82,14 +165,12 @@
         sent.append(copy)
 
     def arrive(part, start, size, mask):
-        target = out_ref.at[slot_at(mask)].at[pl.ds(start, size)]
+        target = targets[0].at[slot_at(mask)].at[pl.ds(start, size)]
         pltpu.make_async_copy(target, target, recv_sem.at[part, mask]).wait()
 
-    own = pltpu.make_async_copy(x_ref, out_ref.at[slot_at(0)], local_sem)
-    own.start()
-    for stage in range(4):
-        for part, start, size in pieces:
-            order = orders[part] + ("b0",)
+    def forward(stage):
+        for part, (order, start, size) in enumerate(pieces):
+            order = order + ("b0",)
             masks = [0]
             if stage > 0:
                 for axis in order[: stage - 1]:
@@ -100,193 +181,292 @@
                     arrive(part, start, size, mask)
                 for axis in order[stage:]:
                     push(part, start, size, mask, axis)
-    for part, start, size in pieces:
+
+    forward(0)
+    swap_copies = []
+    for mask in (15, 14, 13, 11, 7, 12, 10, 6, 9, 5, 3, 8, 4, 2, 1):
+        for number in range(swap_count):
+            copy = pltpu.make_async_remote_copy(
+                src_ref=swaps[number].at[slot_at(mask)],
+                dst_ref=swapped[number].at[here],
+                send_sem=swap_send.at[number, mask],
+                recv_sem=swap_recv.at[number, mask],
+                device_id=device_at(mask),
+                device_id_type=pl.DeviceIdType.MESH,
+            )
+            copy.start()
+            swap_copies.append(copy)
+    ride.start((1, 1))
+    for number in range(gathers):
+        locals_.append((sources[number], targets[number].at[here]))
+    for number in range(swap_count):
+        locals_.append((swaps[number].at[here], swapped[number].at[here]))
+    locals_ = [
+        pltpu.make_async_copy(source, target, local_sem.at[number])
+        for number, (source, target) in enumerate(locals_)
+    ]
+    for copy in locals_:
+        copy.start()
+    for stage in (1, 2, 3):
+        forward(stage)
+    for part, (_, start, size) in enumerate(pieces):
         for mask in range(block_size):
             if mask & bit_of("b0"):
                 arrive(part, start, size, mask)
-    for copy in sent:
+    for number in range(swap_count):
+        for mask in range(1, block_size):
+            target = swapped[number].at[slot_at(mask)]
+            pltpu.make_async_copy(target, target, swap_recv.at[number, mask]).wait()
+    for copy in sent + swap_copies:
         copy.wait_send()
-    own.wait()
-
-
-def block_gather(values, collective):
-    rows, width = values.shape
-    pieces = split_rows(rows, 16)
+    for copy in locals_:
+        copy.wait()
+    ride.finish()
+
+
+def block_move(gathered, swapped, collective, riders=()):
+    pieces = []
+    shapes = []
+    gathers = [] if gathered is None else [gathered]
+    for values in gathers:
+        pieces = split_rows(values.shape[0], hop_orders(riders))
+        shapes.append(jax.ShapeDtypeStruct((block_size,) + values.shape, values.dtype))
+    for values in swapped:
+        shapes.append(jax.ShapeDtypeStruct(values.shape, values.dtype))
+    ride = Ride(riders)
+    swaps = max(1, len(swapped))
+    moved = len(gathers) * [anywhere] + len(swapped) * [in_vmem] + len(riders) * [anywhere]
     return pl.pallas_call(
-        functools.partial(gather_kernel, pieces),
-        out_shape=jax.ShapeDtypeStruct((block_size, rows, width), values.dtype),
-        in_specs=[in_vmem],
-        out_specs=anywhere,
+        functools.partial(move_kernel, pieces, len(swapped), ride),
+        out_shape=shapes + ride.shapes(),
+        in_specs=len(gathers) * [in_vmem] + moved[len(gathers) :],
+        out_specs=moved,
         scratch_shapes=[
-            pltpu.SemaphoreType.DMA((15 * len(pieces),)),
-            pltpu.SemaphoreType.DMA((2, block_size)),
-            pltpu.SemaphoreType.DMA,
-        ],
-        compiler_params=remote_params(collective),
-        name="block_gather",
-    )(values)
-
-
-def scatter_kernel(pieces, source_count, *refs):
-    sources = refs[:source_count]
-    out_ref, own, away, send_sem, recv_sem, load_sem = refs[source_count:]
+            pltpu.SemaphoreType.DMA((max(1, 15 * len(pieces)),)),
+            pltpu.SemaphoreType.DMA((max(1, len(pieces)), block_size)),
+            pltpu.SemaphoreType.DMA((1 + swaps,)),
+            pltpu.SemaphoreType.DMA((swaps, block_size)),
+            pltpu.SemaphoreType.DMA((swaps, block_size)),
+        ]
+        + ride.semaphores(),
+        compiler_params=remote_params(
+            collective, 2 * bytes_of(*gathers) + 4 * bytes_of(*swapped)
+        ),
+        name="block_move",
+    )(*gathers, *swapped, *ride.arrays)
+
+
+def scatter_kernel(pieces, product_rows, transposed, extra_count, ride, *refs):
+    refs = list(refs)
+
+    def take(count):
+        taken = refs[:count]
+        del refs[:count]
+        return taken
+
+    products = len(transposed)
+    count = len(ride.arrays)
+    left_refs, right_refs, extras, riders = (
+        take(products),
+        take(products),
+        take(extra_count),
+        take(count),
+    )
+    (out_ref,), arrivals = take(1), take(count)
+    left_rows = take(products)
+    held, away, send_sem, recv_sem, left_sem, load_sem, ride_send, ride_recv = refs
     core = bit_of("b0")
-    greet([bit_of(axis) for axis in cube])
+    members = 2 * product_rows
+    order_count = [sum(mask >> bit & 1 for bit in range(len(cube))) for mask in range(block_size)]
+    steps = sorted(
+        (mask for mask in range(block_size) if not mask & core),
+        key=lambda mask: (-order_count[mask], -mask),
+    )
+    here = lax.axis_index("b0")
+
+    def left_copy(number, step):
+        pair = slot_at(steps[step]) // 2
+        rows = pl.ds(pl.multiple_of(pair * members, members), members)
+        return pltpu.make_async_copy(
+            left_refs[number].at[rows], left_rows[number].at[step], left_sem.at[number, step]
+        )
+
+    for step in range(8):
+        for number in range(products):
+            left_copy(number, step).start()
+    greet([bit_of(axis) for axis in cube], count > 0)
+    ride.enter(riders, arrivals, ride_send, ride_recv)
     sent = []
 
-    def push(source, number, hop, index, axis):
+    def slot_of(order, hop, mask):
+        clear = [bit_of(axis) for axis in order[:hop]] + [core]
+        masks = [m for m in range(block_size) if not any(m & bit for bit in clear)]
+        return (0, 8, 12, 14)[hop] + masks.index(mask)
+
+    def push(source, number, slot, axis):
         _, _, _, start, size = pieces[number]
         copy = pltpu.make_async_remote_copy(
             src_ref=source,
-            dst_ref=away.at[hop, index].at[pl.ds(start, size)],
+            dst_ref=away.at[slot].at[pl.ds(start, size)],
             send_sem=send_sem.at[len(sent)],
-            recv_sem=recv_sem.at[number, hop, index],
+            recv_sem=recv_sem.at[number, slot],
             device_id=device_at(bit_of(axis)),
             device_id_type=pl.DeviceIdType.MESH,
         )
         copy.start()
         sent.append(copy)
 
-    def sequence(order):
-        first, second, third = (bit_of(axis) for axis in back_orders[order])
-        return [
-            first | second | third,
-            first | second,
-            first | third,
-            first,
-            second | third,
-            second,
-            third,
-            0,
-        ]
-
-    def arrive(number, hop, index):
+    def arrive(number, slot):
         _, _, _, start, size = pieces[number]
-        target = away.at[hop, index].at[pl.ds(start, size)]
-        pltpu.make_async_copy(target, target, recv_sem.at[number, hop, index]).wait()
+        target = away.at[slot].at[pl.ds(start, size)]
+        pltpu.make_async_copy(target, target, recv_sem.at[number, slot]).wait()
+
+    tile = 512
+
+    def work_out(step):
+        for number in range(products):
+            left_copy(number, step).wait()
+
+        def columns(i, carry):
+            at = pl.ds(pl.multiple_of(i * tile, tile), tile)
+            total = None
+            for number in range(products):
+                left = left_rows[number][step]
+                if transposed[number]:
+                    term = lax.dot_general(
+                        left,
+                        right_refs[number][at, :],
+                        (((1,), (1,)), ((), ())),
+                        preferred_element_type=wide,
+                    )
+                else:
+                    term = jnp.dot(left, right_refs[number][:, at], preferred_element_type=wide)
+                total = term if total is None else total + term
+            total = total.astype(low)
+            held[step, 0, pl.ds(0, product_rows), at] = total[:product_rows]
+            held[step, 1, pl.ds(0, product_rows), at] = total[product_rows:]
+            return carry
+
+        lax.fori_loop(0, out_ref.shape[1] // tile, columns, 0)
+        for number, (order, extra, begin, start, size) in enumerate(pieces):
+            rows = pl.ds(begin, size)
+            if extra:
+                source = extras[0].at[slot_at(steps[step] | core)].at[rows]
+            else:
+                source = held.at[step, 1 - here].at[rows]
+            push(source, number, slot_of(order, 0, steps[step]), "b0")
 
     loads = {}
-    for turn in range(8):
-        for number, (order, source, begin, start, size) in enumerate(pieces):
-            mask = sequence(order)[turn]
-            rows = pl.ds(begin, size)
-            push(
-                sources[source].at[slot_at(mask | core)].at[rows], number, 0, mask >> 1, "b0"
-            )
-    for turn in range(8):
-        for number, (order, source, begin, start, size) in enumerate(pieces):
-            mask = sequence(order)[turn]
-            load = pltpu.make_async_copy(
-                sources[source].at[slot_at(mask)].at[pl.ds(begin, size)],
-                own.at[mask >> 1].at[pl.ds(start, size)],
-                load_sem.at[number, mask >> 1],
-            )
-            load.start()
-            loads[number, mask] = load
-    for turn in range(8):
-        for number, (order, source, begin, start, size) in enumerate(pieces):
-            mask = sequence(order)[turn]
-            index = mask >> 1
-            bits = [bit_of(axis) for axis in back_orders[order]]
-            loads[number, mask].wait()
-            hops = [0]
-            arrive(number, 0, index)
+    for step in range(8):
+        for number, (order, extra, begin, start, size) in enumerate(pieces):
+            if extra:
+                loads[number, step] = pltpu.make_async_copy(
+                    extras[0].at[slot_at(steps[step])].at[pl.ds(begin, size)],
+                    held.at[step, here].at[pl.ds(start, size)],
+                    load_sem.at[number, step],
+                )
+                loads[number, step].start()
+
+    def pass_on(step):
+        mask = steps[step]
+        for number, (order, extra, begin, start, size) in enumerate(pieces):
+            bits = [bit_of(axis) for axis in order]
+            if extra:
+                loads[number, step].wait()
+            slots = [slot_of(order, 0, mask)]
             target = None
             for hop, bit in enumerate(bits):
                 if mask & bit:
                     target = hop
                     break
-                arrive(number, hop + 1, index)
-                hops.append(hop + 1)
-
-            def add_tile(i, carry, index=index, start=start, hops=hops, target=target):
+                slots.append(slot_of(order, hop + 1, mask))
+            for slot in slots:
+                arrive(number, slot)
+
+            def add_tile(i, carry, start=start, slots=slots, target=target):
                 at = pl.ds(pl.multiple_of(start + i * 16, 16), 16)
-                total = own[index, at, :].astype(wide)
-                for hop in hops:
-                    total = total + away[hop, index, at, :].astype(wide)
+                total = held[step, here, at, :].astype(wide)
+                for slot in slots:
+                    total = total + away[slot, at, :].astype(wide)
                 if target is None:
                     out_ref[at, :] = total.astype(out_ref.dtype)
                 else:
-                    own[index, at, :] = total.astype(own.dtype)
+                    held[step, here, at, :] = total.astype(low)
                 return carry
 
             lax.fori_loop(0, size // 16, add_tile, 0)
             if target is not None:
                 push(
-                    own.at[index].at[pl.ds(start, size)],
+                    held.at[step, here].at[pl.ds(start, size)],
                     number,
-                    target + 1,
-                    (mask ^ bits[target]) >> 1,
-                    back_orders[order][target],
+                    slot_of(order, target + 1, mask ^ bits[target]),
+                    order[target],
                 )
+
+    for step in range(9):
+        if step < 8:
+            work_out(step)
+        if step == 0:
+            ride.start((1, 1))
+        if step > 0:
+            pass_on(step - 1)
     for copy in sent:
         copy.wait_send()
-
-
-def block_scatter(collective, *partials):
-    width = partials[0].shape[2]
-    pieces = []
-    rows = 0
-    for source, partial in enumerate(partials):
-        for order, begin, size in split_rows(partial.shape[1], 16):
-            pieces.append((order, source, begin, rows + begin, size))
-        rows += partial.shape[1]
+    ride.finish()
+
+
+def block_scatter(products, collective, riders=(), extra=None):
+    ride = Ride(riders)
+    lefts = [left for left, _, _ in products]
+    rights = [right for _, right, _ in products]
+    transposed = [flag for _, _, flag in products]
+    product_rows = lefts[0].shape[0] // block_size
+    width = rights[0].shape[0] if transposed[0] else rights[0].shape[1]
+    extras = [] if extra is None else [extra]
+    orders = [order[::-1] for order in hop_orders(riders)]
+    pieces = [
+        (order, 0, start, start, size) for order, start, size in split_rows(product_rows, orders)
+    ]
+    rows = product_rows
+    for values in extras:
+        for order, start, size in split_rows(values.shape[1], orders):
+            pieces.append((order, 1, start, rows + start, size))
+        rows += values.shape[1]
+    padded = [-(-left.shape[1] // 128) * 128 for left in lefts]
+    held_bytes = (
+        (16 + 15) * rows * width * 2
+        + 2 * rows * width * 4
+        + sum(2 * left.shape[0] * size for left, size in zip(lefts, padded))
+        + 2 * sum(2 * size * width for size in padded)
+        + (8 << 20)
+    )
     return pl.pallas_call(
-        functools.partial(scatter_kernel, pieces, len(partials)),
-        out_shape=jax.ShapeDtypeStruct((rows, width), wide),
-        in_specs=[anywhere] * len(partials),
-        out_specs=in_vmem,
-        scratch_shapes=[
-            pltpu.VMEM((8, rows, width), low),
-            pltpu.VMEM((4, 8, rows, width), low),
+        functools.partial(
+            scatter_kernel, pieces, product_rows, transposed, len(extras), ride
+        ),
+        out_shape=[jax.ShapeDtypeStruct((rows, width), wide)] + ride.shapes(),
+        in_specs=[anywhere] * len(lefts)
+        + [in_vmem] * len(rights)
+        + [anywhere] * (len(extras) + len(riders)),
+        out_specs=[in_vmem] + [anywhere] * len(riders),
+        scratch_shapes=[pltpu.VMEM((8, 2 * product_rows, left.shape[1]), low) for left in lefts]
+        + [
+            pltpu.VMEM((8, 2, rows, width), low),
+            pltpu.VMEM((15, rows, width), low),
             pltpu.SemaphoreType.DMA((15 * len(pieces),)),
-            pltpu.SemaphoreType.DMA((len(pieces), 4, 8)),
+            pltpu.SemaphoreType.DMA((len(pieces), 15)),
+            pltpu.SemaphoreType.DMA((len(lefts), 8)),
             pltpu.SemaphoreType.DMA((len(pieces), 8)),
-        ],
-        compiler_params=remote_params(collective),
+        ]
+        + ride.semaphores(),
+        compiler_params=remote_params(collective, held_bytes),
         name="block_scatter",
-    )(*partials)
-
-
-def swap_kernel(x_ref, out_ref, send_sem, recv_sem, local_sem):
-    greet(list(range(1, block_size)))
-    sent = []
-    here = slot_at(0)
-    for mask in (15, 14, 13, 11, 7, 12, 10, 6, 9, 5, 3, 8, 4, 2, 1):
-        copy = pltpu.make_async_remote_copy(
-            src_ref=x_ref.at[slot_at(mask)],
-            dst_ref=out_ref.at[here],
-            send_sem=send_sem.at[mask],
-            recv_sem=recv_sem.at[mask],
-            device_id=device_at(mask),
-            device_id_type=pl.DeviceIdType.MESH,
-        )
-        copy.start()
-        sent.append(copy)
-    own = pltpu.make_async_copy(x_ref.at[here], out_ref.at[here], local_sem)
-    own.start()
-    for mask in range(1, block_size):
-        target = out_ref.at[slot_at(mask)]
-        pltpu.make_async_copy(target, target, recv_sem.at[mask]).wait()
-    for copy in sent:
-        copy.wait_send()
-    own.wait()
-
-
-def block_swap(values, collective):
-    return pl.pallas_call(
-        swap_kernel,
-        out_shape=jax.ShapeDtypeStruct(values.shape, values.dtype),
-        in_specs=[in_vmem],
-        out_specs=in_vmem,
-        scratch_shapes=[
-            pltpu.SemaphoreType.DMA((block_size,)),
-            pltpu.SemaphoreType.DMA((block_size,)),
-            pltpu.SemaphoreType.DMA,
-        ],
-        compiler_params=remote_params(collective),
-        name="block_swap",
-    )(values)
+    )(*lefts, *rights, *extras, *ride.arrays)
+
+
+def group_shift(values, distance):
+    count = lax.axis_size("g")
+    return lax.ppermute(values, "g", [(i, (i + distance) % count) for i in range(count)])
 
 
 def group_gather(values):
@@ -301,8 +481,7 @@
     count = lax.axis_size("g")
     total = values
     for distance in range(1, count):
-        route = [(i, (i + distance) % count) for i in range(count)]
-        total = total + lax.ppermute(values.astype(low), "g", route).astype(wide)
+        total = total + group_shift(values.astype(low), distance).astype(wide)
     return total
 
 
@@ -367,7 +546,7 @@
             pltpu.SemaphoreType.DMA((count,)),
             pltpu.SemaphoreType.DMA,
         ],
-        compiler_params=remote_params(collective),
+        compiler_params=remote_params(collective, 2 * (count + 1) * 8 * bytes_of(values)),
         name="seq_spread",
     )(values)
 
@@ -561,9 +740,9 @@
     for j, grad in enumerate((grad_rgate, grad_igate)):
         grad_low = grad.astype(low)
         sums.append(jnp.sum(grad_low.astype(wide), 0, keepdims=True))
-        weight_grad_ref[j, 0] = lax.dot_general(
+        weight_grad_ref[j] = lax.dot_general(
             conv_low, grad_low, (((0,), (0,)), ((), ())), preferred_element_type=wide
-        )
+        ).astype(low)
         grad_conv = grad_conv + lax.dot_general(
             grad_low, weight_ref[j, 0], (((1,), (1,)), ((), ())), preferred_element_type=wide
         )
@@ -597,7 +776,7 @@
     sums_ref[...] = jnp.concatenate(sums + [jnp.zeros((6, grad_conv.shape[1]), wide)], 0)
 
 
-def by_heads(kernel, heads, width, operands, outs, name):
+def by_heads(kernel, heads, width, operands, outs):
     def spec(shape):
         if len(shape) == 1:
             return in_smem
@@ -613,8 +792,59 @@
         in_specs=[spec(value.shape) for value in operands],
         out_specs=[spec(shape) for shape, _ in outs],
         compiler_params=pltpu.CompilerParams(vmem_limit_bytes=48000000),
-        name=name,
     )(*operands)
+
+
+def joined_kernel(half, turned_ref, pre_ref, bias_ref, *out_refs):
+    members, _, both = pre_ref.shape
+    unit = both // (2 * half)
+    bias = bias_ref[...]
+    for k in range(half):
+        for member in range(members):
+            parts = [
+                pre_ref[member, :, (j * half + k) * unit : (j * half + k + 1) * unit].astype(wide)
+                for j in range(2)
+            ]
+            at = (k * members + member) * unit
+            for j in range(2):
+                value = jnp.where(turned_ref[0] == 1, parts[1 - j], parts[j])
+                out_refs[j][:, at : at + unit] = value + bias[j : j + 1, at : at + unit]
+
+
+def joined_columns(pre, bias, turned, half):
+    shape = jax.ShapeDtypeStruct((pre.shape[1], bias.shape[1]), wide)
+    return pl.pallas_call(
+        functools.partial(joined_kernel, half),
+        out_shape=[shape, shape],
+        in_specs=[in_smem, in_vmem, in_vmem],
+        out_specs=[in_vmem, in_vmem],
+        compiler_params=pltpu.CompilerParams(vmem_limit_bytes=16 << 20),
+        name="joined_columns",
+    )(jnp.asarray(turned, jnp.int32).reshape(1), pre, bias)
+
+
+def split_kernel(half, turned_ref, grads_ref, out_ref):
+    members, _, both = out_ref.shape
+    unit = both // (2 * half)
+    for k in range(half):
+        for member in range(members):
+            at = (k * members + member) * unit
+            parts = [grads_ref[j, :, at : at + unit] for j in range(2)]
+            for j in range(2):
+                value = jnp.where(turned_ref[0] == 1, parts[1 - j], parts[j])
+                out_ref[member, :, (j * half + k) * unit : (j * half + k + 1) * unit] = value
+
+
+def split_columns(grads, turned, half):
+    _, rows, width = grads.shape
+    return pl.pallas_call(
+        functools.partial(split_kernel, half),
+        out_shape=jax.ShapeDtypeStruct((block_size, rows, 2 * width // block_size), grads.dtype),
+        in_specs=[in_smem, in_vmem],
+        out_specs=in_vmem,
+        compiler_params=pltpu.CompilerParams(vmem_limit_bytes=16 << 20),
+        name="split_columns",
+    )(jnp.asarray(turned, jnp.int32).reshape(1), grads)
 
 
 def normed(values, scales):
@@ -650,6 +880,44 @@
     count = lax.axis_size("g")
     split = values.reshape(rows, count, block_size, width // (count * block_size))
     return split.transpose(2, 0, 1, 3).reshape(block_size, rows, width // block_size)
+
+
+def after(values, earlier):
+    return lax.optimization_barrier((values, earlier))[0]
+
+
+class Exchange:
+    def __init__(self, values):
+        self.values = values
+        self.share = 0
+        self.parts = []
+
+    def next(self, share):
+        tiles = self.values.shape[0] // 16
+        start = tiles * self.share // 16 * 16
+        self.share += share
+        return self.values, start, tiles * self.share // 16 * 16 - start
+
+    def shift(self, share, earlier):
+        values, start, size = self.next(share)
+        part = lax.slice_in_dim(values, start, start + size, axis=0)
+        part = after(part, earlier)
+        self.parts.append(group_shift(part, 1))
+
+    def whole(self):
+        return self.parts[0] if len(self.parts) == 1 else jnp.concatenate(self.parts, 0)
+
+
+def sharing(paired, plan):
+    if not paired:
+        return ()
+    return tuple(exchange.next(share) for exchange, share in plan)
+
+
+def arrived(paired, plan, parts):
+    if paired:
+        for (exchange, _), part in zip(plan, parts):
+            exchange.parts.append(part)
 
 
 def body(
@@ -674,6 +942,8 @@
     heads, head_width = gate_weight.shape[1:3]
     count = lax.axis_size("g")
     half = count // 2
+    paired = count == 2
+    turned = (lax.axis_index("g") == 1) if paired else False
     all_rows = block_size * rows
     position = (
         lax.axis_index("g") * 4 + lax.axis_index("b3") * 2 + lax.axis_index("b2")
@@ -681,10 +951,37 @@
     flat = (rows, width)
     small = (8, width)
 
-    branch_rows = group_gather(branch_weight).reshape(-1, width)
-    mlp_rows = group_gather(mlp_weight)
-    gate_rows = mlp_rows[:half].reshape(-1, width)
-    up_rows = mlp_rows[half:].reshape(-1, width)
+    def in_turn(first, second):
+        if not paired:
+            return first, second
+        return jnp.where(turned, second, first), jnp.where(turned, first, second)
+
+    def turn_halves(values):
+        if not paired:
+            return values
+        return jnp.where(turned, jnp.roll(values, width // 2, 1), values)
+
+    def move(gathered, swapped, collective, plan):
+        outs = block_move(gathered, swapped, collective, sharing(paired, plan))
+        own = (gathered is not None) + len(swapped)
+        arrived(paired, plan, outs[own:])
+        return outs[0] if own == 1 else outs[:own]
+
+    def scatter(products, collective, plan, extra=None):
+        out, *parts = block_scatter(products, collective, sharing(paired, plan), extra)
+        arrived(paired, plan, parts)
+        return out
+
+    def joined(values, exchange):
+        if paired:
+            return jnp.concatenate([values, exchange.whole()], 0)
+        return group_gather(values).reshape(-1, values.shape[1])
+
+    def total(own, exchange, sums):
+        if paired:
+            return own + exchange.whole().astype(wide)
+        return group_sum(sums)
+
     down_rows, hidden_width = down_weight.shape
     unit = hidden_width // (half * block_size)
     down_split = (
@@ -692,19 +989,27 @@
         .transpose(2, 0, 1, 3)
         .reshape(block_size, down_rows, half * unit)
     )
-    down_columns = group_gather(block_swap(down_split, 0)).reshape(width, half * unit)
+    mlp_trade = Exchange(mlp_weight)
+    branch_trade = Exchange(branch_weight)
     out_rows = lax.all_gather(out_weight, places, axis=0, tiled=True)
 
     first_in = normed(source, gain_first).astype(low)
-    first_all = block_gather(first_in, 1).reshape(all_rows, width)
+    first_all, down_own = move(
+        first_in, (down_split,), 1, [(branch_trade, 16)]
+    )
+    down_own = down_own.reshape(block_size * down_rows, half * unit)
+    down_trade = Exchange(down_own)
+    first_all = first_all.reshape(all_rows, width)
+    cot_in = after(turn_halves(cotangent[0]), first_all)
+    cot_all = lax.all_gather(cot_in, cube, axis=0, tiled=True)
     grad_out = cotangent[0]
-    cot_all = block_gather(grad_out, 12).reshape(all_rows, width)
+    branch_rows = joined(branch_weight, branch_trade)
     pre_part = times_rows(first_all, branch_rows).astype(low)
     pre_part = pre_part.reshape(block_size, rows, 2 * width // block_size)
-    pre = block_swap(pre_part, 2).reshape(block_size, rows, count, -1)
-    pre = pre.transpose(1, 2, 0, 3).reshape(rows, 2 * width).astype(wide) + branch_bias
-    gate_pre = pre[:, :width]
-    conv_in = pre[:, width:]
+    pre = move(None, (pre_part,), 2, [(mlp_trade, 7)])
+    if paired:
+        mlp_trade.shift(5, pre)
+    gate_pre, conv_in = joined_columns(pre, branch_bias.reshape(2, width), turned, half)
     conv_before = rim_rows(conv_in[rows - 8 :], 1)
 
     rate = (-8.0 * jax.nn.softplus(decay))[None]
@@ -723,55 +1028,57 @@
             rate,
         ),
         [(flat, wide)] * 6 + [((2, width), wide)],
-        "local_states",
-    )
+    )
+    all_ends = seq_spread(ends, 3)
+    if paired:
+        mlp_trade.shift(4, all_ends)
     states, mixed, entry = by_heads(
         full_states_kernel,
         heads,
         head_width,
-        (position, local, product, seq_spread(ends, 3), gate_pre),
+        (position, local, product, all_ends, gate_pre),
         [(flat, wide), (flat, low), (small, wide)],
-        "full_states",
-    )
-    mixed_all = lax.all_gather(mixed, cube, axis=0, tiled=True)
+    )
     middle = source + times_rows(mixed, out_rows) + out_bias
 
-    grad_hidden = times(cot_all, down_columns)
     second_in = normed(middle, gain_second).astype(low)
-    second_all = block_gather(second_in, 4).reshape(all_rows, width)
-    mlp_gate = times_rows(second_all, gate_rows)
-    mlp_up = times_rows(second_all, up_rows)
+    second_all = move(second_in, (), 4, [(down_trade, 12)])
+    if paired:
+        down_trade.shift(4, second_all)
+    second_all = second_all.reshape(all_rows, width)
+    if paired:
+        rows_a, rows_b = mlp_weight, mlp_trade.whole()
+    else:
+        mlp_rows = group_gather(mlp_weight)
+        rows_a = mlp_rows[:half].reshape(-1, width)
+        rows_b = mlp_rows[half:].reshape(-1, width)
+    down_columns = joined(down_own, down_trade)
+    pre_a = times_rows(second_all, rows_a)
+    mlp_gate, mlp_up = in_turn(pre_a, times_rows(second_all, rows_b))
     mlp_hidden, gated_back = jax.vjp(gated_unit, mlp_gate, mlp_up)
     mlp_hidden = mlp_hidden.astype(low)
-    grad_gate, grad_up = (grad.astype(low) for grad in gated_back(grad_hidden))
-    second_part = times(grad_gate, gate_rows) + times(grad_up, up_rows)
-    grad_second = block_scatter(5, second_part.astype(low).reshape(block_size, rows, width))
-    down_part = times_rows(mlp_hidden, down_columns).astype(low)
-    down_part = down_part.reshape(block_size, rows, width)
-
-    gate_sum = row_sums(grad_gate, second_all)
-    up_sum = row_sums(grad_up, second_all)
-    mlp_sum = jnp.concatenate([gate_sum.astype(low), up_sum.astype(low)], 0)
-    mlp_grad = group_sum(mlp_sum.reshape(count, -1, width))
-    gain_second_term = gain_sums(gate_sum, gate_rows) + gain_sums(up_sum, up_rows)
-    gain_second_term = gain_second_term / gain_second
+    grad_hidden = times(cot_all, down_columns)
+    grad_a, grad_b = in_turn(*(grad.astype(low) for grad in gated_back(grad_hidden)))
+    sum_b = row_sums(grad_b, second_all)
+    sum_b_low = sum_b.astype(low)
+    mlp_back = Exchange(sum_b_low)
+    grad_second = scatter(
+        [(grad_a, rows_a, False), (grad_b, rows_b, False)], 5, [(mlp_back, 8)]
+    )
     down_sum = row_sums(cot_all, mlp_hidden)
-    down_sum = group_sum(down_sum.reshape(count, block_size, down_rows, half * unit))
-    down_grad = (
-        block_swap(down_sum.astype(low), 7)
-        .reshape(block_size, down_rows, half, unit)
-        .transpose(1, 2, 0, 3)
-        .reshape(down_rows, hidden_width)
-        .astype(wide)
-    )
-
-    norm_second, second_back = jax.vjp(lambda values: normed(values, gain_second), middle)
+    down_sums = down_sum.astype(low).reshape(count, block_size * down_rows, half * unit)
+    down_back = Exchange(down_sums[1])
+    down_left = after(mlp_hidden, grad_second)
+    down_full = scatter([(down_left, down_columns, True)], 6, [(mlp_back, 8)])
+    output = (middle + turn_halves(down_full)).astype(low)[None]
+    if paired:
+        down_back.shift(5, down_full)
+
+    _, second_back = jax.vjp(lambda values: normed(values, gain_second), middle)
     grad_middle = grad_out.astype(wide) + second_back(grad_second)[0]
     grad_branch = grad_middle.astype(low)
     out_bias_term = jnp.sum(grad_branch.astype(wide), 0)
     grad_mixed = times(grad_branch, out_rows)
-    branch_all = block_swap(member_columns(grad_branch), 8).reshape(all_rows, -1)
-    out_grad = group_sum(row_sums(branch_all, mixed_all).reshape(count, -1, width))
 
     adjoint, tail, adjoint_ends = by_heads(
         local_adjoint_kernel,
@@ -779,8 +1086,11 @@
         head_width,
         (grad_mixed, gate_pre, decays),
         [(flat, wide), (flat, wide), ((2, width), wide)],
-        "local_adjoint",
-    )
+    )
+    all_adjoint_ends = seq_spread(adjoint_ends, 9)
+    mixed_all = lax.all_gather(after(mixed, all_adjoint_ends), cube, axis=0, tiled=True)
+    if paired:
+        down_back.shift(9, all_adjoint_ends)
     grad_conv, gate_weight_term, gate_sums = by_heads(
         gate_grads_kernel,
         heads,
@@ -789,7 +1099,7 @@
             position,
             adjoint,
             tail,
-            seq_spread(adjoint_ends, 9),
+            all_adjoint_ends,
             decays,
             rgate,
             igate,
@@ -801,8 +1111,7 @@
             gate_weight,
             rate,
         ),
-        [(flat, wide), (gate_weight.shape, wide), (small, wide)],
-        "gate_grads",
+        [(flat, wide), ((2, head_width, width), low), (small, wide)],
     )
     conv_after = rim_rows(grad_conv[:8], -1)
     pre_grads, pre_sums = by_heads(
@@ -811,31 +1120,30 @@
         head_width,
         (grad_conv, conv_after, conv_weight, gate_pre, grad_mixed, states),
         [((2, rows, width), low), (small, wide)],
-        "branch_grads",
-    )
-
-    columns = pre_grads.reshape(2, rows, half, block_size, -1).transpose(3, 1, 0, 2, 4)
-    pre_all = block_swap(columns.reshape(block_size, rows, -1), 10).reshape(all_rows, -1)
+    )
+
+    columns = split_columns(pre_grads, turned, half)
+    pre_all, branch_all = move(None, (columns, member_columns(grad_branch)), 10, [])
+    branch_all = branch_all.reshape(all_rows, -1)
+    sum_a = row_sums(grad_a, second_all)
+    mlp_low = jnp.concatenate([sum_a.astype(low), sum_b_low], 0).reshape(count, -1, width)
+    gain_second_term = gain_sums(sum_a, rows_a) + gain_sums(sum_b, rows_b)
+    out_sum = row_sums(branch_all, mixed_all).reshape(count, -1, width)
+    out_sums = out_sum.astype(low)
+    own_out, other_out = in_turn(out_sum[0], out_sum[1])
+    out_back = Exchange(other_out.astype(low))
+    if paired:
+        down_back.shift(2, pre_all)
+    pre_all = pre_all.reshape(all_rows, -1)
     branch_sum = row_sums(pre_all, first_all)
-    branch_grad = group_sum(branch_sum.reshape(count, -1, width))
-    gain_first_term = gain_sums(branch_sum, branch_rows) / gain_first
-    first_part = times(pre_all, branch_rows).astype(low)
-
-    vectors = jnp.concatenate(
-        [
-            gain_first_term[None],
-            pre_sums[:2],
-            gate_sums[4:8],
-            gate_sums[3:4],
-            gate_sums[:2],
-            gate_sums[2:3] * (-8.0 * jax.nn.sigmoid(decay)),
-            out_bias_term[None],
-            gain_second_term[None],
-            jnp.zeros((block_size - 13, width), wide),
-        ],
-        0,
-    ).astype(low)
-    gate_terms = gate_weight_term.reshape(block_size, -1, width).astype(low)
+    branch_sums = branch_sum.astype(low).reshape(count, -1, width)
+    branch_back = Exchange(branch_sums[1])
+    gain_first_term = gain_sums(branch_sum, branch_rows)
+
+    tops = jnp.stack([out_bias_term, gain_first_term, gain_second_term], 0)
+    vectors = jnp.concatenate([gate_sums, pre_sums[:2], tops, jnp.zeros((3, width), wide)], 0)
+    vectors = vectors.astype(low)
+    gate_terms = gate_weight_term.reshape(block_size, -1, width)
     gate_unit = gate_terms.shape[1]
     shared_part = jnp.concatenate(
         [
@@ -845,32 +1153,48 @@
         ],
         1,
     )
-    scattered = block_scatter(11, first_part.reshape(block_size, rows, width), shared_part)
+    scattered = scatter(
+        [(pre_all, branch_rows, False)], 11, [(branch_back, 10), (out_back, 16)], shared_part
+    )
     grad_first = scattered[:rows]
+    _, first_back = jax.vjp(lambda values: normed(values, gain_first), source)
+    input_grad = (grad_middle + first_back(grad_first)[0])[None]
     shared = group_total(scattered[rows:]).astype(low)
-    norm_first, first_back = jax.vjp(lambda values: normed(values, gain_first), source)
-    input_grad = (grad_middle + first_back(grad_first)[0])[None]
-
-    down_part, shared = lax.optimization_barrier((down_part, shared))
-    down_full = block_scatter(6, down_part)
-    output = (middle + down_full).astype(low)[None]
-    shared_all = block_gather(shared, 13).astype(wide)
-    gate_weight_grad = shared_all[:, :gate_unit].reshape(gate_weight.shape)
-    sums = shared_all[:, gate_unit]
+    mlp_grad = total(sum_a, mlp_back, mlp_low)
+
+    if paired:
+        down_total = down_sum[: block_size * down_rows] + down_back.whole().astype(wide)
+    else:
+        down_total = group_sum(down_sums)
+    down_total = down_total.astype(low).reshape(block_size, down_rows, half * unit)
+    shared_all, down_total = move(shared, (down_total,), 7, [(branch_back, 6)])
+    down_grad = (
+        down_total.reshape(block_size, down_rows, half, unit)
+        .transpose(1, 2, 0, 3)
+        .reshape(down_rows, hidden_width)
+        .astype(wide)
+    )
+    gate_sum = shared_all[:, :gate_unit].reshape(2, head_width, width)
+    gate_weight_grad = jnp.stack(
+        [gate_sum[:, :, h * head_width : (h + 1) * head_width] for h in range(heads)], 1
+    ).astype(wide)
+    sums = shared_all[:, gate_unit].astype(wide)
+    branch_grad = total(branch_sum[: branch_weight.shape[0]], branch_back, branch_sums)
+    out_grad = total(own_out, out_back, out_sums)
     return (
         output,
         input_grad,
-        sums[0],
+        sums[11] / gain_first,
         branch_grad,
-        sums[1:3].reshape(-1),
-        sums[3:7],
-        sums[7],
+        sums[8:10].reshape(-1),
+        sums[4:8],
+        sums[3],
         gate_weight_grad,
-        sums[8:10],
+        sums[:2],
+        sums[2] * (-8.0 * jax.nn.sigmoid(decay)),
+        out_grad,
         sums[10],
-        out_grad,
-        sums[11],
-        sums[12],
+        sums[12] / gain_second,
         mlp_grad,
         down_grad,
     )

time: 1060 us -> 861 us (0.81)
  Pallas kernels: 711 us -> 580 us
  matrix products: 147 us -> 102 us
  other arithmetic: 44.6 us -> 27.6 us
  starting transfers between devices: 4.9 us -> 16.6 us
    pallas_call x12 -> x10, Pallas kernels: 608 us -> 513 us  [the longest x5 289 us: block_move(): pl.pallas_call(functools.partial(move_kernel, pieces, len(swapped), ride)...]
    pallas_call x2, Pallas kernels: 73.1 us -> 36.9 us  [seq_spread(): pl.pallas_call(functools.partial(spread_kernel, group_count), out_shape=j...]
    dot_general x5 -> x2, matrix products: 53.5 us -> 23.1 us  [times(): return jnp.dot(operand, weight, preferred_element_type=wide)]
    convert_element_type x7 -> x3, local copies, waits for them, and re-layouts: 17.3 us -> 5.72 us  [the longest x2 4.13 us: body(): down_grad = down_total.reshape(block_size, down_rows, half, unit).transpo...]
    ppermute x1 -> x7, starting transfers between devices: 0.07 us -> 11.3 us  [group_shift(): lax.ppermute(values, 'g', [(i, (i + distance) % count) for i in range(cou...]
    dot_general x5 -> x4, matrix products: 44.7 us -> 33.8 us  [times_rows(): lax.dot_general(operand, weight, (((1,), (1,)), ((), ())), preferred_elem...]
    unnamed x161 -> x205, local copies, waits for them, and re-layouts: 34.4 us -> 39.5 us
    ppermute x1 -> x7, waiting for transfers between devices: 38.5 us -> 35.3 us  [group_shift(): lax.ppermute(values, 'g', [(i, (i + distance) % count) for i in range(cou...]
  transfers between devices with their start and end apart: 12 -> 12, of which waited for: 2 -> 3; matrix products, arithmetic and copies ran while one was open for 22% -> 13% of each run, Pallas kernels for 68% -> 47%
where the time goes in v2:
time: 861 us; the launch traced here: 852 us
  Pallas kernels  580 us (67%)
  matrix products  102 us (12%)
  local copies, waits for them, and re-layouts  74.7 us (9%)
  waiting for transfers between devices  36.1 us (4%)
  other arithmetic  27.6 us (3%)
  starting transfers between devices  16.6 us (2%)
  between operations  15.4 us (2%)
    pallas_call x5, Pallas kernels, block_move(): pl.pallas_call(functools.partial(move_kernel, pieces, len(swapped), ride)...  289 us
    pallas_call x3, Pallas kernels, block_scatter(): pl.pallas_call(functools.partial(scatter_kernel, pieces, product_rows, tr...  221 us
    dot_general x5, matrix products, row_sums(): lax.dot_general(gradient, operand, (((0,), (0,)), ((), ())), preferred_el...  45 us
    unnamed x205, local copies, waits for them, and re-layouts  39.5 us
    pallas_call x2, Pallas kernels, seq_spread(): pl.pallas_call(functools.partial(spread_kernel, group_count), out_shape=j...  36.9 us
    ppermute x7, waiting for transfers between devices, group_shift(): lax.ppermute(values, 'g', [(i, (i + distance) % count) for i in range(cou...  35.3 us
    dot_general x4, matrix products, times_rows(): lax.dot_general(operand, weight, (((1,), (1,)), ((), ())), preferred_elem...  33.8 us
    pallas_call x5, Pallas kernels, by_heads(): pl.pallas_call(kernel, grid=(heads,), out_shape=[jax.ShapeDtypeStruct(sha...  29.5 us
  transfers between devices with their start and end apart: 12, of which 3 were waited for; matrix products, arithmetic and copies ran while one was open for 13% of the time, Pallas kernels for 47%

profile of v2, /device:TPU:1, one launch (start us, length us, event | category | flops | bytes accessed | tf_op | source)
XLA Modules:
  0.0 852.2 jit_solution(2043228304188118096)
XLA Ops:
  8.0 4.1 reshape.259
  12.1 2.1 copy.85
  15.9 93.8 %block_move.5 = (bf16[16,128,2560]{2,1,0:T(8,128)(2,1)S(1)}, bf16[16,80,480]{2,1,0:T(8,128)(2,1)S(1)}, bf16[160,2560]{1,0:T(8,128)(2,1)S(1)}) custom-call(bf16[128,2560]{1,0:T(8,128)(2,1)S(1)} %fusion.14.refs_0_, bf16[16,80,480]{2,1,0:T(8,128)(2,1)S(1)} %bitcast.148, bf16[160,2560]{1,0:T(8,128)(2,1)S(1)} %copy-done.29), custom_call_target="tpu_custom_call" | custom-call | tf_op jit(solution)/shard_map/block_move/pallas_call | solution.py:239
  109.7 3.8 copy-done
  120.0 8.7 %convolution_convert_fusion = bf16[2048,320]{0,1:T(8,128)(2,1)} fusion(bf16[2048,2560]{1,0:T(8,128)(2,1)} %bitcast.141, bf16[320,2560]{1,0:T(8,128)(2,1)S(1)} %constant_dynamic-update-slice_fusion.refs_1_), kind=kOutput, calls=%fused_computation.20 | convolution fusion | flops 3356098560 | bytes 13434880 | tf_op jit(solution)/shard_map/dot_general | solution.py:859
  128.7 2.5 copy.50
  132.9 58.2 %block_move.6 = (bf16[16,128,320]{2,1,0:T(8,128)(2,1)S(1)}, bf16[208,2560]{1,0:T(8,128)(2,1)S(1)}) custom-call(bf16[16,128,320]{2,1,0:T(8,128)(2,1)S(1)} %bitcast.146, bf16[480,2560]{1,0:T(8,128)(2,1)S(1)} %copy-done.1), custom_call_target="tpu_custom_call" | custom-call | tf_op jit(solution)/shard_map/block_move/pallas_call | solution.py:239
  195.9 3.1 joined_columns.1
  201.8 3.6 collective-permute-start
  208.3 1.7 slice.154
  211.6 9.5 %shard_map.262 = (f32[128,2560]{1,0:T(8,128)S(1)}, f32[128,2560]{1,0:T(8,128)S(1)}, f32[128,2560]{1,0:T(8,128)S(1)}, f32[128,2560]{1,0:T(8,128)S(1)}, f32[128,25...) custom-call(s32[1]{0:T(128)} %bitcast.1.position_ref, f32[128,2560]{1,0:T(8,128)} %copy-done.20, ...), custom_call_target="tpu_custom_call" | custom-call | tf_op jit(solution)/shard_map/pallas_call | solution.py:788
  224.2 30.2 %seq_spread.2.ends_ref = f32[8,2,2560]{2,1,0:T(2,128)S(1)} custom-call(f32[2,2560]{1,0:T(2,128)S(1)} %get-tuple-element.69.x_ref), custom_call_target="tpu_custom_call" | custom-call | tf_op jit(solution)/shard_map/seq_spread/pallas_call | solution.py:539
  255.6 3.9 shard_map.263
  260.6 2.0 constant_dynamic-update-slice_fusion.3
  262.6 23.1 %collective-permute-done.2 = bf16[128,2560]{1,0:T(8,128)(2,1)S(1)} collective-permute-done((bf16[128,2560]{1,0:T(8,128)(2,1)S(1)}, bf16[128,2560]{1,0:T(8,128)(2,1)S(1)}, u32[]{:S(2)}, u32[]{:S(2)}) %collective-permute-start.2) | collective-permute-done | bytes 655392 | tf_op jit(solution)/shard_map/ppermute | solution.py:469
  286.6 9.3 %multiply_reduce_fusion.4 = (f32[128]{0:T(128)S(1)}, f32[128,2560]{1,0:T(8,128)S(1)}) fusion(f32[2560]{0:T(1024)S(1)} %copy-done.81, bf16[128,2560]{1,0:T(8,128)(2,1)} %get-tuple-element.99, bf16[2560,2560]{1,0:T(8,128)(2,1)} %all-gather.4.cloned.1.call-done, bf16[1,128,2560]{2,1,0:T(8,128)(2,1)S(1)} %copy-done.60), kind=kOutput, calls=%fused_computation.51 | convolution fusion | flops 1679359872 | bytes 15739392 | tf_op jit(solution)/shard_map/dot_general | solution.py:859
  297.8 50.6 %block_move.7 = (bf16[16,128,2560]{2,1,0:T(8,128)(2,1)S(1)}, bf16[960,480]{1,0:T(8,128)(2,1)S(1)}) custom-call(bf16[128,2560]{1,0:T(8,128)(2,1)S(1)} %multiply_convert_fusion.2.refs_0_, bf16[1280,480]{1,0:T(8,128)(2,1)S(1)} %bitcast.143), custom_call_target="tpu_custom_call" | custom-call | tf_op jit(solution)/shard_map/block_move/pallas_call | solution.py:239
  348.4 3.4 collective-permute-start.3
  351.8 7.2 fusion.43
  359.0 8.6 %fusion.42 = f32[2048,480]{1,0:T(8,128)} fusion(bf16[2048,2560]{1,0:T(8,128)(2,1)S(1)} %bitcast.151, bf16[480,2560]{1,0:T(8,128)(2,1)} %constant_dynamic-update-slice_fusion.2.refs_3_), kind=kOutput, calls=%fused_computation.117 | convolution fusion | flops 5033164800 | bytes 16875520 | tf_op jit(solution)/shard_map/dot_general | solution.py:859
  367.6 16.3 %broadcast_select_fusion = (bf16[2048,480]{1,0:T(8,128)(2,1)S(1)}, bf16[2048,480]{1,0:T(8,128)(2,1)S(1)}, bf16[2048,480]{1,0:T(8,128)(2,1)S(1)}, f32[2048,480]{1,0:T(8,128)}) fusion(pred[]{:T(512)S(6)} %eq.3, f32[2048,480]{1,0:T(8,128)} %fusion.43, f32[2048,480]{1,0:T(8,128)} %fusion.42, bf16[2048,2560]{1,0:T(8,128)(2,1)} %all-gather.6.cloned.1.call-done, ...), kind=kOutput, calls=%fused_computation.29 | convolution fusion | flops 5067079680 | bytes 30638080 | tf_op jit(solution)/shard_map/dot_general | solution.py:865
  383.9 12.0 %multiply_reduce_fusion = (f32[2560]{0:T(1024)}, bf16[480,2560]{1,0:T(8,128)(2,1)}) fusion(bf16[480,2560]{1,0:T(8,128)(2,1)} %constant_dynamic-update-slice_fusion.2.refs_3_, bf16[2048,480]{1,0:T(8,128)(2,1)S(1)} %get-tuple-element.118.refs_1_, bf16[2048,2560]{1,0:T(8,128)(2,1)} %bitcast.152), kind=kOutput, calls=%fused_computation.3 | convolution fusion | flops 5038077440 | bytes 17377280 | tf_op jit(solution)/shard_map/dot_general | solution.py:869
  396.1 68.3 %block_scatter.3 = (f32[128,2560]{1,0:T(8,128)S(1)}, bf16[240,2560]{1,0:T(8,128)(2,1)S(1)}) custom-call(bf16[2048,480]{1,0:T(8,128)(2,1)S(1)} %broadcast_select_fusion.1.refs_0_, bf16[2048,480]{1,0:T(8,128)(2,1)S(1)} %get-tuple-element.118.refs_1_, bf16[480,2560]{1,0:T(8,128)(2,1)} %refs_2_.3, bf16[480,2560]{1,0:T(8,128)(2,1)} %constant_dynamic-update-slice_fusion.2.refs_3_, ...), custom_call_target="tpu_custom_call" | custom-call | tf_op jit(solution)/shard_map/block_scatter/pallas_call | solution.py:443
  466.5 6.9 fusion.44.grad_mixed_ref
  473.4 2.7 shard_map.264
  478.3 6.7 seq_spread.3.ends_ref
  485.6 4.3 multiply_convert_fusion.1.refs_0_
  490.0 9.6 %fusion.41 = (bf16[2560,480]{0,1:T(8,128)(2,1)S(1)}, f32[2560,480]{0,1:T(8,128)}) fusion(bf16[2048,2560]{1,0:T(8,128)(2,1)} %all-gather.6.cloned.1.call-done, bf16[2048,480]{1,0:T(8,128)(2,1)S(1)} %multiply_convert_fusion.1.refs_0_), kind=kOutput, calls=%fused_computation.116 | convolution fusion | flops 5034393600 | bytes 19824640 | tf_op jit(solution)/shard_map/dot_general | solution.py:869
  504.3 86.1 %block_scatter.4 = (f32[128,2560]{1,0:T(8,128)S(1)}, bf16[240,2560]{1,0:T(8,128)(2,1)S(1)}) custom-call(bf16[2048,480]{1,0:T(8,128)(2,1)S(1)} %multiply_convert_fusion.1.refs_0_, bf16[2560,480]{1,0:T(8,128)(2,1)S(1)} %pad_maximum_fusion.refs_1_, bf16[480,2560]{1,0:T(8,128)(2,1)S(1)} %copy-done.10), custom_call_target="tpu_custom_call" | custom-call | tf_op jit(solution)/shard_map/block_scatter/pallas_call | solution.py:443
  590.5 4.5 collective-permute-start.6
  595.0 11.0 %shard_map.265 = (f32[128,2560]{1,0:T(8,128)S(1)}, bf16[2,256,2560]{2,1,0:T(8,128)(2,1)}, f32[8,2560]{1,0:T(8,128)S(1)}) custom-call(s32[1]{0:T(128)} %bitcast.1.position_ref, f32[128,2560]{1,0:T(8,128)S(1)} %copy-done.41, f32[128,2560]{1,0:T(8,128)S(1)} %copy-done.43, f32[8,2,2560]{2,1,0:T(2,128)S(1)} %seq_spread.3.ends_ref, f32[128,2560]{1,0:T(8,128)S(1)} %copy-done.27, ...), custom_call_target="tpu_custom_call" | custom-call | tf_op jit(solution)/shard_map/pallas_call | solution.py:788
  611.1 10.2 %convert_add_fusion = (f32[480,2560]{1,0:T(8,128)}, f32[2560]{0:T(1024)S(1)}) fusion(bf16[240,2560]{1,0:T(8,128)(2,1)S(1)} %get-tuple-element.109, bf16[240,2560]{1,0:T(8,128)(2,1)S(1)} %copy-done.55, bf16[480,2560]{1,0:T(8,128)(2,1)S(1)} %copy-done.2, bf16[2048,480]{1,0:T(8,128)(2,1)S(1)} %copy-done.14, bf16[2048,2560]{1,0:T(8,128)(2,1)} %bitcast.153), kind=kOutput, calls=%fused_computation.2 | convolution fusion | flops 5042992640 | bytes 22292480 | tf_op jit(solution)/shard_map/dot_general | solution.py:869
  621.3 1.8 slice.201
  630.6 2.3 shard_map.266
  634.1 48.3 %block_move.8 = (bf16[16,128,320]{2,1,0:T(8,128)(2,1)S(1)}, bf16[16,128,160]{2,1,0:T(8,128)(2,1)S(1)}) custom-call(bf16[16,128,320]{2,1,0:T(8,128)(2,1)S(1)} %split_columns.1.refs_0_, bf16[16,128,160]{2,1,0:T(8,128)(2,1)S(1)} %copy-done.28), custom_call_target="tpu_custom_call" | custom-call | tf_op jit(solution)/shard_map/block_move/pallas_call | solution.py:239
  683.6 6.9 multiply_reduce_fusion.2
  690.7 2.9 maximum_maximum_fusion.refs_2_
  693.7 2.8 collective-permute-done.8
  697.2 2.7 concatenate.62
  699.9 3.0 fusion.8
  704.5 6.3 fusion.45
  711.0 66.2 %block_scatter.5 = (f32[176,2560]{1,0:T(8,128)S(1)}, bf16[96,2560]{1,0:T(8,128)(2,1)S(1)}, bf16[80,2560]{1,0:T(8,128)(2,1)S(1)}) custom-call(bf16[2048,320]{1,0:T(8,128)(2,1)S(1)} %bitcast.142, bf16[320,2560]{1,0:T(8,128)(2,1)S(1)} %copy-done.9, bf16[16,48,2560]{2,1,0:T(8,128)(2,1)} %maximum_maximum_fusion.refs_2_, ...), custom_call_target="tpu_custom_call" | custom-call | tf_op jit(solution)/shard_map/block_scatter/pallas_call | solution.py:443
  778.9 2.3 fusion.11
  782.1 9.4 %collective-permute-done.5 = bf16[48,2560]{1,0:T(8,128)(2,1)S(1)} collective-permute-done((bf16[48,2560]{1,0:T(8,128)(2,1)S(1)}, bf16[48,2560]{1,0:T(8,128)(2,1)S(1)}, u32[]{:S(2)}, u32[]{:S(2)}) %collective-permute-start.5) | collective-permute-done | bytes 245792 | tf_op jit(solution)/shard_map/ppermute | solution.py:469
  791.5 38.4 %block_move.9 = (bf16[16,48,2560]{2,1,0:T(8,128)(2,1)S(1)}, bf16[16,80,480]{2,1,0:T(8,128)(2,1)S(1)}, bf16[64,2560]{1,0:T(8,128)(2,1)S(1)}) custom-call(bf16[48,2560]{1,0:T(8,128)(2,1)S(1)} %add_convert_fusion.refs_0_, bf16[16,80,480]{2,1,0:T(8,128)(2,1)S(1)} %bitcast.147, bf16[160,2560]{1,0:T(8,128)(2,1)S(1)} %slice.276.refs_3_.refs_2_), custom_call_target="tpu_custom_call" | custom-call | tf_op jit(solution)/shard_map/block_move/pallas_call | solution.py:239
  835.0 3.0 convert_element_type.136
  839.8 2.6 reshape.277
  842.4 2.8 slice_add_fusion.1
  (278 shorter events, 67.0 us)
Async XLA Ops:
  7.2 279.4 %all-gather.4.cloned.1.call-start = ((), (), s32[]{:S(2)}) async-start(), calls=%async_computation | async-start | bytes 13516800 | tf_op jit(solution)/shard_map/all_gather | solution.py:994
  7.9 359.7 %all-gather.6.cloned.1.call-start = ((), (), s32[]{:S(2)}) async-start(), calls=%async_computation.1 | async-start | bytes 11141120 | tf_op jit(solution)/shard_map/all_gather | solution.py:1004
  14.2 101.2 %copy-start.62 = (bf16[1,128,2560]{2,1,0:T(8,128)(2,1)S(1)}, bf16[1,128,2560]{2,1,0:T(8,128)(2,1)}, u32[]{:S(2)}) copy-start(bf16[1,128,2560]{2,1,0:T(8,128)(2,1)} %param.29) | copy-start | bytes 1966084
  116.5 587.9 %all-gather.8.cloned.1.call-start = ((), (), s32[]{:S(2)}) async-start(), calls=%async_computation.2 | async-start | bytes 11141120 | tf_op jit(solution)/shard_map/all_gather | solution.py:1091
  132.8 72.5 %copy-start.79 = (f32[2560]{0:T(1024)S(1)}, f32[2560]{0:T(1024)}, u32[]{:S(2)}) copy-start(f32[2560]{0:T(1024)} %param.23) | copy-start | bytes 30724
  192.2 68.3 %collective-permute-start.1 = (bf16[144,2560]{1,0:T(8,128)(2,1)}, bf16[144,2560]{1,0:T(8,128)(2,1)}, u32[]{:S(2)}, u32[]{:S(2)}) collective-permute-start(bf16[144,2560]{1,0:T(8,128)(2,1)} %slice.150), channel_id=1, source_target_pairs={{0,16},{16,0},{1,17},{17,1},{2,18},{18,2},{3,19},{19,3},{4,20},{20... | collective-permute-start | bytes 2211848 | tf_op jit(solution)/shard_map/ppermute | solution.py:469
  201.8 8.3 collective-permute-start
  211.5 42.9 %copy-start.72 = (bf16[128,2560]{1,0:T(8,128)(2,1)S(1)}, bf16[128,2560]{1,0:T(8,128)(2,1)}, u32[]{:S(2)}) copy-start(bf16[128,2560]{1,0:T(8,128)(2,1)} %slice.151) | copy-start | bytes 1966084
  211.6 44.0 %copy-start.4 = (f32[128,2560]{1,0:T(8,128)S(1)}, f32[128,2560]{1,0:T(8,128)}, u32[]{:S(2)}) copy-start(f32[128,2560]{1,0:T(8,128)} %copy-done.3) | copy-start | bytes 3932164
  224.2 31.3 %copy-start.25 = (f32[128,2560]{1,0:T(8,128)}, f32[128,2560]{1,0:T(8,128)S(1)}, u32[]{:S(2)}) copy-start(f32[128,2560]{1,0:T(8,128)S(1)} %get-tuple-element.83.decay_ref) | copy-start | bytes 3932164
  254.5 31.3 %collective-permute-start.2 = (bf16[128,2560]{1,0:T(8,128)(2,1)S(1)}, bf16[128,2560]{1,0:T(8,128)(2,1)S(1)}, u32[]{:S(2)}, u32[]{:S(2)}) collective-permute-start(bf16[128,2560]{1,0:T(8,128)(2,1)S(1)} %copy-done.72), channel_id=1, source_target_pairs={{0,16},{16,0},{1,17},{17,1},{2,18},{18,2},{3,19},{19,3},{4,20},{20... | collective-permute-start | bytes 1966088 | tf_op jit(solution)/shard_map/ppermute | solution.py:469
  255.6 31.0 %copy-start.60 = (bf16[1,128,2560]{2,1,0:T(8,128)(2,1)S(1)}, bf16[1,128,2560]{2,1,0:T(8,128)(2,1)}, u32[]{:S(2)}) copy-start(bf16[1,128,2560]{2,1,0:T(8,128)(2,1)} %param.15) | copy-start | bytes 1966084
  255.6 31.0 %copy-start.81 = (f32[2560]{0:T(1024)S(1)}, f32[2560]{0:T(1024)}, u32[]{:S(2)}) copy-start(f32[2560]{0:T(1024)} %param.25) | copy-start | bytes 30724
  286.6 9.4 %copy-start.74 = (f32[2560]{0:T(1024)S(1)}, f32[2560]{0:T(1024)}, u32[]{:S(2)}) copy-start(f32[2560]{0:T(1024)} %param.26) | copy-start | bytes 30724
  296.0 63.0 %copy-start.56 = (f32[128,2560]{1,0:T(8,128)}, f32[128,2560]{1,0:T(8,128)S(1)}, u32[]{:S(2)}) copy-start(f32[128,2560]{1,0:T(8,128)S(1)} %get-tuple-element.135) | copy-start | bytes 3932164
  348.4 10.6 %copy-start.53 = (bf16[16,128,2560]{2,1,0:T(8,128)(2,1)}, bf16[16,128,2560]{2,1,0:T(8,128)(2,1)S(1)}, u32[]{:S(2)}) copy-start(bf16[16,128,2560]{2,1,0:T(8,128)(2,1)S(1)} %get-tuple-element.73) | copy-start | bytes 31457284
  348.4 19.2 %copy-start.44 = (bf16[960,480]{1,0:T(8,128)(2,1)}, bf16[960,480]{1,0:T(8,128)(2,1)S(1)}, u32[]{:S(2)}) copy-start(bf16[960,480]{1,0:T(8,128)(2,1)S(1)} %get-tuple-element.78) | copy-start | bytes 2764804
  348.4 19.2 %collective-permute-start.3 = (bf16[320,480]{1,0:T(8,128)(2,1)}, bf16[320,480]{1,0:T(8,128)(2,1)}, u32[]{:S(2)}, u32[]{:S(2)}) collective-permute-start(bf16[320,480]{1,0:T(8,128)(2,1)} %bitcast.11), channel_id=1, source_target_pairs={{0,16},{16,0},{1,17},{17,1},{2,18},{18,2},{3,19},{19,3},{4,20},{20... | collective-permute-start | bytes 921608 | tf_op jit(solution)/shard_map/ppermute | solution.py:469
  396.1 68.3 %copy-start.13 = (bf16[2048,480]{1,0:T(8,128)(2,1)}, bf16[2048,480]{1,0:T(8,128)(2,1)S(1)}, u32[]{:S(2)}) copy-start(bf16[2048,480]{1,0:T(8,128)(2,1)S(1)} %broadcast_select_fusion.1.refs_0_) | copy-start | bytes 5898244
  396.1 68.4 %copy-start.57 = (f32[128,2560]{1,0:T(8,128)S(1)}, f32[128,2560]{1,0:T(8,128)}, u32[]{:S(2)}) copy-start(f32[128,2560]{1,0:T(8,128)} %copy-done.56) | copy-start | bytes 3932164
  504.3 90.6 %copy-start.27 = (f32[128,2560]{1,0:T(8,128)S(1)}, f32[128,2560]{1,0:T(8,128)}, u32[]{:S(2)}) copy-start(f32[128,2560]{1,0:T(8,128)} %copy-done.25) | copy-start | bytes 3932164
  504.3 90.7 %copy-start.37 = (f32[128,2560]{1,0:T(8,128)S(1)}, f32[128,2560]{1,0:T(8,128)}, u32[]{:S(2)}) copy-start(f32[128,2560]{1,0:T(8,128)} %copy-done.36) | copy-start | bytes 3932164
  504.3 90.7 %copy-start.39 = (f32[128,2560]{1,0:T(8,128)S(1)}, f32[128,2560]{1,0:T(8,128)}, u32[]{:S(2)}) copy-start(f32[128,2560]{1,0:T(8,128)} %copy-done.38) | copy-start | bytes 3932164
  504.3 90.7 %copy-start.41 = (f32[128,2560]{1,0:T(8,128)S(1)}, f32[128,2560]{1,0:T(8,128)}, u32[]{:S(2)}) copy-start(f32[128,2560]{1,0:T(8,128)} %copy-done.40) | copy-start | bytes 3932164
  504.3 90.7 %copy-start.43 = (f32[128,2560]{1,0:T(8,128)S(1)}, f32[128,2560]{1,0:T(8,128)}, u32[]{:S(2)}) copy-start(f32[128,2560]{1,0:T(8,128)} %copy-done.42) | copy-start | bytes 3932164
  590.5 18.7 %copy-start.21 = (f32[128,2560]{1,0:T(8,128)}, f32[128,2560]{1,0:T(8,128)S(1)}, u32[]{:S(2)}) copy-start(f32[128,2560]{1,0:T(8,128)S(1)} %get-tuple-element.82) | copy-start | bytes 3932164
  590.5 106.0 %collective-permute-start.6 = (bf16[400,480]{0,1:T(8,128)(2,1)}, bf16[400,480]{0,1:T(8,128)(2,1)}, u32[]{:S(2)}, u32[]{:S(2)}) collective-permute-start(bf16[400,480]{0,1:T(8,128)(2,1)} %slice.199), channel_id=1, source_target_pairs={{0,16},{16,0},{1,17},{17,1},{2,18},{18,2},{3,19},{19,3},{4,20},{20... | collective-permute-start | bytes 1152008 | tf_op jit(solution)/shard_map/ppermute | solution.py:469
  595.0 16.1 %copy-start.14 = (bf16[2048,480]{1,0:T(8,128)(2,1)S(1)}, bf16[2048,480]{1,0:T(8,128)(2,1)}, u32[]{:S(2)}) copy-start(bf16[2048,480]{1,0:T(8,128)(2,1)} %copy-done.13) | copy-start | bytes 5898244
  595.0 16.1 %copy-start.55 = (bf16[240,2560]{1,0:T(8,128)(2,1)S(1)}, bf16[240,2560]{1,0:T(8,128)(2,1)}, u32[]{:S(2)}) copy-start(bf16[240,2560]{1,0:T(8,128)(2,1)} %copy-done.54) | copy-start | bytes 3686404
  606.0 15.3 %copy-start.33 = (f32[128,2560]{1,0:T(8,128)}, f32[128,2560]{1,0:T(8,128)S(1)}, u32[]{:S(2)}) copy-start(f32[128,2560]{1,0:T(8,128)S(1)} %get-tuple-element.92.grad_conv_ref) | copy-start | bytes 3932164
  606.0 20.6 %collective-permute-start.4 = (f32[8,2560]{1,0:T(8,128)S(1)}, f32[8,2560]{1,0:T(8,128)S(1)}, u32[]{:S(2)}, u32[]{:S(2)}) collective-permute-start(f32[8,2560]{1,0:T(8,128)S(1)} %slice.158), channel_id=1, source_target_pairs={{4,0},{8,4},{12,8},{16,12},{20,16},{24,20},{28,24},{5,1},{9,5},{13... | collective-permute-start | bytes 245768 | tf_op jit(solution)/shard_map/ppermute | solution.py:557
  607.6 89.6 %collective-permute-start.7 = (bf16[720,480]{0,1:T(8,128)(2,1)}, bf16[720,480]{0,1:T(8,128)(2,1)}, u32[]{:S(2)}, u32[]{:S(2)}) collective-permute-start(bf16[720,480]{0,1:T(8,128)(2,1)} %slice.200), channel_id=1, source_target_pairs={{0,16},{16,0},{1,17},{17,1},{2,18},{18,2},{3,19},{19,3},{4,20},{20... | collective-permute-start | bytes 2073608 | tf_op jit(solution)/shard_map/ppermute | solution.py:469
  611.1 10.2 %copy-start.82 = (f32[2560]{0:T(1024)S(1)}, f32[2560]{0:T(1024)}, u32[]{:S(2)}) copy-start(f32[2560]{0:T(1024)} %get-tuple-element.124) | copy-start | bytes 30724
  611.1 12.0 %copy-start.67 = (bf16[128,2560]{1,0:T(8,128)(2,1)S(1)}, bf16[128,2560]{1,0:T(8,128)(2,1)}, u32[]{:S(2)}) copy-start(bf16[128,2560]{1,0:T(8,128)(2,1)} %copy-done.66) | copy-start | bytes 1966084
  632.9 50.6 %copy-start.75 = (bf16[160,480]{0,1:T(8,128)(2,1)S(1)}, bf16[160,480]{0,1:T(8,128)(2,1)}, u32[]{:S(2)}) copy-start(bf16[160,480]{0,1:T(8,128)(2,1)} %slice.201) | copy-start | bytes 460804
  632.9 50.6 %copy-start.73 = (bf16[16,1,2560]{2,1,0:T(2,128)(2,1)S(1)}, bf16[16,1,2560]{2,1,0:T(2,128)(2,1)}, u32[]{:S(2)}) copy-start(bf16[16,1,2560]{2,1,0:T(2,128)(2,1)} %copy_dynamic-update-slice_fusion) | copy-start | bytes 245764
  632.9 50.7 %copy-start.8 = (bf16[320,2560]{1,0:T(8,128)(2,1)S(1)}, bf16[320,2560]{1,0:T(8,128)(2,1)}, u32[]{:S(2)}) copy-start(bf16[320,2560]{1,0:T(8,128)(2,1)} %copy-done.7) | copy-start | bytes 4915204
  683.5 13.0 %collective-permute-start.8 = (bf16[160,480]{0,1:T(8,128)(2,1)S(1)}, bf16[160,480]{0,1:T(8,128)(2,1)S(1)}, u32[]{:S(2)}, u32[]{:S(2)}) collective-permute-start(bf16[160,480]{0,1:T(8,128)(2,1)S(1)} %copy-done.75), channel_id=1, source_target_pairs={{0,16},{16,0},{1,17},{17,1},{2,18},{18,2},{3,19},{19,3},{4,20},{20... | collective-permute-start | bytes 460808 | tf_op jit(solution)/shard_map/ppermute | solution.py:469
  710.9 66.3 %copy-start.61 = (bf16[1,128,2560]{2,1,0:T(8,128)(2,1)S(1)}, bf16[1,128,2560]{2,1,0:T(8,128)(2,1)}, u32[]{:S(2)}) copy-start(bf16[1,128,2560]{2,1,0:T(8,128)(2,1)} %param.15) | copy-start | bytes 1966084
  710.9 66.3 %copy-start.78 = (f32[2560]{0:T(1024)S(1)}, f32[2560]{0:T(1024)}, u32[]{:S(2)}) copy-start(f32[2560]{0:T(1024)} %param.16) | copy-start | bytes 30724
  710.9 66.6 %copy-start.91 = (f32[128]{0:T(128)S(1)}, f32[128]{0:T(128)}, u32[]{:S(2)}) copy-start(f32[128]{0:T(128)} %copy-done.90) | copy-start | bytes 1540
  711.0 66.9 %copy-start.58 = (f32[128,2560]{1,0:T(8,128)S(1)}, f32[128,2560]{1,0:T(8,128)}, u32[]{:S(2)}) copy-start(f32[128,2560]{1,0:T(8,128)} %copy-done.56) | copy-start | bytes 3932164
  711.0 66.9 %copy-start.68 = (f32[128,1280]{1,0:T(8,128)S(1)}, f32[128,1280]{1,0:T(8,128)}, u32[]{:S(2)}) copy-start(f32[128,1280]{1,0:T(8,128)} %get-tuple-element.128) | copy-start | bytes 1966084
  711.0 66.9 %copy-start.69 = (f32[128,1280]{1,0:T(8,128)S(1)}, f32[128,1280]{1,0:T(8,128)}, u32[]{:S(2)}) copy-start(f32[128,1280]{1,0:T(8,128)} %get-tuple-element.129) | copy-start | bytes 1966084
  711.0 66.9 %copy-start.85 = (f32[128]{0:T(128)S(1)}, f32[128]{0:T(128)}, u32[]{:S(2)}) copy-start(f32[128]{0:T(128)} %copy-done.83) | copy-start | bytes 1540
  711.0 66.9 %copy-start.87 = (f32[128]{0:T(128)S(1)}, f32[128]{0:T(128)}, u32[]{:S(2)}) copy-start(f32[128]{0:T(128)} %copy-done.86) | copy-start | bytes 1540
  711.0 66.9 %copy-start.89 = (f32[128]{0:T(128)S(1)}, f32[128]{0:T(128)}, u32[]{:S(2)}) copy-start(f32[128]{0:T(128)} %copy-done.88) | copy-start | bytes 1540
  777.6 13.9 %collective-permute-start.5 = (bf16[48,2560]{1,0:T(8,128)(2,1)S(1)}, bf16[48,2560]{1,0:T(8,128)(2,1)S(1)}, u32[]{:S(2)}, u32[]{:S(2)}) collective-permute-start(bf16[48,2560]{1,0:T(8,128)(2,1)S(1)} %slice.277), channel_id=1, source_target_pairs={{0,16},{16,0},{1,17},{17,1},{2,18},{18,2},{3,19},{19,3},{4,20},{20... | collective-permute-start | bytes 737288 | tf_op jit(solution)/shard_map/ppermute | solution.py:469
  (57 other events, 164.6 us)
Sparse Core Ops, SparseCore 0:
  10.8 159.3 all-gather.3
  171.8 81.6 all-gather.5
  485.2 108.0 all-gather.7

commit v3 on v2

--- a/solution.py
+++ b/solution.py
@@ -614,23 +614,7 @@
     return (lax.broadcasted_iota(jnp.int32, shape, 0) == 0) & (position == 0)
 
 
-def local_states_kernel(
-    position_ref,
-    conv_in_ref,
-    before_ref,
-    taps_ref,
-    bias_ref,
-    weight_ref,
-    gate_bias_ref,
-    rate_ref,
-    conv_out_ref,
-    rgate_ref,
-    igate_ref,
-    decay_ref,
-    local_ref,
-    product_ref,
-    ends_ref,
-):
+def conv_and_gates(conv_in_ref, before_ref, taps_ref, bias_ref, weight_ref, gate_bias_ref):
     ext = jnp.concatenate([before_ref[...], conv_in_ref[...]], 0)
     conv_out = lagged_sum(ext, taps_ref[...], bias_ref[...])
     conv_low = conv_out.astype(low)
@@ -641,15 +625,32 @@
         )
         for j in range(2)
     ]
+    return ext, conv_out, conv_low, gates
+
+
+def local_states_kernel(
+    position_ref,
+    conv_in_ref,
+    before_ref,
+    taps_ref,
+    bias_ref,
+    weight_ref,
+    gate_bias_ref,
+    rate_ref,
+    decay_ref,
+    local_ref,
+    product_ref,
+    ends_ref,
+):
+    _, conv_out, _, gates = conv_and_gates(
+        conv_in_ref, before_ref, taps_ref, bias_ref, weight_ref, gate_bias_ref
+    )
     log_rate = rate_ref[...] * gates[0]
     rates = jnp.exp(log_rate)
     scaling = jnp.where(
         opening_rows(rates.shape, position_ref[0]), 1.0, jnp.sqrt(one_minus_square(log_rate))
     )
     product, states = scan_rows(rates, scaling * gates[1] * conv_out, shifted)
-    conv_out_ref[...] = conv_out
-    rgate_ref[...] = gates[0]
-    igate_ref[...] = gates[1]
     decay_ref[...] = rates
     local_ref[...] = states
     product_ref[...] = product
@@ -699,14 +700,14 @@
     product_ref,
     ends_ref,
     decay_ref,
-    rgate_ref,
-    igate_ref,
-    conv_out_ref,
     states_ref,
     entry_ref,
     conv_in_ref,
     before_ref,
+    taps_ref,
+    bias_ref,
     weight_ref,
+    gate_bias_ref,
     rate_ref,
     grad_conv_ref,
     weight_grad_ref,
@@ -719,9 +720,9 @@
         entry = jnp.where(s > position, earlier, entry)
     adjoint = local_ref[...] + product_ref[...] * entry
     rates = decay_ref[...]
-    rgate = rgate_ref[...]
-    igate = igate_ref[...]
-    conv_out = conv_out_ref[...]
+    ext, conv_out, conv_low, (rgate, igate) = conv_and_gates(
+        conv_in_ref, before_ref, taps_ref, bias_ref, weight_ref, gate_bias_ref
+    )
     row = lax.broadcasted_iota(jnp.int32, rates.shape, 0)
     before = jnp.where(row == 0, entry_ref[0:1, :], pltpu.roll(states_ref[...], 1, 0))
     opening = opening_rows(rates.shape, position)
@@ -735,7 +736,6 @@
     grad_rgate = grad_log * rate_ref[...] * rgate * (1.0 - rgate)
     grad_igate = adjoint * scaling * conv_out * igate * (1.0 - igate)
     grad_conv = adjoint * scaling * igate
-    conv_low = conv_out.astype(low)
     sums = []
     for j, grad in enumerate((grad_rgate, grad_igate)):
         grad_low = grad.astype(low)
@@ -749,7 +749,6 @@
     grad_conv_ref[...] = grad_conv
     sums.append(jnp.sum(grad_log * rgate, 0, keepdims=True))
     sums.append(jnp.sum(grad_conv, 0, keepdims=True))
-    ext = jnp.concatenate([before_ref[...], conv_in_ref[...]], 0)
     for lag in range(4):
         moved = pltpu.roll(ext, lag, 0) if lag else ext
         sums.append(jnp.sum(grad_conv * moved[8:, :], 0, keepdims=True))
@@ -791,7 +790,7 @@
         out_shape=[jax.ShapeDtypeStruct(shape, dtype) for shape, dtype in outs],
         in_specs=[spec(value.shape) for value in operands],
         out_specs=[spec(shape) for shape, _ in outs],
-        compiler_params=pltpu.CompilerParams(vmem_limit_bytes=48000000),
+        compiler_params=pltpu.CompilerParams(vmem_limit_bytes=12 << 20),
     )(*operands)
 
 
@@ -821,6 +820,49 @@
         compiler_params=pltpu.CompilerParams(vmem_limit_bytes=16 << 20),
         name="joined_columns",
     )(jnp.asarray(turned, jnp.int32).reshape(1), pre, bias)
+
+
+def down_split_kernel(half, rows_ref, out_ref):
+    members, _, own = out_ref.shape
+    unit = own // half
+    for k in range(half):
+        for member in range(members):
+            at = (k * members + member) * unit
+            out_ref[member, :, k * unit : (k + 1) * unit] = rows_ref[:, at : at + unit]
+
+
+def down_split_units(rows, half):
+    count, width = rows.shape
+    return pl.pallas_call(
+        functools.partial(down_split_kernel, half),
+        out_shape=jax.ShapeDtypeStruct((block_size, count, width // block_size), rows.dtype),
+        in_specs=[in_vmem],
+        out_specs=in_vmem,
+        compiler_params=pltpu.CompilerParams(vmem_limit_bytes=12 << 20),
+        name="down_split",
+    )(rows)
+
+
+def down_join_kernel(half, parts_ref, out_ref):
+    members, _, own = parts_ref.shape
+    unit = own // half
+    for k in range(half):
+        for member in range(members):
+            at = (k * members + member) * unit
+            part = parts_ref[member, :, k * unit : (k + 1) * unit]
+            out_ref[:, at : at + unit] = part.astype(wide)
+
+
+def down_join_units(parts, half):
+    members, count, own = parts.shape
+    return pl.pallas_call(
+        functools.partial(down_join_kernel, half),
+        out_shape=jax.ShapeDtypeStruct((count, members * own), wide),
+        in_specs=[in_vmem],
+        out_specs=in_vmem,
+        compiler_params=pltpu.CompilerParams(vmem_limit_bytes=12 << 20),
+        name="down_join",
+    )(parts)
 
 
 def split_kernel(half, turned_ref, grads_ref, out_ref):
@@ -984,18 +1026,14 @@
 
     down_rows, hidden_width = down_weight.shape
     unit = hidden_width // (half * block_size)
-    down_split = (
-        down_weight.reshape(down_rows, half, block_size, unit)
-        .transpose(2, 0, 1, 3)
-        .reshape(block_size, down_rows, half * unit)
-    )
+    down_split = down_split_units(down_weight, half)
     mlp_trade = Exchange(mlp_weight)
     branch_trade = Exchange(branch_weight)
     out_rows = lax.all_gather(out_weight, places, axis=0, tiled=True)
 
     first_in = normed(source, gain_first).astype(low)
     first_all, down_own = move(
-        first_in, (down_split,), 1, [(branch_trade, 16)]
+        first_in, (down_split,), 1, [(branch_trade, 16), (mlp_trade, 2)]
     )
     down_own = down_own.reshape(block_size * down_rows, half * unit)
     down_trade = Exchange(down_own)
@@ -1008,12 +1046,12 @@
     pre_part = pre_part.reshape(block_size, rows, 2 * width // block_size)
     pre = move(None, (pre_part,), 2, [(mlp_trade, 7)])
     if paired:
-        mlp_trade.shift(5, pre)
+        mlp_trade.shift(3, pre)
     gate_pre, conv_in = joined_columns(pre, branch_bias.reshape(2, width), turned, half)
     conv_before = rim_rows(conv_in[rows - 8 :], 1)
 
     rate = (-8.0 * jax.nn.softplus(decay))[None]
-    conv_out, rgate, igate, decays, local, product, ends = by_heads(
+    decays, local, product, ends = by_heads(
         local_states_kernel,
         heads,
         head_width,
@@ -1027,7 +1065,7 @@
             gate_bias,
             rate,
         ),
-        [(flat, wide)] * 6 + [((2, width), wide)],
+        [(flat, wide)] * 3 + [((2, width), wide)],
     )
     all_ends = seq_spread(ends, 3)
     if paired:
@@ -1074,8 +1112,9 @@
     if paired:
         down_back.shift(5, down_full)
 
-    _, second_back = jax.vjp(lambda values: normed(values, gain_second), middle)
-    grad_middle = grad_out.astype(wide) + second_back(grad_second)[0]
+    _, second_back = jax.vjp(normed, middle, gain_second)
+    grad_mid_norm, gain_second_term = second_back(grad_second)
+    grad_middle = grad_out.astype(wide) + grad_mid_norm
     grad_branch = grad_middle.astype(low)
     out_bias_term = jnp.sum(grad_branch.astype(wide), 0)
     grad_mixed = times(grad_branch, out_rows)
@@ -1088,7 +1127,7 @@
         [(flat, wide), (flat, wide), ((2, width), wide)],
     )
     all_adjoint_ends = seq_spread(adjoint_ends, 9)
-    mixed_all = lax.all_gather(after(mixed, all_adjoint_ends), cube, axis=0, tiled=True)
+    mixed_all = lax.all_gather(after(mixed, down_full), cube, axis=0, tiled=True)
     if paired:
         down_back.shift(9, all_adjoint_ends)
     grad_conv, gate_weight_term, gate_sums = by_heads(
@@ -1101,14 +1140,14 @@
             tail,
             all_adjoint_ends,
             decays,
-            rgate,
-            igate,
-            conv_out,
             states,
             entry,
             conv_in,
             conv_before,
+            conv_weight,
+            conv_bias[None],
             gate_weight,
+            gate_bias,
             rate,
         ),
         [(flat, wide), ((2, head_width, width), low), (small, wide)],
@@ -1125,9 +1164,6 @@
     columns = split_columns(pre_grads, turned, half)
     pre_all, branch_all = move(None, (columns, member_columns(grad_branch)), 10, [])
     branch_all = branch_all.reshape(all_rows, -1)
-    sum_a = row_sums(grad_a, second_all)
-    mlp_low = jnp.concatenate([sum_a.astype(low), sum_b_low], 0).reshape(count, -1, width)
-    gain_second_term = gain_sums(sum_a, rows_a) + gain_sums(sum_b, rows_b)
     out_sum = row_sums(branch_all, mixed_all).reshape(count, -1, width)
     out_sums = out_sum.astype(low)
     own_out, other_out = in_turn(out_sum[0], out_sum[1])
@@ -1160,6 +1196,8 @@
     _, first_back = jax.vjp(lambda values: normed(values, gain_first), source)
     input_grad = (grad_middle + first_back(grad_first)[0])[None]
     shared = group_total(scattered[rows:]).astype(low)
+    sum_a = row_sums(after(grad_a, scattered), second_all)
+    mlp_low = jnp.concatenate([sum_a.astype(low), sum_b_low], 0).reshape(count, -1, width)
     mlp_grad = total(sum_a, mlp_back, mlp_low)
 
     if paired:
@@ -1168,12 +1206,7 @@
         down_total = group_sum(down_sums)
     down_total = down_total.astype(low).reshape(block_size, down_rows, half * unit)
     shared_all, down_total = move(shared, (down_total,), 7, [(branch_back, 6)])
-    down_grad = (
-        down_total.reshape(block_size, down_rows, half, unit)
-        .transpose(1, 2, 0, 3)
-        .reshape(down_rows, hidden_width)
-        .astype(wide)
-    )
+    down_grad = down_join_units(down_total, half)
     gate_sum = shared_all[:, :gate_unit].reshape(2, head_width, width)
     gate_weight_grad = jnp.stack(
         [gate_sum[:, :, h * head_width : (h + 1) * head_width] for h in range(heads)], 1
@@ -1194,7 +1227,7 @@
         sums[2] * (-8.0 * jax.nn.sigmoid(decay)),
         out_grad,
         sums[10],
-        sums[12] / gain_second,
+        sums[12],
         mlp_grad,
         down_grad,
     )

time: 861 us -> 824 us (0.957)
  waiting for transfers between devices: 36.1 us -> 22.6 us
  Pallas kernels: 580 us -> 567 us
    pallas_call x5, Pallas kernels: 289 us -> 311 us  [block_move(): pl.pallas_call(functools.partial(move_kernel, pieces, len(swapped), ride)...]
    pallas_call x3, Pallas kernels: 221 us -> 201 us  [block_scatter(): pl.pallas_call(functools.partial(scatter_kernel, pieces, product_rows, tr...]
    pallas_call x2, Pallas kernels: 36.9 us -> 22.6 us  [seq_spread(): pl.pallas_call(functools.partial(spread_kernel, group_count), out_shape=j...]
    ppermute x7, waiting for transfers between devices: 35.3 us -> 21.9 us  [group_shift(): lax.ppermute(values, 'g', [(i, (i + distance) % count) for i in range(cou...]
    unnamed x205 -> x216, local copies, waits for them, and re-layouts: 39.5 us -> 47.2 us
  transfers between devices with their start and end apart: 12 -> 12, of which waited for: 3 -> 2; matrix products, arithmetic and copies ran while one was open for 13% -> 14% of each run, Pallas kernels for 47% -> 40%
where the time goes in v3:
time: 824 us; the launch traced here: 817 us
  Pallas kernels  567 us (69%)
  matrix products  95.1 us (12%)
  local copies, waits for them, and re-layouts  73.8 us (9%)
  other arithmetic  27.5 us (3%)
  waiting for transfers between devices  22.6 us (3%)
  between operations  15.5 us (2%)
  starting transfers between devices  15.4 us (2%)
    pallas_call x5, Pallas kernels, block_move(): pl.pallas_call(functools.partial(move_kernel, pieces, len(swapped), ride)...  311 us
    pallas_call x3, Pallas kernels, block_scatter(): pl.pallas_call(functools.partial(scatter_kernel, pieces, product_rows, tr...  201 us
    unnamed x216, local copies, waits for them, and re-layouts  47.2 us
    dot_general x5, matrix products, row_sums(): lax.dot_general(gradient, operand, (((0,), (0,)), ((), ())), preferred_el...  37.1 us
    dot_general x4, matrix products, times_rows(): lax.dot_general(operand, weight, (((1,), (1,)), ((), ())), preferred_elem...  33.9 us
    pallas_call x5, Pallas kernels, by_heads(): pl.pallas_call(kernel, grid=(heads,), out_shape=[jax.ShapeDtypeStruct(sha...  26.3 us
    dot_general x2, matrix products, times(): return jnp.dot(operand, weight, preferred_element_type=wide)  24.1 us
    pallas_call x2, Pallas kernels, seq_spread(): pl.pallas_call(functools.partial(spread_kernel, group_count), out_shape=j...  22.6 us
  transfers between devices with their start and end apart: 12, of which 2 were waited for; matrix products, arithmetic and copies ran while one was open for 14% of the time, Pallas kernels for 40%

profile of v3, /device:TPU:1, one launch (start us, length us, event | category | flops | bytes accessed | tf_op | source)
XLA Modules:
  0.0 817.0 jit_solution(15192460939163988690)
XLA Ops:
  14.7 99.1 %block_move.5 = (bf16[16,128,2560]{2,1,0:T(8,128)(2,1)S(1)}, bf16[16,80,480]{2,1,0:T(8,128)(2,1)S(1)}, bf16[160,2560]{1,0:T(8,128)(2,1)S(1)}, bf16[48,2560]{1,0:T(8,128)(2,1)S(1)}) custom-call(bf16[128,2560]{1,0:T(8,128)(2,1)S(1)} %fusion.14.refs_0_, bf16[16,80,480]{2,1,0:T(8,128)(2,1)S(1)} %copy-done.29, bf16[160,2560]{1,0:T(8,128)(2,1)S(1)} %copy-done.36, ...), custom_call_target="tpu_custom_call" | custom-call | tf_op jit(solution)/shard_map/block_move/pallas_call | solution.py:239
  113.8 3.8 copy-done.1
  123.8 8.7 %convolution_convert_fusion.1 = bf16[2048,320]{0,1:T(8,128)(2,1)} fusion(bf16[2048,2560]{1,0:T(8,128)(2,1)} %bitcast.127, bf16[320,2560]{1,0:T(8,128)(2,1)S(1)} %constant_dynamic-update-slice_fusion.refs_1_), kind=kOutput, calls=%fused_computation.19 | convolution fusion | flops 3356098560 | bytes 13434880 | tf_op jit(solution)/shard_map/dot_general | solution.py:901
  132.5 2.5 copy.49
  136.7 58.7 %block_move.6 = (bf16[16,128,320]{2,1,0:T(8,128)(2,1)S(1)}, bf16[208,2560]{1,0:T(8,128)(2,1)S(1)}) custom-call(bf16[16,128,320]{2,1,0:T(8,128)(2,1)S(1)} %bitcast.132, bf16[480,2560]{1,0:T(8,128)(2,1)S(1)} %copy-done), custom_call_target="tpu_custom_call" | custom-call | tf_op jit(solution)/shard_map/block_move/pallas_call | solution.py:239
  198.8 3.1 joined_columns.1
  204.6 3.9 collective-permute-start
  214.8 1.8 copy-done.6
  219.4 7.4 shard_map.262
  226.8 12.4 %seq_spread.2.ends_ref = f32[8,2,2560]{2,1,0:T(2,128)S(1)} custom-call(f32[2,2560]{1,0:T(2,128)S(1)} %get-tuple-element.68.x_ref), custom_call_target="tpu_custom_call" | custom-call | tf_op jit(solution)/shard_map/seq_spread/pallas_call | solution.py:539
  241.4 3.9 shard_map.263
  246.4 1.8 constant_dynamic-update-slice_fusion.3
  248.3 20.1 %collective-permute-done.2 = bf16[128,2560]{1,0:T(8,128)(2,1)S(1)} collective-permute-done((bf16[128,2560]{1,0:T(8,128)(2,1)S(1)}, bf16[128,2560]{1,0:T(8,128)(2,1)S(1)}, u32[]{:S(2)}, u32[]{:S(2)}) %collective-permute-start.2) | collective-permute-done | bytes 655392 | tf_op jit(solution)/shard_map/ppermute | solution.py:469
  269.2 9.3 %multiply_reduce_fusion.3 = (f32[128]{0:T(128)S(1)}, f32[128,2560]{1,0:T(8,128)S(1)}) fusion(f32[2560]{0:T(1024)S(1)} %copy-done.90, bf16[128,2560]{1,0:T(8,128)(2,1)} %get-tuple-element.96, bf16[2560,2560]{1,0:T(8,128)(2,1)} %all-gather.4.cloned.1.call-done, bf16[1,128,2560]{2,1,0:T(8,128)(2,1)S(1)} %copy-done.64), kind=kOutput, calls=%fused_computation.49 | convolution fusion | flops 1679359872 | bytes 15739392 | tf_op jit(solution)/shard_map/dot_general | solution.py:901
  280.4 53.4 %block_move.7 = (bf16[16,128,2560]{2,1,0:T(8,128)(2,1)S(1)}, bf16[960,480]{1,0:T(8,128)(2,1)S(1)}) custom-call(bf16[128,2560]{1,0:T(8,128)(2,1)S(1)} %multiply_convert_fusion.2.refs_0_, bf16[1280,480]{1,0:T(8,128)(2,1)S(1)} %bitcast.129), custom_call_target="tpu_custom_call" | custom-call | tf_op jit(solution)/shard_map/block_move/pallas_call | solution.py:239
  334.8 3.2 collective-permute-start.3
  337.9 7.2 fusion.43
  345.1 8.7 %fusion.42 = f32[2048,480]{1,0:T(8,128)} fusion(bf16[2048,2560]{1,0:T(8,128)(2,1)S(1)} %bitcast.137, bf16[480,2560]{1,0:T(8,128)(2,1)} %constant_dynamic-update-slice_fusion.2.refs_3_), kind=kOutput, calls=%fused_computation.115 | convolution fusion | flops 5033164800 | bytes 16875520 | tf_op jit(solution)/shard_map/dot_general | solution.py:901
  353.8 16.8 %broadcast_select_fusion = (bf16[2048,480]{1,0:T(8,128)(2,1)S(1)}, bf16[2048,480]{1,0:T(8,128)(2,1)}, bf16[2048,480]{1,0:T(8,128)(2,1)}, f32[2048,480]{1,0:T(8,128)}) fusion(pred[]{:T(512)S(6)} %eq.3, f32[2048,480]{1,0:T(8,128)} %fusion.43, f32[2048,480]{1,0:T(8,128)} %fusion.42, bf16[2048,2560]{1,0:T(8,128)(2,1)} %all-gather.6.cloned.1.call-done, ...), kind=kOutput, calls=%fused_computation.27 | convolution fusion | flops 5067079680 | bytes 30638080 | tf_op jit(solution)/shard_map/dot_general | solution.py:907
  370.7 4.5 multiply_convert_fusion.1.refs_0_
  375.2 2.7 copy-done.56
  377.9 6.7 convolution_convert_fusion.refs_4_.refs_2_
  384.8 68.6 %block_scatter.3 = (f32[128,2560]{1,0:T(8,128)S(1)}, bf16[240,2560]{1,0:T(8,128)(2,1)S(1)}) custom-call(bf16[2048,480]{1,0:T(8,128)(2,1)S(1)} %broadcast_select_fusion.1.refs_0_, bf16[2048,480]{1,0:T(8,128)(2,1)S(1)} %get-tuple-element.118.refs_1_, bf16[480,2560]{1,0:T(8,128)(2,1)} %refs_2_.3, bf16[480,2560]{1,0:T(8,128)(2,1)} %constant_dynamic-update-slice_fusion.2.refs_3_, ...), custom_call_target="tpu_custom_call" | custom-call | tf_op jit(solution)/shard_map/block_scatter/pallas_call | solution.py:443
  455.5 65.2 %block_scatter.4 = (f32[128,2560]{1,0:T(8,128)S(1)}, bf16[240,2560]{1,0:T(8,128)(2,1)S(1)}) custom-call(bf16[2048,480]{1,0:T(8,128)(2,1)S(1)} %multiply_convert_fusion.1.refs_0_, bf16[2560,480]{1,0:T(8,128)(2,1)S(1)} %pad_maximum_fusion.refs_1_, bf16[480,2560]{1,0:T(8,128)(2,1)S(1)} %copy-done.11), custom_call_target="tpu_custom_call" | custom-call | tf_op jit(solution)/shard_map/block_scatter/pallas_call | solution.py:443
  522.0 2.2 multiply_reduce_fusion.1
  524.8 7.3 fusion.44.grad_mixed_ref
  532.2 2.7 shard_map.264
  534.9 10.2 %seq_spread.3.ends_ref = f32[8,2,2560]{2,1,0:T(2,128)S(1)} custom-call(f32[2,2560]{1,0:T(2,128)S(1)} %get-tuple-element.86.x_ref), custom_call_target="tpu_custom_call" | custom-call | tf_op jit(solution)/shard_map/seq_spread/pallas_call | solution.py:539
  545.2 9.9 %shard_map.265 = (f32[128,2560]{1,0:T(8,128)S(1)}, bf16[2,256,2560]{2,1,0:T(8,128)(2,1)S(1)}, f32[8,2560]{1,0:T(8,128)S(1)}) custom-call(s32[1]{0:T(128)} %bitcast.1.position_ref, f32[128,2560]{1,0:T(8,128)S(1)} %get-tuple-element.84.local_ref, f32[128,2560]{1,0:T(8,128)S(1)} %get-tuple-element.85.product_ref, f32[8,2,2560]{2,1,0:T(2,128)S(1)} %seq_spread.3.ends_ref, ...), custom_call_target="tpu_custom_call" | custom-call | tf_op jit(solution)/shard_map/pallas_call | solution.py:787
  559.7 7.9 fusion.41
  570.1 1.8 slice.201
  571.9 2.3 slice.200
  574.2 1.8 slice.199
  577.8 2.0 collective-permute-start.6
  583.8 2.3 shard_map.266
  587.4 60.6 %block_move.8 = (bf16[16,128,320]{2,1,0:T(8,128)(2,1)S(1)}, bf16[16,128,160]{2,1,0:T(8,128)(2,1)S(1)}) custom-call(bf16[16,128,320]{2,1,0:T(8,128)(2,1)S(1)} %split_columns.1.refs_0_, bf16[16,128,160]{2,1,0:T(8,128)(2,1)S(1)} %copy-done.35), custom_call_target="tpu_custom_call" | custom-call | tf_op jit(solution)/shard_map/block_move/pallas_call | solution.py:239
  650.5 6.6 multiply_reduce_fusion
  657.2 2.9 maximum_maximum_fusion.refs_2_
  663.5 2.7 concatenate.62
  666.1 3.0 fusion.8
  670.7 6.3 fusion.45
  677.2 67.6 %block_scatter.5 = (f32[176,2560]{1,0:T(8,128)S(1)}, bf16[96,2560]{1,0:T(8,128)(2,1)S(1)}, bf16[80,2560]{1,0:T(8,128)(2,1)S(1)}) custom-call(bf16[2048,320]{1,0:T(8,128)(2,1)S(1)} %bitcast.128, bf16[320,2560]{1,0:T(8,128)(2,1)S(1)} %copy-done.10, bf16[16,48,2560]{2,1,0:T(8,128)(2,1)} %maximum_maximum_fusion.refs_2_, ...), custom_call_target="tpu_custom_call" | custom-call | tf_op jit(solution)/shard_map/block_scatter/pallas_call | solution.py:443
  745.2 1.9 collective-permute-start.5
  747.3 9.7 %convert_add_fusion = f32[480,2560]{1,0:T(8,128)} fusion(bf16[240,2560]{1,0:T(8,128)(2,1)S(1)} %copy-done.60, bf16[240,2560]{1,0:T(8,128)(2,1)S(1)} %copy-done.58, bf16[2048,480]{1,0:T(8,128)(2,1)S(1)} %copy-done.15, bf16[2048,2560]{1,0:T(8,128)(2,1)} %bitcast.138), kind=kOutput, calls=%fused_computation.2 | convolution fusion | flops 5039308800 | bytes 19824640 | tf_op jit(solution)/shard_map/dot_general | solution.py:911
  757.0 2.3 fusion.11
  760.3 39.2 %block_move.9 = (bf16[16,48,2560]{2,1,0:T(8,128)(2,1)S(1)}, bf16[16,80,480]{2,1,0:T(8,128)(2,1)S(1)}, bf16[64,2560]{1,0:T(8,128)(2,1)S(1)}) custom-call(bf16[48,2560]{1,0:T(8,128)(2,1)S(1)} %add_convert_fusion.refs_0_, bf16[16,80,480]{2,1,0:T(8,128)(2,1)S(1)} %bitcast.133, bf16[160,2560]{1,0:T(8,128)(2,1)S(1)} %slice.276.refs_3_.refs_2_), custom_call_target="tpu_custom_call" | custom-call | tf_op jit(solution)/shard_map/block_move/pallas_call | solution.py:239
  801.4 3.0 convert_element_type.116
  804.4 1.8 down_join.1
  (286 shorter events, 69.9 us)
Async XLA Ops:
  7.2 262.0 %all-gather.4.cloned.1.call-start = ((), (), s32[]{:S(2)}) async-start(), calls=%async_computation | async-start | bytes 13516800 | tf_op jit(solution)/shard_map/all_gather | solution.py:1032
  7.9 345.9 %all-gather.6.cloned.1.call-start = ((), (), s32[]{:S(2)}) async-start(), calls=%async_computation.1 | async-start | bytes 11141120 | tf_op jit(solution)/shard_map/all_gather | solution.py:1042
  14.7 105.6 %copy-start.66 = (bf16[1,128,2560]{2,1,0:T(8,128)(2,1)S(1)}, bf16[1,128,2560]{2,1,0:T(8,128)(2,1)}, u32[]{:S(2)}) copy-start(bf16[1,128,2560]{2,1,0:T(8,128)(2,1)} %param.29) | copy-start | bytes 1966084
  121.4 549.4 %all-gather.8.cloned.1.call-start = ((), (), s32[]{:S(2)}) async-start(), calls=%async_computation.2 | async-start | bytes 11141120 | tf_op jit(solution)/shard_map/all_gather | solution.py:1130
  196.6 13.5 %copy-start.88 = (f32[2560]{0:T(1024)S(1)}, f32[2560]{0:T(1024)}, u32[]{:S(2)}) copy-start(f32[2560]{0:T(1024)} %param.23) | copy-start | bytes 30724
  198.8 10.7 %copy-start.52 = (bf16[48,2560]{1,0:T(8,128)(2,1)S(1)}, bf16[48,2560]{1,0:T(8,128)(2,1)}, u32[]{:S(2)}) copy-start(bf16[48,2560]{1,0:T(8,128)(2,1)} %copy-done.51) | copy-start | bytes 737284
  204.6 10.2 %collective-permute-start = (f32[8,2560]{1,0:T(8,128)}, f32[8,2560]{1,0:T(8,128)}, u32[]{:S(2)}, u32[]{:S(2)}) collective-permute-start(f32[8,2560]{1,0:T(8,128)} %slice.149), channel_id=1, source_target_pairs={{0,4},{4,8},{8,12},{12,16},{16,20},{20,24},{24,28},{1,5},{5,9},{9,... | collective-permute-start | bytes 245768 | tf_op jit(solution)/shard_map/ppermute | solution.py:557
  209.3 37.1 %collective-permute-start.1 = (bf16[96,2560]{1,0:T(8,128)(2,1)}, bf16[96,2560]{1,0:T(8,128)(2,1)}, u32[]{:S(2)}, u32[]{:S(2)}) collective-permute-start(bf16[96,2560]{1,0:T(8,128)(2,1)} %slice.150), channel_id=1, source_target_pairs={{0,16},{16,0},{1,17},{17,1},{2,18},{18,2},{3,19},{19,3},{4,20},{20... | collective-permute-start | bytes 1474568 | tf_op jit(solution)/shard_map/ppermute | solution.py:469
  219.4 19.9 %copy-start.78 = (bf16[128,2560]{1,0:T(8,128)(2,1)S(1)}, bf16[128,2560]{1,0:T(8,128)(2,1)}, u32[]{:S(2)}) copy-start(bf16[128,2560]{1,0:T(8,128)(2,1)} %slice.151) | copy-start | bytes 1966084
  219.4 22.0 %copy-start.3 = (f32[128,2560]{1,0:T(8,128)S(1)}, f32[128,2560]{1,0:T(8,128)}, u32[]{:S(2)}) copy-start(f32[128,2560]{1,0:T(8,128)} %copy-done.2) | copy-start | bytes 3932164
  226.8 18.5 %copy-start.33 = (f32[128,2560]{1,0:T(8,128)}, f32[128,2560]{1,0:T(8,128)S(1)}, u32[]{:S(2)}) copy-start(f32[128,2560]{1,0:T(8,128)S(1)} %get-tuple-element.83.decay_ref) | copy-start | bytes 3932164
  239.2 29.1 %collective-permute-start.2 = (bf16[128,2560]{1,0:T(8,128)(2,1)S(1)}, bf16[128,2560]{1,0:T(8,128)(2,1)S(1)}, u32[]{:S(2)}, u32[]{:S(2)}) collective-permute-start(bf16[128,2560]{1,0:T(8,128)(2,1)S(1)} %copy-done.78), channel_id=1, source_target_pairs={{0,16},{16,0},{1,17},{17,1},{2,18},{18,2},{3,19},{19,3},{4,20},{20... | collective-permute-start | bytes 1966088 | tf_op jit(solution)/shard_map/ppermute | solution.py:469
  241.4 27.8 %copy-start.64 = (bf16[1,128,2560]{2,1,0:T(8,128)(2,1)S(1)}, bf16[1,128,2560]{2,1,0:T(8,128)(2,1)}, u32[]{:S(2)}) copy-start(bf16[1,128,2560]{2,1,0:T(8,128)(2,1)} %param.15) | copy-start | bytes 1966084
  241.4 27.8 %copy-start.90 = (f32[2560]{0:T(1024)S(1)}, f32[2560]{0:T(1024)}, u32[]{:S(2)}) copy-start(f32[2560]{0:T(1024)} %param.25) | copy-start | bytes 30724
  278.6 66.5 %copy-start.61 = (f32[128,2560]{1,0:T(8,128)}, f32[128,2560]{1,0:T(8,128)S(1)}, u32[]{:S(2)}) copy-start(f32[128,2560]{1,0:T(8,128)S(1)} %get-tuple-element.131) | copy-start | bytes 3932164
  278.6 56.2 %copy-start.82 = (bf16[4,80,480]{2,1,0:T(8,128)(2,1)S(1)}, bf16[4,80,480]{2,1,0:T(8,128)(2,1)}, u32[]{:S(2)}) copy-start(bf16[4,80,480]{2,1,0:T(8,128)(2,1)} %slice.154) | copy-start | bytes 921604
  334.8 10.3 %copy-start.55 = (bf16[16,128,2560]{2,1,0:T(8,128)(2,1)}, bf16[16,128,2560]{2,1,0:T(8,128)(2,1)S(1)}, u32[]{:S(2)}) copy-start(bf16[16,128,2560]{2,1,0:T(8,128)(2,1)S(1)} %get-tuple-element.72) | copy-start | bytes 31457284
  334.8 19.0 %collective-permute-start.3 = (bf16[320,480]{1,0:T(8,128)(2,1)S(1)}, bf16[320,480]{1,0:T(8,128)(2,1)S(1)}, u32[]{:S(2)}, u32[]{:S(2)}) collective-permute-start(bf16[320,480]{1,0:T(8,128)(2,1)S(1)} %bitcast.153), channel_id=1, source_target_pairs={{0,16},{16,0},{1,17},{17,1},{2,18},{18,2},{3,19},{19,3},{4,20},{20... | collective-permute-start | bytes 921608 | tf_op jit(solution)/shard_map/ppermute | solution.py:469
  375.2 78.6 %copy-start.16 = (bf16[2048,480]{1,0:T(8,128)(2,1)}, bf16[2048,480]{1,0:T(8,128)(2,1)S(1)}, u32[]{:S(2)}) copy-start(bf16[2048,480]{1,0:T(8,128)(2,1)S(1)} %multiply_convert_fusion.1.refs_0_) | copy-start | bytes 5898244
  384.8 68.6 %copy-start.14 = (bf16[2048,480]{1,0:T(8,128)(2,1)}, bf16[2048,480]{1,0:T(8,128)(2,1)S(1)}, u32[]{:S(2)}) copy-start(bf16[2048,480]{1,0:T(8,128)(2,1)S(1)} %broadcast_select_fusion.1.refs_0_) | copy-start | bytes 5898244
  384.8 68.6 %copy-start.47 = (bf16[960,480]{1,0:T(8,128)(2,1)S(1)}, bf16[960,480]{1,0:T(8,128)(2,1)}, u32[]{:S(2)}) copy-start(bf16[960,480]{1,0:T(8,128)(2,1)} %copy-done.45) | copy-start | bytes 2764804
  524.8 20.4 %copy-start.31 = (f32[128,2560]{1,0:T(8,128)S(1)}, f32[128,2560]{1,0:T(8,128)}, u32[]{:S(2)}) copy-start(f32[128,2560]{1,0:T(8,128)} %copy-done.30) | copy-start | bytes 3932164
  524.8 34.9 %slice-start.1 = ((s8[10485760]{0:T(1024)(128)(4,1)}), s8[4194304]{0:T(1024)(128)(4,1)S(1)}, s32[]{:S(2)}) async-start(s8[10485760]{0:T(1024)(128)(4,1)} %bitcast.157), calls=%async_computation.4 | async-start | bytes 8388608
  524.8 34.9 %slice-start.2 = ((s8[10485760]{0:T(1024)(128)(4,1)}), s8[4194304]{0:T(1024)(128)(4,1)S(1)}, s32[]{:S(2)}) async-start(s8[10485760]{0:T(1024)(128)(4,1)} %bitcast.157), calls=%async_computation.5 | async-start | bytes 8388608
  532.1 13.1 %copy-start.7 = (bf16[2,10,256,256]{3,2,1,0:T(8,128)(2,1)S(1)}, bf16[2,10,256,256]{3,2,1,0:T(8,128)(2,1)}, u32[]{:S(2)}) copy-start(bf16[2,10,256,256]{3,2,1,0:T(8,128)(2,1)} %weight_ref.3) | copy-start | bytes 7864324
  532.1 13.1 %copy-start.24 = (f32[128,2560]{1,0:T(8,128)S(1)}, f32[128,2560]{1,0:T(8,128)}, u32[]{:S(2)}) copy-start(f32[128,2560]{1,0:T(8,128)} %copy-done.22) | copy-start | bytes 3932164
  532.1 13.1 %copy-start.50 = (f32[4,2560]{1,0:T(4,128)S(1)}, f32[4,2560]{1,0:T(4,128)}, u32[]{:S(2)}) copy-start(f32[4,2560]{1,0:T(4,128)} %taps_ref.5) | copy-start | bytes 122884
  532.2 13.1 %copy-start.54 = (f32[2,2560]{1,0:T(2,128)S(1)}, f32[2,2560]{1,0:T(2,128)}, u32[]{:S(2)}) copy-start(f32[2,2560]{1,0:T(2,128)} %gate_bias_ref.3) | copy-start | bytes 61444
  532.2 27.5 %slice-start.3 = ((s8[10485760]{0:T(1024)(128)(4,1)}), s8[2097152]{0:T(1024)(128)(4,1)S(1)}, s32[]{:S(2)}) async-start(s8[10485760]{0:T(1024)(128)(4,1)} %bitcast.157), calls=%async_computation.6 | async-start | bytes 4194304
  545.2 14.5 %copy-start.17 = (bf16[2048,480]{1,0:T(8,128)(2,1)S(1)}, bf16[2048,480]{1,0:T(8,128)(2,1)}, u32[]{:S(2)}) copy-start(bf16[2048,480]{1,0:T(8,128)(2,1)} %copy-done.16) | copy-start | bytes 5898244
  557.7 22.1 %collective-permute-start.4 = (f32[8,2560]{1,0:T(8,128)S(1)}, f32[8,2560]{1,0:T(8,128)S(1)}, u32[]{:S(2)}, u32[]{:S(2)}) collective-permute-start(f32[8,2560]{1,0:T(8,128)S(1)} %slice.158), channel_id=1, source_target_pairs={{4,0},{8,4},{12,8},{16,12},{20,16},{24,20},{28,24},{5,1},{9,5},{13... | collective-permute-start | bytes 245768 | tf_op jit(solution)/shard_map/ppermute | solution.py:557
  577.4 86.0 %collective-permute-start.7 = (bf16[720,480]{0,1:T(8,128)(2,1)}, bf16[720,480]{0,1:T(8,128)(2,1)}, u32[]{:S(2)}, u32[]{:S(2)}) collective-permute-start(bf16[720,480]{0,1:T(8,128)(2,1)} %slice.200), channel_id=1, source_target_pairs={{0,16},{16,0},{1,17},{17,1},{2,18},{18,2},{3,19},{19,3},{4,20},{20... | collective-permute-start | bytes 2073608 | tf_op jit(solution)/shard_map/ppermute | solution.py:469
  577.8 84.2 %collective-permute-start.6 = (bf16[400,480]{0,1:T(8,128)(2,1)}, bf16[400,480]{0,1:T(8,128)(2,1)S(1)}, u32[]{:S(2)}, u32[]{:S(2)}) collective-permute-start(bf16[400,480]{0,1:T(8,128)(2,1)} %slice.199), channel_id=1, source_target_pairs={{0,16},{16,0},{1,17},{17,1},{2,18},{18,2},{3,19},{19,3},{4,20},{20... | collective-permute-start | bytes 1152008 | tf_op jit(solution)/shard_map/ppermute | solution.py:469
  586.1 62.8 %copy-start.83 = (bf16[160,480]{0,1:T(8,128)(2,1)S(1)}, bf16[160,480]{0,1:T(8,128)(2,1)}, u32[]{:S(2)}) copy-start(bf16[160,480]{0,1:T(8,128)(2,1)} %slice.201) | copy-start | bytes 460804
  586.1 64.3 %copy-start.81 = (bf16[16,1,2560]{2,1,0:T(2,128)(2,1)S(1)}, bf16[16,1,2560]{2,1,0:T(2,128)(2,1)}, u32[]{:S(2)}) copy-start(bf16[16,1,2560]{2,1,0:T(2,128)(2,1)} %copy_dynamic-update-slice_fusion) | copy-start | bytes 245764
  586.2 64.4 %copy-start.9 = (bf16[320,2560]{1,0:T(8,128)(2,1)S(1)}, bf16[320,2560]{1,0:T(8,128)(2,1)}, u32[]{:S(2)}) copy-start(bf16[320,2560]{1,0:T(8,128)(2,1)} %copy-done.8) | copy-start | bytes 4915204
  649.0 13.0 %collective-permute-start.8 = (bf16[160,480]{0,1:T(8,128)(2,1)S(1)}, bf16[160,480]{0,1:T(8,128)(2,1)S(1)}, u32[]{:S(2)}, u32[]{:S(2)}) collective-permute-start(bf16[160,480]{0,1:T(8,128)(2,1)S(1)} %copy-done.83), channel_id=1, source_target_pairs={{0,16},{16,0},{1,17},{17,1},{2,18},{18,2},{3,19},{19,3},{4,20},{20... | collective-permute-start | bytes 460808 | tf_op jit(solution)/shard_map/ppermute | solution.py:469
  677.2 67.8 %copy-start.65 = (bf16[1,128,2560]{2,1,0:T(8,128)(2,1)S(1)}, bf16[1,128,2560]{2,1,0:T(8,128)(2,1)}, u32[]{:S(2)}) copy-start(bf16[1,128,2560]{2,1,0:T(8,128)(2,1)} %param.15) | copy-start | bytes 1966084
  677.2 67.8 %copy-start.86 = (f32[2560]{0:T(1024)S(1)}, f32[2560]{0:T(1024)}, u32[]{:S(2)}) copy-start(f32[2560]{0:T(1024)} %param.16) | copy-start | bytes 30724
  677.2 70.0 %copy-start.58 = (bf16[240,2560]{1,0:T(8,128)(2,1)S(1)}, bf16[240,2560]{1,0:T(8,128)(2,1)}, u32[]{:S(2)}) copy-start(bf16[240,2560]{1,0:T(8,128)(2,1)} %copy-done.57) | copy-start | bytes 3686404
  677.2 70.0 %copy-start.60 = (bf16[240,2560]{1,0:T(8,128)(2,1)S(1)}, bf16[240,2560]{1,0:T(8,128)(2,1)}, u32[]{:S(2)}) copy-start(bf16[240,2560]{1,0:T(8,128)(2,1)} %copy-done.59) | copy-start | bytes 3686404
  745.2 15.0 %collective-permute-start.5 = (bf16[48,2560]{1,0:T(8,128)(2,1)S(1)}, bf16[48,2560]{1,0:T(8,128)(2,1)S(1)}, u32[]{:S(2)}, u32[]{:S(2)}) collective-permute-start(bf16[48,2560]{1,0:T(8,128)(2,1)S(1)} %slice.277), channel_id=1, source_target_pairs={{0,16},{16,0},{1,17},{17,1},{2,18},{18,2},{3,19},{19,3},{4,20},{20... | collective-permute-start | bytes 737288 | tf_op jit(solution)/shard_map/ppermute | solution.py:469
  747.2 9.7 %copy-start.27 = (f32[128,2560]{1,0:T(8,128)S(1)}, f32[128,2560]{1,0:T(8,128)}, u32[]{:S(2)}) copy-start(f32[128,2560]{1,0:T(8,128)} %copy-done.25) | copy-start | bytes 3932164
  747.2 9.7 %copy-start.63 = (f32[128,2560]{1,0:T(8,128)S(1)}, f32[128,2560]{1,0:T(8,128)}, u32[]{:S(2)}) copy-start(f32[128,2560]{1,0:T(8,128)} %copy-done.61) | copy-start | bytes 3932164
  747.2 9.7 %copy-start.68 = (bf16[1,128,2560]{2,1,0:T(8,128)(2,1)S(1)}, bf16[1,128,2560]{2,1,0:T(8,128)(2,1)}, u32[]{:S(2)}) copy-start(bf16[1,128,2560]{2,1,0:T(8,128)(2,1)} %param.29) | copy-start | bytes 1966084
  747.2 9.7 %copy-start.73 = (f32[128,1280]{1,0:T(8,128)S(1)}, f32[128,1280]{1,0:T(8,128)}, u32[]{:S(2)}) copy-start(f32[128,1280]{1,0:T(8,128)} %get-tuple-element.124) | copy-start | bytes 1966084
  747.2 9.7 %copy-start.74 = (f32[128,1280]{1,0:T(8,128)S(1)}, f32[128,1280]{1,0:T(8,128)}, u32[]{:S(2)}) copy-start(f32[128,1280]{1,0:T(8,128)} %get-tuple-element.125) | copy-start | bytes 1966084
  747.2 9.7 %copy-start.92 = (f32[128]{0:T(128)S(1)}, f32[128]{0:T(128)}, u32[]{:S(2)}) copy-start(f32[128]{0:T(128)} %copy-done.91) | copy-start | bytes 1540
  (63 other events, 201.5 us)
Sparse Core Ops, SparseCore 0:
  10.9 163.5 all-gather.3
  176.1 87.2 all-gather.5
  522.0 66.1 all-gather.7

commit v4 on v3

--- a/solution.py
+++ b/solution.py
@@ -1046,7 +1046,7 @@
     pre_part = pre_part.reshape(block_size, rows, 2 * width // block_size)
     pre = move(None, (pre_part,), 2, [(mlp_trade, 7)])
     if paired:
-        mlp_trade.shift(3, pre)
+        mlp_trade.shift(4, pre)
     gate_pre, conv_in = joined_columns(pre, branch_bias.reshape(2, width), turned, half)
     conv_before = rim_rows(conv_in[rows - 8 :], 1)
 
@@ -1069,7 +1069,7 @@
     )
     all_ends = seq_spread(ends, 3)
     if paired:
-        mlp_trade.shift(4, all_ends)
+        mlp_trade.shift(3, all_ends)
     states, mixed, entry = by_heads(
         full_states_kernel,
         heads,
@@ -1110,7 +1110,7 @@
     down_full = scatter([(down_left, down_columns, True)], 6, [(mlp_back, 8)])
     output = (middle + turn_halves(down_full)).astype(low)[None]
     if paired:
-        down_back.shift(5, down_full)
+        down_back.shift(2, down_full)
 
     _, second_back = jax.vjp(normed, middle, gain_second)
     grad_mid_norm, gain_second_term = second_back(grad_second)
@@ -1129,7 +1129,7 @@
     all_adjoint_ends = seq_spread(adjoint_ends, 9)
     mixed_all = lax.all_gather(after(mixed, down_full), cube, axis=0, tiled=True)
     if paired:
-        down_back.shift(9, all_adjoint_ends)
+        down_back.shift(8, all_adjoint_ends)
     grad_conv, gate_weight_term, gate_sums = by_heads(
         gate_grads_kernel,
         heads,
@@ -1169,7 +1169,7 @@
     own_out, other_out = in_turn(out_sum[0], out_sum[1])
     out_back = Exchange(other_out.astype(low))
     if paired:
-        down_back.shift(2, pre_all)
+        down_back.shift(6, pre_all)
     pre_all = pre_all.reshape(all_rows, -1)
     branch_sum = row_sums(pre_all, first_all)
     branch_sums = branch_sum.astype(low).reshape(count, -1, width)
@@ -1190,7 +1190,7 @@
         1,
     )
     scattered = scatter(
-        [(pre_all, branch_rows, False)], 11, [(branch_back, 10), (out_back, 16)], shared_part
+        [(pre_all, branch_rows, False)], 11, [(branch_back, 8), (out_back, 16)], shared_part
     )
     grad_first = scattered[:rows]
     _, first_back = jax.vjp(lambda values: normed(values, gain_first), source)
@@ -1205,7 +1205,7 @@
     else:
         down_total = group_sum(down_sums)
     down_total = down_total.astype(low).reshape(block_size, down_rows, half * unit)
-    shared_all, down_total = move(shared, (down_total,), 7, [(branch_back, 6)])
+    shared_all, down_total = move(shared, (down_total,), 7, [(branch_back, 8)])
     down_grad = down_join_units(down_total, half)
     gate_sum = shared_all[:, :gate_unit].reshape(2, head_width, width)
     gate_weight_grad = jnp.stack(

time: 824 us -> 829 us (level)
    unnamed x216 -> x220, local copies, waits for them, and re-layouts: 47.2 us -> 46.4 us
where the time goes in v4:
time: 829 us; the launch traced here: 822 us
  Pallas kernels  569 us (69%)
  matrix products  94.8 us (11%)
  local copies, waits for them, and re-layouts  75.1 us (9%)
  other arithmetic  28.3 us (3%)
  waiting for transfers between devices  25.5 us (3%)
  between operations  15.5 us (2%)
  starting transfers between devices  13.9 us (2%)
    pallas_call x5, Pallas kernels, block_move(): pl.pallas_call(functools.partial(move_kernel, pieces, len(swapped), ride)...  305 us
    pallas_call x3, Pallas kernels, block_scatter(): pl.pallas_call(functools.partial(scatter_kernel, pieces, product_rows, tr...  201 us
    unnamed x220, local copies, waits for them, and re-layouts  46.4 us
    dot_general x5, matrix products, row_sums(): lax.dot_general(gradient, operand, (((0,), (0,)), ((), ())), preferred_el...  36.8 us
    dot_general x4, matrix products, times_rows(): lax.dot_general(operand, weight, (((1,), (1,)), ((), ())), preferred_elem...  33.9 us
    pallas_call x2, Pallas kernels, seq_spread(): pl.pallas_call(functools.partial(spread_kernel, group_count), out_shape=j...  30.7 us
    pallas_call x5, Pallas kernels, by_heads(): pl.pallas_call(kernel, grid=(heads,), out_shape=[jax.ShapeDtypeStruct(sha...  26.2 us
    ppermute x7, waiting for transfers between devices, group_shift(): lax.ppermute(values, 'g', [(i, (i + distance) % count) for i in range(cou...  24.8 us
  transfers between devices with their start and end apart: 12, of which 2 were waited for; matrix products, arithmetic and copies ran while one was open for 14% of the time, Pallas kernels for 40%

profile of v4, /device:TPU:1, one launch (start us, length us, event | category | flops | bytes accessed | tf_op | source)
XLA Modules:
  0.0 821.6 jit_solution(10680212622998778343)
XLA Ops:
  14.7 99.1 %block_move.5 = (bf16[16,128,2560]{2,1,0:T(8,128)(2,1)S(1)}, bf16[16,80,480]{2,1,0:T(8,128)(2,1)S(1)}, bf16[160,2560]{1,0:T(8,128)(2,1)S(1)}, bf16[48,2560]{1,0:T(8,128)(2,1)S(1)}) custom-call(bf16[128,2560]{1,0:T(8,128)(2,1)S(1)} %fusion.14.refs_0_, bf16[16,80,480]{2,1,0:T(8,128)(2,1)S(1)} %copy-done.29, bf16[160,2560]{1,0:T(8,128)(2,1)S(1)} %copy-done.37, ...), custom_call_target="tpu_custom_call" | custom-call | tf_op jit(solution)/shard_map/block_move/pallas_call | solution.py:239
  113.8 3.8 copy-done.1
  123.8 8.7 %convolution_convert_fusion.1 = bf16[2048,320]{0,1:T(8,128)(2,1)} fusion(bf16[2048,2560]{1,0:T(8,128)(2,1)} %bitcast.127, bf16[320,2560]{1,0:T(8,128)(2,1)S(1)} %constant_dynamic-update-slice_fusion.refs_1_), kind=kOutput, calls=%fused_computation.19 | convolution fusion | flops 3356098560 | bytes 13434880 | tf_op jit(solution)/shard_map/dot_general | solution.py:901
  132.5 2.5 copy.49
  136.7 58.7 %block_move.6 = (bf16[16,128,320]{2,1,0:T(8,128)(2,1)S(1)}, bf16[208,2560]{1,0:T(8,128)(2,1)S(1)}) custom-call(bf16[16,128,320]{2,1,0:T(8,128)(2,1)S(1)} %bitcast.132, bf16[480,2560]{1,0:T(8,128)(2,1)S(1)} %copy-done), custom_call_target="tpu_custom_call" | custom-call | tf_op jit(solution)/shard_map/block_move/pallas_call | solution.py:239
  198.8 3.1 joined_columns.1
  204.6 3.9 collective-permute-start
  213.1 1.7 copy-done.6
  217.6 7.3 shard_map.262
  226.1 20.4 %seq_spread.2.ends_ref = f32[8,2,2560]{2,1,0:T(2,128)S(1)} custom-call(f32[2,2560]{1,0:T(2,128)S(1)} %get-tuple-element.68.x_ref), custom_call_target="tpu_custom_call" | custom-call | tf_op jit(solution)/shard_map/seq_spread/pallas_call | solution.py:539
  250.3 3.9 shard_map.263
  255.2 2.0 constant_dynamic-update-slice_fusion.3
  257.2 11.9 %collective-permute-done.2 = bf16[96,2560]{1,0:T(8,128)(2,1)S(1)} collective-permute-done((bf16[96,2560]{1,0:T(8,128)(2,1)S(1)}, bf16[96,2560]{1,0:T(8,128)(2,1)S(1)}, u32[]{:S(2)}, u32[]{:S(2)}) %collective-permute-start.2) | collective-permute-done | bytes 491552 | tf_op jit(solution)/shard_map/ppermute | solution.py:469
  269.9 9.4 %multiply_reduce_fusion.3 = (f32[128]{0:T(128)S(1)}, f32[128,2560]{1,0:T(8,128)S(1)}) fusion(f32[2560]{0:T(1024)S(1)} %copy-done.89, bf16[128,2560]{1,0:T(8,128)(2,1)} %get-tuple-element.96, bf16[2560,2560]{1,0:T(8,128)(2,1)} %all-gather.4.cloned.1.call-done, bf16[1,128,2560]{2,1,0:T(8,128)(2,1)S(1)} %copy-done.64), kind=kOutput, calls=%fused_computation.49 | convolution fusion | flops 1679359872 | bytes 15739392 | tf_op jit(solution)/shard_map/dot_general | solution.py:901
  281.1 53.7 %block_move.7 = (bf16[16,128,2560]{2,1,0:T(8,128)(2,1)S(1)}, bf16[960,480]{1,0:T(8,128)(2,1)S(1)}) custom-call(bf16[128,2560]{1,0:T(8,128)(2,1)S(1)} %multiply_convert_fusion.2.refs_0_, bf16[1280,480]{1,0:T(8,128)(2,1)S(1)} %bitcast.129), custom_call_target="tpu_custom_call" | custom-call | tf_op jit(solution)/shard_map/block_move/pallas_call | solution.py:239
  335.8 2.2 collective-permute-start.3
  338.0 7.2 fusion.43
  345.2 8.7 %fusion.42 = f32[2048,480]{1,0:T(8,128)} fusion(bf16[2048,2560]{1,0:T(8,128)(2,1)S(1)} %bitcast.137, bf16[480,2560]{1,0:T(8,128)(2,1)} %constant_dynamic-update-slice_fusion.2.refs_3_), kind=kOutput, calls=%fused_computation.115 | convolution fusion | flops 5033164800 | bytes 16875520 | tf_op jit(solution)/shard_map/dot_general | solution.py:901
  353.9 16.8 %broadcast_select_fusion = (bf16[2048,480]{1,0:T(8,128)(2,1)S(1)}, bf16[2048,480]{1,0:T(8,128)(2,1)}, bf16[2048,480]{1,0:T(8,128)(2,1)}, f32[2048,480]{1,0:T(8,128)}) fusion(pred[]{:T(512)S(6)} %eq.3, f32[2048,480]{1,0:T(8,128)} %fusion.43, f32[2048,480]{1,0:T(8,128)} %fusion.42, bf16[2048,2560]{1,0:T(8,128)(2,1)} %all-gather.6.cloned.1.call-done, ...), kind=kOutput, calls=%fused_computation.27 | convolution fusion | flops 5067079680 | bytes 30638080 | tf_op jit(solution)/shard_map/dot_general | solution.py:907
  370.8 4.5 multiply_convert_fusion.1.refs_0_
  375.3 2.7 copy-done.56
  378.0 6.7 convolution_convert_fusion.refs_4_.refs_2_
  384.9 68.3 %block_scatter.3 = (f32[128,2560]{1,0:T(8,128)S(1)}, bf16[240,2560]{1,0:T(8,128)(2,1)S(1)}) custom-call(bf16[2048,480]{1,0:T(8,128)(2,1)S(1)} %broadcast_select_fusion.1.refs_0_, bf16[2048,480]{1,0:T(8,128)(2,1)S(1)} %get-tuple-element.118.refs_1_, bf16[480,2560]{1,0:T(8,128)(2,1)} %refs_2_.3, bf16[480,2560]{1,0:T(8,128)(2,1)} %constant_dynamic-update-slice_fusion.2.refs_3_, ...), custom_call_target="tpu_custom_call" | custom-call | tf_op jit(solution)/shard_map/block_scatter/pallas_call | solution.py:443
  455.3 65.2 %block_scatter.4 = (f32[128,2560]{1,0:T(8,128)S(1)}, bf16[240,2560]{1,0:T(8,128)(2,1)S(1)}) custom-call(bf16[2048,480]{1,0:T(8,128)(2,1)S(1)} %multiply_convert_fusion.1.refs_0_, bf16[2560,480]{1,0:T(8,128)(2,1)S(1)} %pad_maximum_fusion.refs_1_, bf16[480,2560]{1,0:T(8,128)(2,1)S(1)} %copy-done.11), custom_call_target="tpu_custom_call" | custom-call | tf_op jit(solution)/shard_map/block_scatter/pallas_call | solution.py:443
  522.3 2.1 multiply_reduce_fusion.1
  525.6 7.3 fusion.44.grad_mixed_ref
  533.0 2.7 shard_map.264
  535.7 10.3 %seq_spread.3.ends_ref = f32[8,2,2560]{2,1,0:T(2,128)S(1)} custom-call(f32[2,2560]{1,0:T(2,128)S(1)} %get-tuple-element.86.x_ref), custom_call_target="tpu_custom_call" | custom-call | tf_op jit(solution)/shard_map/seq_spread/pallas_call | solution.py:539
  546.0 9.9 %shard_map.265 = (f32[128,2560]{1,0:T(8,128)S(1)}, bf16[2,256,2560]{2,1,0:T(8,128)(2,1)S(1)}, f32[8,2560]{1,0:T(8,128)S(1)}) custom-call(s32[1]{0:T(128)} %bitcast.1.position_ref, f32[128,2560]{1,0:T(8,128)S(1)} %get-tuple-element.84.local_ref, f32[128,2560]{1,0:T(8,128)S(1)} %get-tuple-element.85.product_ref, f32[8,2,2560]{2,1,0:T(2,128)S(1)} %seq_spread.3.ends_ref, ...), custom_call_target="tpu_custom_call" | custom-call | tf_op jit(solution)/shard_map/pallas_call | solution.py:787
  560.5 7.9 fusion.41
  570.9 2.1 slice.201
  573.0 2.2 slice.200
  578.5 2.1 collective-permute-start.6
  584.5 2.3 shard_map.266
  588.1 52.3 %block_move.8 = (bf16[16,128,320]{2,1,0:T(8,128)(2,1)S(1)}, bf16[16,128,160]{2,1,0:T(8,128)(2,1)S(1)}) custom-call(bf16[16,128,320]{2,1,0:T(8,128)(2,1)S(1)} %split_columns.1.refs_0_, bf16[16,128,160]{2,1,0:T(8,128)(2,1)S(1)} %copy-done.36), custom_call_target="tpu_custom_call" | custom-call | tf_op jit(solution)/shard_map/block_move/pallas_call | solution.py:239
  641.7 6.6 multiply_reduce_fusion
  648.4 2.9 maximum_maximum_fusion.refs_2_
  651.4 12.9 %collective-permute-done.8 = bf16[480,480]{0,1:T(8,128)(2,1)} collective-permute-done((bf16[480,480]{0,1:T(8,128)(2,1)S(1)}, bf16[480,480]{0,1:T(8,128)(2,1)}, u32[]{:S(2)}, u32[]{:S(2)}) %collective-permute-start.8) | collective-permute-done | bytes 460832 | tf_op jit(solution)/shard_map/ppermute | solution.py:469
  664.3 3.5 concatenate.62
  667.9 3.3 fusion.8
  671.2 2.4 copy.62
  673.6 6.0 fusion.45
  679.8 67.8 %block_scatter.5 = (f32[176,2560]{1,0:T(8,128)S(1)}, bf16[80,2560]{1,0:T(8,128)(2,1)S(1)}, bf16[80,2560]{1,0:T(8,128)(2,1)S(1)}) custom-call(bf16[2048,320]{1,0:T(8,128)(2,1)S(1)} %bitcast.128, bf16[320,2560]{1,0:T(8,128)(2,1)S(1)} %copy-done.10, bf16[16,48,2560]{2,1,0:T(8,128)(2,1)} %maximum_maximum_fusion.refs_2_, ...), custom_call_target="tpu_custom_call" | custom-call | tf_op jit(solution)/shard_map/block_scatter/pallas_call | solution.py:443
  749.6 9.7 %convert_add_fusion = f32[480,2560]{1,0:T(8,128)} fusion(bf16[240,2560]{1,0:T(8,128)(2,1)S(1)} %copy-done.60, bf16[240,2560]{1,0:T(8,128)(2,1)S(1)} %copy-done.58, bf16[2048,480]{1,0:T(8,128)(2,1)S(1)} %copy-done.15, bf16[2048,2560]{1,0:T(8,128)(2,1)} %bitcast.138), kind=kOutput, calls=%fused_computation.2 | convolution fusion | flops 5039308800 | bytes 19824640 | tf_op jit(solution)/shard_map/dot_general | solution.py:911
  759.4 2.3 fusion.11
  763.2 40.9 %block_move.9 = (bf16[16,48,2560]{2,1,0:T(8,128)(2,1)S(1)}, bf16[16,80,480]{2,1,0:T(8,128)(2,1)S(1)}, bf16[80,2560]{1,0:T(8,128)(2,1)S(1)}) custom-call(bf16[48,2560]{1,0:T(8,128)(2,1)S(1)} %add_convert_fusion.refs_0_, bf16[16,80,480]{2,1,0:T(8,128)(2,1)S(1)} %bitcast.133, bf16[160,2560]{1,0:T(8,128)(2,1)S(1)} %slice.276.refs_3_.refs_2_), custom_call_target="tpu_custom_call" | custom-call | tf_op jit(solution)/shard_map/block_move/pallas_call | solution.py:239
  806.0 3.0 convert_element_type.116
  809.0 1.8 down_join.1
  (290 shorter events, 69.6 us)
Async XLA Ops:
  7.2 262.7 %all-gather.4.cloned.1.call-start = ((), (), s32[]{:S(2)}) async-start(), calls=%async_computation | async-start | bytes 13516800 | tf_op jit(solution)/shard_map/all_gather | solution.py:1032
  7.9 346.0 %all-gather.6.cloned.1.call-start = ((), (), s32[]{:S(2)}) async-start(), calls=%async_computation.1 | async-start | bytes 11141120 | tf_op jit(solution)/shard_map/all_gather | solution.py:1042
  14.7 105.6 %copy-start.66 = (bf16[1,128,2560]{2,1,0:T(8,128)(2,1)S(1)}, bf16[1,128,2560]{2,1,0:T(8,128)(2,1)}, u32[]{:S(2)}) copy-start(bf16[1,128,2560]{2,1,0:T(8,128)(2,1)} %param.29) | copy-start | bytes 1966084
  121.4 552.2 %all-gather.8.cloned.1.call-start = ((), (), s32[]{:S(2)}) async-start(), calls=%async_computation.2 | async-start | bytes 11141120 | tf_op jit(solution)/shard_map/all_gather | solution.py:1130
  196.6 13.6 %copy-start.86 = (f32[2560]{0:T(1024)S(1)}, f32[2560]{0:T(1024)}, u32[]{:S(2)}) copy-start(f32[2560]{0:T(1024)} %param.23) | copy-start | bytes 30724
  198.8 10.7 %copy-start.52 = (bf16[48,2560]{1,0:T(8,128)(2,1)S(1)}, bf16[48,2560]{1,0:T(8,128)(2,1)}, u32[]{:S(2)}) copy-start(bf16[48,2560]{1,0:T(8,128)(2,1)} %copy-done.51) | copy-start | bytes 737284
  204.6 8.5 %collective-permute-start = (f32[8,2560]{1,0:T(8,128)}, f32[8,2560]{1,0:T(8,128)}, u32[]{:S(2)}, u32[]{:S(2)}) collective-permute-start(f32[8,2560]{1,0:T(8,128)} %slice.149), channel_id=1, source_target_pairs={{0,4},{4,8},{8,12},{12,16},{16,20},{20,24},{24,28},{1,5},{5,9},{9,... | collective-permute-start | bytes 245768 | tf_op jit(solution)/shard_map/ppermute | solution.py:557
  209.4 45.9 %collective-permute-start.1 = (bf16[128,2560]{1,0:T(8,128)(2,1)}, bf16[128,2560]{1,0:T(8,128)(2,1)}, u32[]{:S(2)}, u32[]{:S(2)}) collective-permute-start(bf16[128,2560]{1,0:T(8,128)(2,1)} %slice.150), channel_id=1, source_target_pairs={{0,16},{16,0},{1,17},{17,1},{2,18},{18,2},{3,19},{19,3},{4,20},{20... | collective-permute-start | bytes 1966088 | tf_op jit(solution)/shard_map/ppermute | solution.py:469
  217.6 28.8 %copy-start.80 = (bf16[96,2560]{1,0:T(8,128)(2,1)S(1)}, bf16[96,2560]{1,0:T(8,128)(2,1)}, u32[]{:S(2)}) copy-start(bf16[96,2560]{1,0:T(8,128)(2,1)} %slice.151) | copy-start | bytes 1474564
  226.1 24.2 %copy-start.3 = (f32[128,2560]{1,0:T(8,128)S(1)}, f32[128,2560]{1,0:T(8,128)}, u32[]{:S(2)}) copy-start(f32[128,2560]{1,0:T(8,128)} %copy-done.2) | copy-start | bytes 3932164
  246.5 22.6 %collective-permute-start.2 = (bf16[96,2560]{1,0:T(8,128)(2,1)S(1)}, bf16[96,2560]{1,0:T(8,128)(2,1)S(1)}, u32[]{:S(2)}, u32[]{:S(2)}) collective-permute-start(bf16[96,2560]{1,0:T(8,128)(2,1)S(1)} %copy-done.80), channel_id=1, source_target_pairs={{0,16},{16,0},{1,17},{17,1},{2,18},{18,2},{3,19},{19,3},{4,20},{20... | collective-permute-start | bytes 1474568 | tf_op jit(solution)/shard_map/ppermute | solution.py:469
  250.3 19.7 %copy-start.64 = (bf16[1,128,2560]{2,1,0:T(8,128)(2,1)S(1)}, bf16[1,128,2560]{2,1,0:T(8,128)(2,1)}, u32[]{:S(2)}) copy-start(bf16[1,128,2560]{2,1,0:T(8,128)(2,1)} %param.15) | copy-start | bytes 1966084
  250.3 19.7 %copy-start.89 = (f32[2560]{0:T(1024)S(1)}, f32[2560]{0:T(1024)}, u32[]{:S(2)}) copy-start(f32[2560]{0:T(1024)} %param.25) | copy-start | bytes 30724
  279.3 65.9 %copy-start.61 = (f32[128,2560]{1,0:T(8,128)}, f32[128,2560]{1,0:T(8,128)S(1)}, u32[]{:S(2)}) copy-start(f32[128,2560]{1,0:T(8,128)S(1)} %get-tuple-element.131) | copy-start | bytes 3932164
  279.3 56.5 %copy-start.82 = (bf16[4,80,480]{2,1,0:T(8,128)(2,1)S(1)}, bf16[4,80,480]{2,1,0:T(8,128)(2,1)}, u32[]{:S(2)}) copy-start(bf16[4,80,480]{2,1,0:T(8,128)(2,1)} %slice.154) | copy-start | bytes 921604
  335.8 18.1 %collective-permute-start.3 = (bf16[320,480]{1,0:T(8,128)(2,1)S(1)}, bf16[320,480]{1,0:T(8,128)(2,1)S(1)}, u32[]{:S(2)}, u32[]{:S(2)}) collective-permute-start(bf16[320,480]{1,0:T(8,128)(2,1)S(1)} %bitcast.153), channel_id=1, source_target_pairs={{0,16},{16,0},{1,17},{17,1},{2,18},{18,2},{3,19},{19,3},{4,20},{20... | collective-permute-start | bytes 921608 | tf_op jit(solution)/shard_map/ppermute | solution.py:469
  375.3 78.3 %copy-start.16 = (bf16[2048,480]{1,0:T(8,128)(2,1)}, bf16[2048,480]{1,0:T(8,128)(2,1)S(1)}, u32[]{:S(2)}) copy-start(bf16[2048,480]{1,0:T(8,128)(2,1)S(1)} %multiply_convert_fusion.1.refs_0_) | copy-start | bytes 5898244
  384.8 68.3 %copy-start.14 = (bf16[2048,480]{1,0:T(8,128)(2,1)}, bf16[2048,480]{1,0:T(8,128)(2,1)S(1)}, u32[]{:S(2)}) copy-start(bf16[2048,480]{1,0:T(8,128)(2,1)S(1)} %broadcast_select_fusion.1.refs_0_) | copy-start | bytes 5898244
  384.8 68.3 %copy-start.47 = (bf16[960,480]{1,0:T(8,128)(2,1)S(1)}, bf16[960,480]{1,0:T(8,128)(2,1)}, u32[]{:S(2)}) copy-start(bf16[960,480]{1,0:T(8,128)(2,1)} %copy-done.45) | copy-start | bytes 2764804
  525.5 20.4 %copy-start.31 = (f32[128,2560]{1,0:T(8,128)S(1)}, f32[128,2560]{1,0:T(8,128)}, u32[]{:S(2)}) copy-start(f32[128,2560]{1,0:T(8,128)} %copy-done.30) | copy-start | bytes 3932164
  525.5 35.0 %slice-start.1 = ((s8[10485760]{0:T(1024)(128)(4,1)}), s8[4194304]{0:T(1024)(128)(4,1)S(1)}, s32[]{:S(2)}) async-start(s8[10485760]{0:T(1024)(128)(4,1)} %bitcast.157), calls=%async_computation.4 | async-start | bytes 8388608
  525.6 35.0 %slice-start.2 = ((s8[10485760]{0:T(1024)(128)(4,1)}), s8[4194304]{0:T(1024)(128)(4,1)S(1)}, s32[]{:S(2)}) async-start(s8[10485760]{0:T(1024)(128)(4,1)} %bitcast.157), calls=%async_computation.5 | async-start | bytes 8388608
  532.9 13.1 %copy-start.7 = (bf16[2,10,256,256]{3,2,1,0:T(8,128)(2,1)S(1)}, bf16[2,10,256,256]{3,2,1,0:T(8,128)(2,1)}, u32[]{:S(2)}) copy-start(bf16[2,10,256,256]{3,2,1,0:T(8,128)(2,1)} %weight_ref.3) | copy-start | bytes 7864324
  532.9 13.1 %copy-start.24 = (f32[128,2560]{1,0:T(8,128)S(1)}, f32[128,2560]{1,0:T(8,128)}, u32[]{:S(2)}) copy-start(f32[128,2560]{1,0:T(8,128)} %copy-done.22) | copy-start | bytes 3932164
  532.9 13.1 %copy-start.50 = (f32[4,2560]{1,0:T(4,128)S(1)}, f32[4,2560]{1,0:T(4,128)}, u32[]{:S(2)}) copy-start(f32[4,2560]{1,0:T(4,128)} %taps_ref.5) | copy-start | bytes 122884
  532.9 13.1 %copy-start.54 = (f32[2,2560]{1,0:T(2,128)S(1)}, f32[2,2560]{1,0:T(2,128)}, u32[]{:S(2)}) copy-start(f32[2,2560]{1,0:T(2,128)} %gate_bias_ref.3) | copy-start | bytes 61444
  532.9 27.6 %slice-start.3 = ((s8[10485760]{0:T(1024)(128)(4,1)}), s8[2097152]{0:T(1024)(128)(4,1)S(1)}, s32[]{:S(2)}) async-start(s8[10485760]{0:T(1024)(128)(4,1)} %bitcast.157), calls=%async_computation.6 | async-start | bytes 4194304
  546.0 14.5 %copy-start.17 = (bf16[2048,480]{1,0:T(8,128)(2,1)S(1)}, bf16[2048,480]{1,0:T(8,128)(2,1)}, u32[]{:S(2)}) copy-start(bf16[2048,480]{1,0:T(8,128)(2,1)} %copy-done.16) | copy-start | bytes 5898244
  558.5 22.0 %collective-permute-start.4 = (f32[8,2560]{1,0:T(8,128)S(1)}, f32[8,2560]{1,0:T(8,128)S(1)}, u32[]{:S(2)}, u32[]{:S(2)}) collective-permute-start(f32[8,2560]{1,0:T(8,128)S(1)} %slice.158), channel_id=1, source_target_pairs={{4,0},{8,4},{12,8},{16,12},{20,16},{24,20},{28,24},{5,1},{9,5},{13... | collective-permute-start | bytes 245768 | tf_op jit(solution)/shard_map/ppermute | solution.py:557
  578.2 86.1 %collective-permute-start.7 = (bf16[640,480]{0,1:T(8,128)(2,1)}, bf16[640,480]{0,1:T(8,128)(2,1)}, u32[]{:S(2)}, u32[]{:S(2)}) collective-permute-start(bf16[640,480]{0,1:T(8,128)(2,1)} %slice.200), channel_id=1, source_target_pairs={{0,16},{16,0},{1,17},{17,1},{2,18},{18,2},{3,19},{19,3},{4,20},{20... | collective-permute-start | bytes 1843208 | tf_op jit(solution)/shard_map/ppermute | solution.py:469
  578.5 72.9 %collective-permute-start.6 = (bf16[160,480]{0,1:T(8,128)(2,1)}, bf16[160,480]{0,1:T(8,128)(2,1)S(1)}, u32[]{:S(2)}, u32[]{:S(2)}) collective-permute-start(bf16[160,480]{0,1:T(8,128)(2,1)} %slice.199), channel_id=1, source_target_pairs={{0,16},{16,0},{1,17},{17,1},{2,18},{18,2},{3,19},{19,3},{4,20},{20... | collective-permute-start | bytes 460808 | tf_op jit(solution)/shard_map/ppermute | solution.py:469
  586.9 53.5 %copy-start.79 = (bf16[480,480]{0,1:T(8,128)(2,1)S(1)}, bf16[480,480]{0,1:T(8,128)(2,1)}, u32[]{:S(2)}) copy-start(bf16[480,480]{0,1:T(8,128)(2,1)} %slice.201) | copy-start | bytes 1382404
  586.9 54.8 %copy-start.81 = (bf16[16,1,2560]{2,1,0:T(2,128)(2,1)S(1)}, bf16[16,1,2560]{2,1,0:T(2,128)(2,1)}, u32[]{:S(2)}) copy-start(bf16[16,1,2560]{2,1,0:T(2,128)(2,1)} %copy_dynamic-update-slice_fusion) | copy-start | bytes 245764
  586.9 54.8 %copy-start.88 = (bf16[2560]{0:T(1024)(128)(2,1)S(1)}, bf16[2560]{0:T(1024)(128)(2,1)}, u32[]{:S(2)}) copy-start(bf16[2560]{0:T(1024)(128)(2,1)} %get-tuple-element.116) | copy-start | bytes 15364
  586.9 54.8 %copy-start.9 = (bf16[320,2560]{1,0:T(8,128)(2,1)S(1)}, bf16[320,2560]{1,0:T(8,128)(2,1)}, u32[]{:S(2)}) copy-start(bf16[320,2560]{1,0:T(8,128)(2,1)} %copy-done.8) | copy-start | bytes 4915204
  640.4 24.0 %collective-permute-start.8 = (bf16[480,480]{0,1:T(8,128)(2,1)S(1)}, bf16[480,480]{0,1:T(8,128)(2,1)}, u32[]{:S(2)}, u32[]{:S(2)}) collective-permute-start(bf16[480,480]{0,1:T(8,128)(2,1)S(1)} %copy-done.79), channel_id=1, source_target_pairs={{0,16},{16,0},{1,17},{17,1},{2,18},{18,2},{3,19},{19,3},{4,20},{20... | collective-permute-start | bytes 1382408 | tf_op jit(solution)/shard_map/ppermute | solution.py:469
  679.7 67.9 %copy-start.65 = (bf16[1,128,2560]{2,1,0:T(8,128)(2,1)S(1)}, bf16[1,128,2560]{2,1,0:T(8,128)(2,1)}, u32[]{:S(2)}) copy-start(bf16[1,128,2560]{2,1,0:T(8,128)(2,1)} %param.15) | copy-start | bytes 1966084
  679.7 67.9 %copy-start.84 = (f32[2560]{0:T(1024)S(1)}, f32[2560]{0:T(1024)}, u32[]{:S(2)}) copy-start(f32[2560]{0:T(1024)} %param.16) | copy-start | bytes 30724
  679.7 69.8 %copy-start.58 = (bf16[240,2560]{1,0:T(8,128)(2,1)S(1)}, bf16[240,2560]{1,0:T(8,128)(2,1)}, u32[]{:S(2)}) copy-start(bf16[240,2560]{1,0:T(8,128)(2,1)} %copy-done.57) | copy-start | bytes 3686404
  679.7 69.8 %copy-start.60 = (bf16[240,2560]{1,0:T(8,128)(2,1)S(1)}, bf16[240,2560]{1,0:T(8,128)(2,1)}, u32[]{:S(2)}) copy-start(bf16[240,2560]{1,0:T(8,128)(2,1)} %copy-done.59) | copy-start | bytes 3686404
  747.9 14.7 %collective-permute-start.5 = (bf16[48,2560]{1,0:T(8,128)(2,1)S(1)}, bf16[48,2560]{1,0:T(8,128)(2,1)S(1)}, u32[]{:S(2)}, u32[]{:S(2)}) collective-permute-start(bf16[48,2560]{1,0:T(8,128)(2,1)S(1)} %slice.277), channel_id=1, source_target_pairs={{0,16},{16,0},{1,17},{17,1},{2,18},{18,2},{3,19},{19,3},{4,20},{20... | collective-permute-start | bytes 737288 | tf_op jit(solution)/shard_map/ppermute | solution.py:469
  749.6 9.8 %copy-start.27 = (f32[128,2560]{1,0:T(8,128)S(1)}, f32[128,2560]{1,0:T(8,128)}, u32[]{:S(2)}) copy-start(f32[128,2560]{1,0:T(8,128)} %copy-done.25) | copy-start | bytes 3932164
  749.6 9.7 %copy-start.63 = (f32[128,2560]{1,0:T(8,128)S(1)}, f32[128,2560]{1,0:T(8,128)}, u32[]{:S(2)}) copy-start(f32[128,2560]{1,0:T(8,128)} %copy-done.61) | copy-start | bytes 3932164
  749.6 9.7 %copy-start.68 = (bf16[1,128,2560]{2,1,0:T(8,128)(2,1)S(1)}, bf16[1,128,2560]{2,1,0:T(8,128)(2,1)}, u32[]{:S(2)}) copy-start(bf16[1,128,2560]{2,1,0:T(8,128)(2,1)} %param.29) | copy-start | bytes 1966084
  749.6 9.7 %copy-start.73 = (f32[128,1280]{1,0:T(8,128)S(1)}, f32[128,1280]{1,0:T(8,128)}, u32[]{:S(2)}) copy-start(f32[128,1280]{1,0:T(8,128)} %get-tuple-element.124) | copy-start | bytes 1966084
  749.6 9.7 %copy-start.74 = (f32[128,1280]{1,0:T(8,128)S(1)}, f32[128,1280]{1,0:T(8,128)}, u32[]{:S(2)}) copy-start(f32[128,1280]{1,0:T(8,128)} %get-tuple-element.125) | copy-start | bytes 1966084
  749.6 9.7 %copy-start.91 = (f32[128]{0:T(128)S(1)}, f32[128]{0:T(128)}, u32[]{:S(2)}) copy-start(f32[128]{0:T(128)} %copy-done.90) | copy-start | bytes 1540
  749.6 9.7 %copy-start.93 = (f32[128]{0:T(128)S(1)}, f32[128]{0:T(128)}, u32[]{:S(2)}) copy-start(f32[128]{0:T(128)} %copy-done.92) | copy-start | bytes 1540
  (65 other events, 226.5 us)
Sparse Core Ops, SparseCore 0:
  10.9 163.5 all-gather.3
  176.1 87.0 all-gather.5
  521.8 65.4 all-gather.7
